TPU v7x, 32 devices: a whole 2x2x4 slice. The times are simulated.
32 devices in a mesh: lat: 4 (over z), lon: 2 (over y), hid: 4 (over x, core).
Axes of the slice: x: 2, y: 2, z: 4, core: 2. Of those that a mesh axis runs over, the one named last changes fastest.
Arguments:
- grid_latent: float32 [32, 256, 512], P('lat', 'lon'), may hold values from -6 to 6
- mesh_latent: float32 [4, 2, 512, 512], P('lat', 'lon'), may hold values from -6 to 6
- grid_edge_feats: float32 [4, 2, 4, 1024], P('lat', 'lon'), may hold values from -6 to 6
- grid_senders: int32 [4, 2, 1024], P('lat', 'lon'), may hold values from 0 to 8191, as said below
- grid_receivers: int32 [4, 2, 1024], P('lat', 'lon'), may hold values from -1 to 4095, as said below
- mesh_edge_feats: float32 [4, 2, 4, 512], P('lat', 'lon'), may hold values from -6 to 6
- mesh_senders: int32 [4, 2, 512], P('lat', 'lon'), may hold values from 0 to 4095, as said below
- mesh_receivers: int32 [4, 2, 512], P('lat', 'lon'), may hold values from -1 to 4095, as said below
- edge_weight: float32 [2, 4, 512], P(None, None, 'hid'), may hold values from -1.75 to 1.75
- sender_weight: float32 [2, 512, 512], P(None, None, 'hid'), may hold values from -0.15625 to 0.15625
- receiver_weight: float32 [2, 512, 512], P(None, None, 'hid'), may hold values from -0.15625 to 0.15625
- first_bias: float32 [2, 512], P(None, 'hid'), may hold values from -1 to 1
- out_weight: float32 [2, 512, 512], P(None, 'hid'), may hold values from -4 to 4
- out_bias: float32 [2, 512], replicated, may hold values from -3 to 3
- norm_gain: float32 [2, 512], replicated, may hold values from 0.5 to 1.5
- norm_shift: float32 [2, 512], replicated, may hold values from -3 to 3
Outputs:
- mesh_out: float32 [4, 2, 512, 512], P('lat', 'lon', None, 'hid')
Inputs may be any that keep to these rules, and one draw needn't show every extreme that they name: `grid_senders`: A live slot of patch (a, b) sends from a grid cell of block (a, b) or within 2 cells outside it in latitude (never past the first or last row) and in longitude (wrapping round); a padding slot names the first cell of its own block. `grid_receivers`: in each patch's block of 1024 slots the live slots come first and their receivers are nodes of that patch in non-decreasing order; -1 marks padding; in every draw some patch has all 1024 slots live. `mesh_senders`: A live slot of patch (a, b) sends from a node of patch (a + p, b + q), p and q in -1, 0, 1, with latitude never leaving the range and longitude wrapping round; a padding slot names a node of its own patch. `mesh_receivers`: in each patch's block of 512 slots the live slots come first and their receivers are nodes of that patch in non-decreasing order; -1 marks padding; in every draw some patch has all 512 slots live.
All inputs are finite; a program needn't handle non-finite values.
Results may differ from a plain program's by a relative error of at most 0.0003.
Values sent between devices are 32-bit elements; how exact they have to be, the bound alone decides.
No kernel may reach another device: no remote copies, remote signals or barrier semaphores. Data moves between devices by JAX's collectives and lax.ppermute only.
A program may use at most 64 MiB of HBM per device.

v0:
```python
import jax
import jax.numpy as jnp
from jax import lax
from jax.sharding import PartitionSpec as P

RIM = 2


HIGHEST = lax.Precision.HIGHEST
epsilon = 1e-05


def padded_2(block, sides, width):
    for axis, dim in sides:
        count = lax.axis_size(axis)
        forward = [(i, i + 1) for i in range(count - 1)]
        forward.append((count - 1, 0))
        backward = [(target, source) for source, target in forward]
        low = lax.ppermute(
            lax.slice_in_dim(block, block.shape[dim] - width, None, axis=dim), axis, forward
        )
        high = lax.ppermute(lax.slice_in_dim(block, 0, width, axis=dim), axis, backward)
        block = jnp.concatenate([low, block, high], axis=dim)
    return block


def matmul(left, right):
    return jnp.dot(left, right, precision=HIGHEST, preferred_element_type=jnp.float32)


def contract_first(left, right):
    return lax.dot_general(
        left, right, (((0,), (0,)), ((), ())), precision=HIGHEST, preferred_element_type=jnp.float32
    )


def normalise_whole(section_index, partial_value, onehot, out_bias, norm_gain, norm_shift):
    summed = lax.psum(partial_value, "hid") + out_bias[section_index]
    center = jnp.mean(summed, axis=1, keepdims=True)
    centred = summed - center
    spread = jnp.mean(centred * centred, axis=1, keepdims=True)
    normed = (
        centred * lax.rsqrt(spread + epsilon) * norm_gain[section_index] + norm_shift[section_index]
    )
    return contract_first(onehot, normed)


def per_device(
    grid_latent,
    mesh_latent,
    grid_edge_feats,
    grid_senders,
    grid_receivers,
    mesh_edge_feats,
    mesh_senders,
    mesh_receivers,
    edge_weight,
    sender_weight,
    receiver_weight,
    first_bias,
    out_weight,
    out_bias,
    norm_gain,
    norm_shift,
):
    lat_index = lax.axis_index("lat")
    lon_index = lax.axis_index("lon")
    lon_count = lax.axis_size("lon")
    hid_index = lax.axis_index("hid")
    hid_count = lax.axis_size("hid")
    block_rows, block_cols, latent_width = grid_latent.shape
    node_count = mesh_latent.shape[2]
    patch_index = lat_index * lon_count + lon_index
    mesh_own = mesh_latent.reshape(node_count, latent_width)
    node_ids = jnp.arange(node_count, dtype=jnp.int32)

    def aggregate(section_index, send_rows, receivers, receiver_table, feats):
        local_node = receivers.reshape(-1) - patch_index * node_count
        onehot = (local_node[:, None] == node_ids[None, :]).astype(jnp.float32)
        recv_terms = matmul(receiver_table, receiver_weight[section_index])
        recv_rows = jnp.take(recv_terms, jnp.clip(local_node, 0, node_count - 1), axis=0)
        edge_terms = contract_first(feats.reshape(feats.shape[2], -1), edge_weight[section_index])
        hidden = jax.nn.silu(send_rows + recv_rows + edge_terms + first_bias[section_index])
        partial_value = matmul(hidden, out_weight[section_index])
        incoming = normalise_whole(
            section_index, partial_value, onehot, out_bias, norm_gain, norm_shift
        )
        return incoming

    own_terms = matmul(grid_latent.reshape(block_rows * block_cols, latent_width), sender_weight[0])
    own_terms = own_terms.reshape(block_rows, block_cols, own_terms.shape[1])
    padded = padded_2(own_terms, (("lat", 0), ("lon", 1)), RIM)
    grid_table = padded.reshape(-1, own_terms.shape[2])
    total_lon = block_cols * lon_count
    grid_ids = grid_senders.reshape(-1)
    cell_row = grid_ids // total_lon - lat_index * block_rows + RIM
    cell_col = (grid_ids % total_lon - lon_index * block_cols + RIM) % total_lon
    grid_rows = jnp.take(grid_table, cell_row * (block_cols + 2 * RIM) + cell_col, axis=0)
    incoming = aggregate(0, grid_rows, grid_receivers, mesh_own, grid_edge_feats)
    mesh_mid = mesh_own + incoming
    own_terms = matmul(mesh_mid, sender_weight[1])
    padded = padded_2(
        own_terms.reshape(1, 1, node_count, own_terms.shape[1]), (("lat", 0), ("lon", 1)), 1
    )
    mesh_table = padded.reshape(-1, own_terms.shape[1])
    mesh_ids = mesh_senders.reshape(-1)
    source_patch = mesh_ids // node_count
    row_offset = source_patch // lon_count - lat_index + 1
    col_offset = (source_patch % lon_count - lon_index + 1) % lon_count
    mesh_rows = jnp.take(
        mesh_table, (row_offset * 3 + col_offset) * node_count + mesh_ids % node_count, axis=0
    )
    incoming = aggregate(1, mesh_rows, mesh_receivers, mesh_mid, mesh_edge_feats)
    share_width = latent_width // hid_count
    mesh_out = lax.dynamic_slice_in_dim(
        mesh_mid + incoming, hid_index * share_width, share_width, 1
    )
    return mesh_out.reshape(1, 1, node_count, share_width)


def solution(mesh):
    return jax.shard_map(
        per_device,
        mesh=mesh,
        in_specs=(
            P("lat", "lon", None),
            P("lat", "lon", None, None),
            P("lat", "lon", None, None),
            P("lat", "lon", None),
            P("lat", "lon", None),
            P("lat", "lon", None, None),
            P("lat", "lon", None),
            P("lat", "lon", None),
            P(None, None, "hid"),
            P(None, None, "hid"),
            P(None, None, "hid"),
            P(None, "hid"),
            P(None, "hid", None),
            P(),
            P(),
            P(),
        ),
        out_specs=P("lat", "lon", None, "hid"),
        check_vma=False,
    )
```

profile of v0, /device:TPU:9, one launch (start us, length us, event | category | flops | bytes accessed | tf_op | source)
XLA Modules:
  0.0 205.1 jit_solution(4760105120833202359)
XLA Ops:
  6.5 1.6 copy-done
  8.1 2.7 %fusion.44 = f32[1024,128]{1,0:T(8,128)S(1)} fusion(f32[1024,512]{1,0:T(8,128)S(1)} %bitcast.98, f32[2,512,128]{2,1,0:T(8,128)} %param.25), kind=kOutput, calls=%fused_computation.58 | convolution fusion | flops 805306368 | bytes 2883584 | tf_op jit(solution)/shard_map/dot_general | solution.py:28
  10.9 1.3 collective-permute-start
  12.3 0.2 collective-permute-start.1
  12.4 0.1 compare_select_fusion.1
  12.6 2.2 %fusion.10 = f32[512,128]{1,0:T(8,128)S(1)} fusion(f32[1,1,512,512]{3,2,1,0:T(8,128)} %param.17, f32[2,512,128]{2,1,0:T(8,128)} %param.26), kind=kOutput, calls=%fused_computation.18 | convolution fusion | flops 402653184 | bytes 1572864 | tf_op jit(solution)/shard_map/dot_general | solution.py:28
  14.8 0.5 collective-permute-done
  15.3 4.7 %collective-permute-done.1 = f32[2,128,128]{2,1,0:T(8,128)S(1)} collective-permute-done((f32[2,128,128]{2,1,0:T(8,128)S(1)}, f32[2,128,128]{2,1,0:T(8,128)S(1)}, u32[]{:S(2)}, u32[]{:S(2)}) %collective-permute-start.1) | collective-permute-done | bytes 131104 | tf_op jit(solution)/shard_map/ppermute | solution.py:22
  20.1 1.3 collective-permute-start.2
  21.4 0.2 collective-permute-start.3
  21.6 2.8 %gather_fusion.1 = f32[1024,128]{1,0:T(8,128)S(1)} fusion(f32[512,128]{1,0:T(8,128)S(1)} %fusion.10, s32[1024]{0:T(1024)S(1)} %broadcast_clamp_fusion), kind=kCustom, calls=%fused_computation.1 | custom fusion | bytes 1052672 | tf_op jit(solution)/shard_map/jit(_take)/gather | solution.py:81
  24.4 2.0 pad_maximum_fusion.1
  26.4 1.2 reshape.537
  27.6 0.0 copy-start.12
  27.6 0.0 copy-start.16
  27.6 4.0 %gather_fusion = f32[1024,128]{1,0:T(8,128)} fusion(f32[1584,128]{1,0:T(8,128)S(1)} %reshape.537, s32[1024]{0:T(1024)S(1)} %broadcast_clamp_fusion.1), kind=kCustom, calls=%fused_computation | custom fusion | bytes 1052672 | tf_op jit(solution)/shard_map/jit(_take)/gather | solution.py:98
  31.6 2.5 %fusion.9 = f32[1024,128]{1,0:T(8,128)S(1)} fusion(f32[1024,128]{1,0:T(8,128)S(1)} %gather_fusion.1, f32[1024,128]{1,0:T(8,128)} %gather_fusion, f32[128]{0:T(128)S(1)} %get-tuple-element.20, pred[1024]{0:T(1024)(128)(4,1)S(1)} %get-tuple-element.21, pred[1024]{0:T(1024)(128)(4,1)S(1)} %get-tuple-element.22, f32[1,1,4,1024]{3,2,1,0:T(4,128)S(1)} %copy-done.12, ...), kind=kOutput, calls=%fused_computation.16 | convolution fusion | flops 6946816 | bytes 1593856 | tf_op jit(solution)/shard_map/dot_general | solution.py:32
  34.2 4.1 %fusion.30 = f32[1024,512]{1,0:T(8,128)} fusion(f32[1024,128]{1,0:T(8,128)S(1)} %fusion.9, f32[2,128,512]{2,1,0:T(8,128)} %param.28), kind=kOutput, calls=%fused_computation.43 | convolution fusion | flops 805830656 | bytes 2883584 | tf_op jit(solution)/shard_map/dot_general | solution.py:28
  38.3 0.0 all-reduce.3.cloned.1.call-update
  38.3 0.0 all-reduce.5.cloned.1.call-start
  38.3 0.1 compare_select_fusion.5
  38.5 51.8 %all-reduce.3.cloned.1.call-done = f32[1024,512]{1,0:T(8,128)} async-done(((f32[1024,512]{1,0:T(8,128)}), f32[1024,512]{1,0:T(8,128)}) %all-reduce.3.cloned.1.call-update) | async-done | bytes 2097168 | tf_op jit(solution)/shard_map/psum | solution.py:38
  90.3 2.0 add_reduce_fusion
  92.2 0.3 copy-done.1
  92.5 0.5 multiply_reduce_fusion
  93.1 2.7 %fusion.6 = f32[512,512]{1,0:T(8,128)S(1)} fusion(f32[1024,512]{1,0:T(8,128)S(1)} %copy-done.1, f32[1,1,512,512]{3,2,1,0:T(8,128)S(1)} %copy-done.5, f32[512]{0:T(512)S(1)} %bitcast.123, f32[512]{0:T(512)S(1)} %bitcast.122, f32[1024]{0:T(1024)S(1)} %add_rsqrt_fusion, f32[1024]{0:T(1024)S(1)} %broadcast_multiply_fusion, f32[512]{0:T(512)S(1)} %bitcast.109, ...), kind=kOutput, calls=%fused_computation.14 | convolution fusion | flops 3224633344 | bytes 4212736 | tf_op jit(solution)/shard_map/dot_general | solution.py:32
  95.8 1.0 convolution_bitcast_fusion
  96.8 1.3 collective-permute-start.4
  98.0 0.3 collective-permute-start.5
  98.3 5.5 %collective-permute-done.4 = f32[1,1,512,128]{3,2,1,0:T(8,128)S(1)} collective-permute-done((f32[1,1,512,128]{3,2,1,0:T(8,128)S(1)}, f32[1,1,512,128]{3,2,1,0:T(8,128)S(1)}, u32[]{:S(2)}, u32[]{:S(2)}) %collective-permute-start.4) | collective-permute-done | bytes 262176 | tf_op jit(solution)/shard_map/ppermute | solution.py:19
  103.8 7.8 %collective-permute-done.5 = f32[1,1,512,128]{3,2,1,0:T(8,128)S(1)} collective-permute-done((f32[1,1,512,128]{3,2,1,0:T(8,128)S(1)}, f32[1,1,512,128]{3,2,1,0:T(8,128)S(1)}, u32[]{:S(2)}, u32[]{:S(2)}) %collective-permute-start.5) | collective-permute-done | bytes 262176 | tf_op jit(solution)/shard_map/ppermute | solution.py:22
  111.6 1.0 pad_maximum_fusion.2
  112.5 1.2 collective-permute-start.6
  113.7 0.3 collective-permute-start.7
  114.1 1.3 fusion.69
  115.4 1.0 fusion.39
  116.4 1.6 gather_fusion.3
  118.0 13.5 %collective-permute-done.6 = f32[3,1,512,128]{3,2,1,0:T(8,128)} collective-permute-done((f32[3,1,512,128]{3,2,1,0:T(8,128)}, f32[3,1,512,128]{3,2,1,0:T(8,128)}, u32[]{:S(2)}, u32[]{:S(2)}) %collective-permute-start.6) | collective-permute-done | bytes 786464 | tf_op jit(solution)/shard_map/ppermute | solution.py:19
  131.5 16.9 %collective-permute-done.7 = f32[3,1,512,128]{3,2,1,0:T(8,128)} collective-permute-done((f32[3,1,512,128]{3,2,1,0:T(8,128)}, f32[3,1,512,128]{3,2,1,0:T(8,128)}, u32[]{:S(2)}, u32[]{:S(2)}) %collective-permute-start.7) | collective-permute-done | bytes 786464 | tf_op jit(solution)/shard_map/ppermute | solution.py:22
  148.3 3.2 %pad_maximum_fusion = f32[3,3,512,128]{3,2,1,0:T(8,128)} fusion(f32[3,1,512,128]{3,2,1,0:T(8,128)} %collective-permute-done.7, f32[1,1,512,128]{3,2,1,0:T(8,128)} %copy-done.7, f32[1,1,512,128]{3,2,1,0:T(8,128)} %copy-done.3, f32[1,1,512,128]{3,2,1,0:T(8,128)} %copy-done.6, f32[3,1,512,128]{3,2,1,0:T(8,128)} %collective-permute-done.6), kind=kLoop, calls=%fused_computation.4 | loop fusion | flops 2359296 | bytes 4718592 | tf_op jit(solution)/shard_map/concatenate | solution.py:23
  151.5 3.3 %gather_fusion.2 = f32[512,128]{1,0:T(8,128)} fusion(f32[4608,128]{1,0:T(8,128)} %bitcast.99, s32[1024]{0:T(1024)S(1)} %pad_clamp_fusion.1), kind=kCustom, calls=%fused_computation.2 | custom fusion | bytes 526336 | tf_op jit(solution)/shard_map/jit(_take)/gather | solution.py:110
  154.9 3.2 %fusion.37 = f32[512,512]{1,0:T(8,128)} fusion(f32[2,128,512]{2,1,0:T(8,128)} %param.28, f32[512,128]{1,0:T(8,128)S(1)} %copy-done.4, f32[512,128]{1,0:T(8,128)} %gather_fusion.3, f32[512,128]{1,0:T(8,128)} %gather_fusion.2, f32[128]{0:T(128)S(1)} %get-tuple-element.19, pred[512]{0:T(512)(128)(4,1)S(1)} %get-tuple-element.23, ...), kind=kOutput, calls=%fused_computation.51 | convolution fusion | flops 403243008 | bytes 2098688 | tf_op jit(solution)/shard_map/dot_general | solution.py:28
  158.0 0.0 all-reduce.5.cloned.1.call-update
  158.1 34.9 %all-reduce.5.cloned.1.call-done = f32[512,512]{1,0:T(8,128)} async-done(((f32[512,512]{1,0:T(8,128)}), f32[512,512]{1,0:T(8,128)}) %all-reduce.5.cloned.1.call-update) | async-done | bytes 1048592 | tf_op jit(solution)/shard_map/psum | solution.py:38
  193.0 1.5 add_reduce_fusion.1
  194.4 1.5 multiply_reduce_fusion.1
  196.0 1.5 fusion.12
  197.4 0.8 fusion.36
  (63 shorter events, 0.3 us)
Async XLA Ops:
  6.5 1.6 copy-start
  6.5 5.9 %copy-start.13 = (s32[1,1,1024]{2,1,0:T(1,128)S(1)}, s32[1,1,1024]{2,1,0:T(1,128)}, u32[]{:S(2)}) copy-start(s32[1,1,1024]{2,1,0:T(1,128)} %param.19) | copy-start | bytes 12292
  6.5 6.0 %copy-start.17 = (s32[1,1,1024]{2,1,0:T(1,128)S(1)}, s32[1,1,1024]{2,1,0:T(1,128)}, u32[]{:S(2)}) copy-start(s32[1,1,1024]{2,1,0:T(1,128)} %param.20) | copy-start | bytes 12292
  6.5 83.7 %all-reduce.3.cloned.1.call-start = ((), (), s32[]{:S(2)}) async-start(), calls=%async_computation | async-start | bytes 4194304 | tf_op jit(solution)/shard_map/psum | solution.py:38
  10.9 10.7 %copy-start.22 = (f32[2,128]{1,0:T(2,128)S(1)}, f32[2,128]{1,0:T(2,128)}, u32[]{:S(2)}) copy-start(f32[2,128]{1,0:T(2,128)} %param.27) | copy-start | bytes 3076
  10.9 4.4 %collective-permute-start = (f32[2,128,128]{2,1,0:T(8,128)S(1)}, f32[2,128,128]{2,1,0:T(8,128)S(1)}, u32[]{:S(2)}, u32[]{:S(2)}) collective-permute-start(f32[2,128,128]{2,1,0:T(8,128)S(1)} %bitcast.103), channel_id=1, source_target_pairs={{0,8},{8,16},{16,24},{24,0},{1,9},{9,17},{17,25},{25,1},{2,10},{10... | collective-permute-start | bytes 393224 | tf_op jit(solution)/shard_map/ppermute | solution.py:19
  12.3 7.8 %collective-permute-start.1 = (f32[2,128,128]{2,1,0:T(8,128)S(1)}, f32[2,128,128]{2,1,0:T(8,128)S(1)}, u32[]{:S(2)}, u32[]{:S(2)}) collective-permute-start(f32[2,128,128]{2,1,0:T(8,128)S(1)} %bitcast.102), channel_id=1, source_target_pairs={{8,0},{16,8},{24,16},{0,24},{9,1},{17,9},{25,17},{1,25},{10,2},{18... | collective-permute-start | bytes 393224 | tf_op jit(solution)/shard_map/ppermute | solution.py:22
  15.3 6.2 %copy-start.8 = (f32[2,128,128]{2,1,0:T(8,128)}, f32[2,128,128]{2,1,0:T(8,128)S(1)}, u32[]{:S(2)}) copy-start(f32[2,128,128]{2,1,0:T(8,128)S(1)} %collective-permute-done) | copy-start | bytes 393220
  20.0 1.6 copy-start.9
  20.1 4.4 %collective-permute-start.2 = (f32[12,2,128]{2,1,0:T(2,128)S(1)}, f32[12,2,128]{2,1,0:T(2,128)S(1)}, u32[]{:S(2)}, u32[]{:S(2)}) collective-permute-start(f32[12,2,128]{2,1,0:T(2,128)S(1)} %get-tuple-element.9), channel_id=1, source_target_pairs={{0,4},{4,0},{1,5},{5,1},{2,6},{6,2},{3,7},{7,3},{8,12},{12,8},{9,1... | collective-permute-start | bytes 36872 | tf_op jit(solution)/shard_map/ppermute | solution.py:19
  21.4 3.1 %collective-permute-start.3 = (f32[12,2,128]{2,1,0:T(2,128)S(1)}, f32[12,2,128]{2,1,0:T(2,128)S(1)}, u32[]{:S(2)}, u32[]{:S(2)}) collective-permute-start(f32[12,2,128]{2,1,0:T(2,128)S(1)} %get-tuple-element.10), channel_id=1, source_target_pairs={{4,0},{0,4},{5,1},{1,5},{6,2},{2,6},{7,3},{3,7},{12,8},{8,12},{13,... | collective-permute-start | bytes 36872 | tf_op jit(solution)/shard_map/ppermute | solution.py:22
  27.6 4.0 %copy-start.12 = (f32[1,1,4,1024]{3,2,1,0:T(4,128)S(1)}, f32[1,1,4,1024]{3,2,1,0:T(4,128)}, u32[]{:S(2)}) copy-start(f32[1,1,4,1024]{3,2,1,0:T(4,128)} %param.18) | copy-start | bytes 49156
  27.6 4.0 %copy-start.16 = (f32[2,4,128]{2,1,0:T(4,128)S(1)}, f32[2,4,128]{2,1,0:T(4,128)}, u32[]{:S(2)}) copy-start(f32[2,4,128]{2,1,0:T(4,128)} %param.24) | copy-start | bytes 12292
  34.1 4.2 %copy-start.15 = (s32[1,1,512]{2,1,0:T(1,128)S(1)}, s32[1,1,512]{2,1,0:T(1,128)}, u32[]{:S(2)}) copy-start(s32[1,1,512]{2,1,0:T(1,128)} %param.22) | copy-start | bytes 6148
  34.1 4.3 %copy-start.18 = (f32[2,512]{1,0:T(2,128)S(1)}, f32[2,512]{1,0:T(2,128)}, u32[]{:S(2)}) copy-start(f32[2,512]{1,0:T(2,128)} %param.29) | copy-start | bytes 12292
  34.1 4.3 %copy-start.19 = (f32[2,512]{1,0:T(2,128)S(1)}, f32[2,512]{1,0:T(2,128)}, u32[]{:S(2)}) copy-start(f32[2,512]{1,0:T(2,128)} %param.30) | copy-start | bytes 12292
  34.2 4.3 %copy-start.20 = (f32[2,512]{1,0:T(2,128)S(1)}, f32[2,512]{1,0:T(2,128)}, u32[]{:S(2)}) copy-start(f32[2,512]{1,0:T(2,128)} %param.31) | copy-start | bytes 12292
  38.3 154.7 %all-reduce.5.cloned.1.call-start = ((), (), s32[]{:S(2)}) async-start(), calls=%async_computation.1 | async-start | bytes 2097152 | tf_op jit(solution)/shard_map/psum | solution.py:38
  90.3 2.2 %copy-start.1 = (f32[1024,512]{1,0:T(8,128)S(1)}, f32[1024,512]{1,0:T(8,128)}, u32[]{:S(2)}) copy-start(f32[1024,512]{1,0:T(8,128)} %all-reduce.3.cloned.1.call-done) | copy-start | bytes 6291460
  90.3 2.8 %copy-start.5 = (f32[1,1,512,512]{3,2,1,0:T(8,128)S(1)}, f32[1,1,512,512]{3,2,1,0:T(8,128)}, u32[]{:S(2)}) copy-start(f32[1,1,512,512]{3,2,1,0:T(8,128)} %param.17) | copy-start | bytes 3145732
  93.0 2.7 %copy-start.11 = (f32[2,512,128]{2,1,0:T(8,128)S(1)}, f32[2,512,128]{2,1,0:T(8,128)}, u32[]{:S(2)}) copy-start(f32[2,512,128]{2,1,0:T(8,128)} %param.25) | copy-start | bytes 1572868
  93.1 5.3 %copy-start.21 = (s32[1,1,512]{2,1,0:T(1,128)S(1)}, s32[1,1,512]{2,1,0:T(1,128)}, u32[]{:S(2)}) copy-start(s32[1,1,512]{2,1,0:T(1,128)} %param.23) | copy-start | bytes 6148
  95.8 18.3 %copy-start.14 = (f32[1,1,4,512]{3,2,1,0:T(4,128)S(1)}, f32[1,1,4,512]{3,2,1,0:T(4,128)}, u32[]{:S(2)}) copy-start(f32[1,1,4,512]{3,2,1,0:T(4,128)} %param.21) | copy-start | bytes 24580
  95.8 19.6 %copy-start.10 = (f32[2,512,128]{2,1,0:T(8,128)S(1)}, f32[2,512,128]{2,1,0:T(8,128)}, u32[]{:S(2)}) copy-start(f32[2,512,128]{2,1,0:T(8,128)} %param.26) | copy-start | bytes 1572868
  96.8 17.3 %copy-start.3 = (f32[1,1,512,128]{3,2,1,0:T(8,128)}, f32[1,1,512,128]{3,2,1,0:T(8,128)S(1)}, u32[]{:S(2)}) copy-start(f32[1,1,512,128]{3,2,1,0:T(8,128)S(1)} %convolution_bitcast_fusion) | copy-start | bytes 786436
  96.8 7.0 %collective-permute-start.4 = (f32[1,1,512,128]{3,2,1,0:T(8,128)S(1)}, f32[1,1,512,128]{3,2,1,0:T(8,128)S(1)}, u32[]{:S(2)}, u32[]{:S(2)}) collective-permute-start(f32[1,1,512,128]{3,2,1,0:T(8,128)S(1)} %convolution_bitcast_fusion), channel_id=1, source_target_pairs={{0,8},{8,16},{16,24},{24,0},{1,9},{9,17},{17,25},{25,1},{2,10},{10... | collective-permute-start | bytes 786440 | tf_op jit(solution)/shard_map/ppermute | solution.py:19
  98.0 13.5 %collective-permute-start.5 = (f32[1,1,512,128]{3,2,1,0:T(8,128)S(1)}, f32[1,1,512,128]{3,2,1,0:T(8,128)S(1)}, u32[]{:S(2)}, u32[]{:S(2)}) collective-permute-start(f32[1,1,512,128]{3,2,1,0:T(8,128)S(1)} %convolution_bitcast_fusion), channel_id=1, source_target_pairs={{8,0},{16,8},{24,16},{0,24},{9,1},{17,9},{25,17},{1,25},{10,2},{18... | collective-permute-start | bytes 786440 | tf_op jit(solution)/shard_map/ppermute | solution.py:22
  103.8 11.6 %copy-start.6 = (f32[1,1,512,128]{3,2,1,0:T(8,128)}, f32[1,1,512,128]{3,2,1,0:T(8,128)S(1)}, u32[]{:S(2)}) copy-start(f32[1,1,512,128]{3,2,1,0:T(8,128)S(1)} %collective-permute-done.4) | copy-start | bytes 786436
  111.6 3.8 %copy-start.7 = (f32[1,1,512,128]{3,2,1,0:T(8,128)}, f32[1,1,512,128]{3,2,1,0:T(8,128)S(1)}, u32[]{:S(2)}) copy-start(f32[1,1,512,128]{3,2,1,0:T(8,128)S(1)} %collective-permute-done.5) | copy-start | bytes 786436
  112.5 18.9 %collective-permute-start.6 = (f32[3,1,512,128]{3,2,1,0:T(8,128)}, f32[3,1,512,128]{3,2,1,0:T(8,128)}, u32[]{:S(2)}, u32[]{:S(2)}) collective-permute-start(f32[3,1,512,128]{3,2,1,0:T(8,128)} %pad_maximum_fusion.2), channel_id=1, source_target_pairs={{0,4},{4,0},{1,5},{5,1},{2,6},{6,2},{3,7},{7,3},{8,12},{12,8},{9,1... | collective-permute-start | bytes 2359304 | tf_op jit(solution)/shard_map/ppermute | solution.py:19
  113.7 34.6 %collective-permute-start.7 = (f32[3,1,512,128]{3,2,1,0:T(8,128)}, f32[3,1,512,128]{3,2,1,0:T(8,128)}, u32[]{:S(2)}, u32[]{:S(2)}) collective-permute-start(f32[3,1,512,128]{3,2,1,0:T(8,128)} %pad_maximum_fusion.2), channel_id=1, source_target_pairs={{4,0},{0,4},{5,1},{1,5},{6,2},{2,6},{7,3},{3,7},{12,8},{8,12},{13,... | collective-permute-start | bytes 2359304 | tf_op jit(solution)/shard_map/ppermute | solution.py:22
  151.5 3.4 %copy-start.4 = (f32[512,128]{1,0:T(8,128)S(1)}, f32[512,128]{1,0:T(8,128)}, u32[]{:S(2)}) copy-start(f32[512,128]{1,0:T(8,128)} %fusion.69) | copy-start | bytes 786436
  193.0 3.0 %copy-start.2 = (f32[512,512]{1,0:T(8,128)S(1)}, f32[512,512]{1,0:T(8,128)}, u32[]{:S(2)}) copy-start(f32[512,512]{1,0:T(8,128)} %all-reduce.5.cloned.1.call-done) | copy-start | bytes 3145732
Sparse Core Ops, SparseCore 0:
  38.4 51.8 all-reduce.2
  158.2 34.7 all-reduce.4
where the time goes:
time: 208 us; the launch traced here: 205 us
  waiting for transfers between devices  135 us (65%)
  matrix products  22.1 us (11%)
  local copies, waits for them, and re-layouts  15 us (7%)
  between operations  13.8 us (7%)
  other arithmetic  12.6 us (6%)
  starting transfers between devices  6.08 us (3%)
    psum x2, waiting for transfers between devices, normalise_whole(): summed = lax.psum(partial_value, 'hid') + out_bias[section_index]  86.7 us
    ppermute x4, waiting for transfers between devices, padded_2(): lax.ppermute(lax.slice_in_dim(block, 0, width, axis=dim), axis, backward)  29.3 us
    ppermute x4, waiting for transfers between devices, padded_2(): lax.ppermute(lax.slice_in_dim(block, block.shape[dim] - width, None, axis...  19.4 us
    dot_general x6, matrix products, matmul(): jnp.dot(left, right, precision=HIGHEST, preferred_element_type=jnp.float32)  14.2 us
    dot_general x4, matrix products, contract_first(): lax.dot_general(left, right, (((0,), (0,)), ((), ())), precision=HIGHEST,...  7.93 us
    concatenate x3, other arithmetic, padded_2(): block = jnp.concatenate([low, block, high], axis=dim)  6.11 us
    ppermute x4, starting transfers between devices, padded_2(): lax.ppermute(lax.slice_in_dim(block, block.shape[dim] - width, None, axis...  5.1 us
    gather x2, local copies, waits for them, and re-layouts, aggregate(): jnp.take(recv_terms, jnp.clip(local_node, 0, node_count - 1), axis=0)  4.45 us
  transfers between devices with their start and end apart: 10, of which 8 were waited for; matrix products, arithmetic and copies ran while one was open for 5% of the time, Pallas kernels for 0%

commit v1 on v0

v1 whole, which is shorter than its diff:
```python
import jax
import jax.numpy as jnp
from jax import lax
from jax.experimental import pallas as pl
from jax.experimental.pallas import tpu as pltpu
from jax.sharding import PartitionSpec as P

RIM = 2
LANES = 128
EDGE_CHUNK = 256
epsilon = 1e-05
F32 = jnp.float32
BF16 = jnp.bfloat16


def split(value):
    high = value.astype(BF16)
    low = (value - high.astype(F32)).astype(BF16)
    return high, low


def dot(left, right):
    return jnp.dot(left, right, preferred_element_type=F32)


def dot_split(left, right):
    left_high, left_low = split(left)
    right_high, right_low = split(right)
    return dot(
        jnp.concatenate([left_high, left_high, left_low], axis=1),
        jnp.concatenate([right_high, right_low, right_high], axis=0),
    )


def down_lanes(index_row):
    return jnp.transpose(jnp.broadcast_to(index_row, (LANES, index_row.shape[1])))


def onehot_rows(index_cols, count):
    lane = lax.broadcasted_iota(jnp.int32, index_cols.shape, 1)
    blocks = [
        jnp.where(index_cols == lane + start, 1.0, 0.0).astype(BF16)
        for start in range(0, count, LANES)
    ]
    return jnp.concatenate(blocks, axis=1)


def pick(index_row, table):
    width = table.shape[1]
    high, low = split(table)
    both = dot(
        onehot_rows(down_lanes(index_row), table.shape[0]), jnp.concatenate([high, low], axis=1)
    )
    return both[:, :width] + both[:, width:]


def edge_terms(feats, weight):
    return lax.dot_general(
        feats,
        weight,
        (((0,), (0,)), ((), ())),
        precision=lax.Precision.HIGHEST,
        preferred_element_type=F32,
    )


def call(body, outs, flops, *args):
    return pl.pallas_call(
        body,
        out_shape=outs,
        cost_estimate=pl.CostEstimate(flops=flops, bytes_accessed=1 << 20, transcendentals=0),
    )(*args)


def shape(*dims):
    return jax.ShapeDtypeStruct(dims, F32)


def exchange(value, axes, move):
    sizes = [lax.axis_size(axis) for axis in axes]
    pairs = []
    total = 1
    for size in sizes:
        total *= size
    for source in range(total):
        rest, target, stride, fits = source, 0, 1, True
        for size, (step, wraps) in list(zip(sizes, move))[::-1]:
            place = rest % size + step
            rest //= size
            if wraps:
                place %= size
            elif not 0 <= place < size:
                fits = False
            target += place * stride
            stride *= size
        if fits:
            pairs.append((source, target))
    return lax.ppermute(value, axes if len(axes) > 1 else axes[0], pairs)


def gather_hid(value):
    count = lax.axis_size("hid")
    pieces = [value]
    for step in range(1, count):
        source, hop = (pieces[step - 1], 1) if step % 2 else (value, step)
        pieces.append(lax.ppermute(source, "hid", [(i, i ^ hop) for i in range(count)]))
    return pieces


def layer_norm(message, gain, shift):
    centred = message - jnp.mean(message, axis=1, keepdims=True)
    spread = jnp.mean(centred * centred, axis=1, keepdims=True)
    return centred * lax.rsqrt(spread + epsilon) * gain + shift


def normed_chunks(hidden_refs, weight_refs, bias_ref, gain_ref, shift_ref, store):
    right = jnp.concatenate([ref[...] for ref in weight_refs], axis=0)
    right_high, right_low = split(right)
    right = jnp.concatenate([right_high, right_low, right_high], axis=0)
    edges = hidden_refs[0].shape[0]
    step = min(EDGE_CHUNK, edges)
    for start in range(0, edges, step):
        left = jnp.concatenate([ref[start : start + step, :] for ref in hidden_refs], axis=1)
        left_high, left_low = split(left)
        left = jnp.concatenate([left_high, left_high, left_low], axis=1)
        message = dot(left, right) + bias_ref[...]
        store(start, step, layer_norm(message, gain_ref[...], shift_ref[...]))


def aggregate(receiver_row, nodes, normed_ref):
    node = lax.broadcasted_iota(jnp.int32, (nodes, receiver_row.shape[1]), 0)
    onehot = jnp.where(node == receiver_row, 1.0, 0.0).astype(BF16)
    width = normed_ref.shape[1] // 2
    both = dot(onehot, normed_ref[...])
    return both[:, :width] + both[:, width:]


def per_device(
    grid_latent,
    mesh_latent,
    grid_edge_feats,
    grid_senders,
    grid_receivers,
    mesh_edge_feats,
    mesh_senders,
    mesh_receivers,
    edge_weight,
    sender_weight,
    receiver_weight,
    first_bias,
    out_weight,
    out_bias,
    norm_gain,
    norm_shift,
):
    lat_index = lax.axis_index("lat")
    lon_index = lax.axis_index("lon")
    lon_count = lax.axis_size("lon")
    hid_index = lax.axis_index("hid")
    hid_count = lax.axis_size("hid")
    rows, cols, width = grid_latent.shape
    nodes = mesh_latent.shape[2]
    units = sender_weight.shape[2]
    grid_edges = grid_senders.shape[2]
    mesh_edges = mesh_senders.shape[2]
    patch = lat_index * lon_count + lon_index
    mesh_own = mesh_latent.reshape(nodes, width)
    cells = grid_latent.reshape(rows * cols, width)
    two_lon = lon_count == 2

    grid_ids = grid_senders.reshape(1, grid_edges)
    total_lon = cols * lon_count
    cell_row = grid_ids // total_lon - lat_index * rows
    cell_col = (grid_ids % total_lon - lon_index * cols + RIM) % total_lon - RIM
    in_rows = (cell_row >= 0) & (cell_row < rows)
    in_cols = (cell_col >= 0) & (cell_col < cols)
    side_slot = jnp.where(cell_col < 0, cell_col + 2 * RIM, cell_col - cols)
    own_cell = jnp.where(in_rows & in_cols, cell_row * cols + cell_col, -1)
    side_size = rows * 2 * RIM
    id_rows = -(-mesh_edges // LANES)
    lat_size = RIM * cols + RIM * 2 * RIM
    lat_pad = -(lat_size + id_rows) % 16
    lat_rows = lat_size + id_rows + lat_pad
    rim_row = jnp.where(cell_row < 0, cell_row + RIM, cell_row - rows)
    rim_place = jnp.where(in_cols, rim_row * cols + cell_col, RIM * cols + rim_row * 2 * RIM + side_slot)
    rim_place = rim_place + side_size + jnp.where(cell_row < 0, 0, lat_rows)
    rim_cell = jnp.where(
        in_rows, jnp.where(in_cols, -1, cell_row * 2 * RIM + side_slot), rim_place
    )
    grid_recv = grid_receivers.reshape(1, grid_edges) - patch * nodes
    mesh_recv = mesh_receivers.reshape(1, mesh_edges) - patch * nodes

    def sender_nodes(ids):
        source = ids // nodes
        here = source // lon_count == lat_index
        offset = (source % lon_count - lon_index) % lon_count
        node = ids % nodes
        tables = [0, 1] if two_lon else [0, lon_count - 1, 1]
        return [jnp.where(here & (offset == place), node, -1) for place in tables]

    mesh_ids = mesh_senders.reshape(1, mesh_edges)
    ids_sent = jnp.pad(
        mesh_ids.reshape(-1).astype(F32), (0, (id_rows + lat_pad) * LANES - mesh_edges)
    ).reshape(id_rows + lat_pad, LANES)

    weight_pieces = gather_hid(out_weight)
    out_weights = [[piece[section] for piece in weight_pieces] for section in range(2)]

    def terms_body(cell_ref, weight_ref, term_ref, side_ref):
        term_ref[...] = dot_split(cell_ref[...], weight_ref[...])
        for row in range(rows):
            start = row * 2 * RIM
            side_ref[start : start + RIM, :] = term_ref[row * cols : row * cols + RIM, :]
            side_ref[start + RIM : start + 2 * RIM, :] = term_ref[
                (row + 1) * cols - RIM : (row + 1) * cols, :
            ]

    terms, sides = call(
        terms_body,
        (shape(rows * cols, units), shape(side_size, units)),
        6 * rows * cols * width * units,
        cells,
        sender_weight[0],
    )
    if two_lon:
        side_got = exchange(sides, ("lon",), ((1, True),))
    else:
        parts = sides.reshape(rows, 2, RIM, units)
        from_high = exchange(parts[:, 0], ("lon",), ((-1, True),))
        from_low = exchange(parts[:, 1], ("lon",), ((1, True),))
        side_got = jnp.stack([from_high, from_low], axis=1).reshape(side_size, units)

    def rim_sent(first):
        return jnp.concatenate(
            [
                terms[first * cols : (first + RIM) * cols],
                side_got[first * 2 * RIM : (first + RIM) * 2 * RIM],
                ids_sent,
            ],
            axis=0,
        )

    rim_low = exchange(rim_sent(rows - RIM), ("lat",), ((1, False),))
    rim_high = exchange(rim_sent(0), ("lat",), ((-1, False),))

    def grid_first_body(term_ref, mesh_ref, weight_ref, feat_ref, edge_ref, bias_ref, send_ref, recv_ref, pre_ref):
        received = dot_split(mesh_ref[...], weight_ref[...])
        pre_ref[...] = (
            pick(send_ref[...], term_ref[...])
            + pick(recv_ref[...], received)
            + edge_terms(feat_ref[...], edge_ref[...])
            + bias_ref[...]
        )

    grid_pre = call(
        grid_first_body,
        shape(grid_edges, units),
        8 * grid_edges * rows * cols * units,
        terms,
        mesh_own,
        receiver_weight[0],
        grid_edge_feats.reshape(-1, grid_edges),
        edge_weight[0],
        first_bias[0:1],
        own_cell,
        grid_recv,
    )

    def grid_hidden_body(pre_ref, side_ref, low_ref, high_ref, send_ref, hidden_ref):
        pad = -(side_size + 2 * lat_rows) % LANES
        table = jnp.concatenate(
            [side_ref[...], low_ref[...], high_ref[...], jnp.zeros((pad, units), F32)], axis=0
        )
        total = pre_ref[...] + pick(send_ref[...], table)
        hidden_ref[...] = total / (1.0 + jnp.exp(-total))

    grid_hidden = call(
        grid_hidden_body,
        shape(grid_edges, units),
        4 * grid_edges * rows * cols * units,
        grid_pre,
        side_got,
        rim_low,
        rim_high,
        rim_cell,
    )
    grid_pieces = gather_hid(grid_hidden)

    def grid_message_body(*refs):
        hidden_refs, weight_refs = refs[:hid_count], refs[hid_count : 2 * hid_count]
        bias_ref, gain_ref, shift_ref, recv_ref, mesh_ref, send_ref = refs[2 * hid_count : -3]
        mid_ref, term_ref, normed_ref = refs[-3:]

        def store(start, step, normed):
            high, low = split(normed)
            normed_ref[start : start + step, :width] = high
            normed_ref[start : start + step, width:] = low

        normed_chunks(hidden_refs, weight_refs, bias_ref, gain_ref, shift_ref, store)
        middle = mesh_ref[...] + aggregate(recv_ref[...], nodes, normed_ref)
        mid_ref[...] = middle
        term_ref[...] = dot_split(middle, send_ref[...])

    mesh_mid, mesh_terms = pl.pallas_call(
        grid_message_body,
        out_shape=(shape(nodes, width), shape(nodes, units)),
        scratch_shapes=[pltpu.VMEM((grid_edges, 2 * width), BF16)],
        cost_estimate=pl.CostEstimate(
            flops=12 * grid_edges * width * width, bytes_accessed=1 << 22, transcendentals=0
        ),
    )(
        *grid_pieces,
        *out_weights[0],
        out_bias[0:1],
        norm_gain[0:1],
        norm_shift[0:1],
        grid_recv,
        mesh_own,
        sender_weight[1],
    )

    if two_lon:
        others = [exchange(mesh_terms, ("lon",), ((1, True),))]
    else:
        others = [
            exchange(mesh_terms, ("lon",), ((1, True),)),
            exchange(mesh_terms, ("lon",), ((-1, True),)),
        ]

    def ids_of(rim):
        return rim[lat_size : lat_size + id_rows].reshape(1, -1)[:, :mesh_edges].astype(jnp.int32)

    own_nodes = sender_nodes(mesh_ids)
    low_nodes = sender_nodes(ids_of(rim_low))
    high_nodes = sender_nodes(ids_of(rim_high))

    def mesh_first_body(term_ref, mid_ref, weight_ref, feat_ref, edge_ref, bias_ref, recv_ref, own_ref, low_ref, high_ref, pre_ref, down_ref, up_ref):
        table = term_ref[...]
        down_ref[...] = pick(low_ref[...], table)
        up_ref[...] = pick(high_ref[...], table)
        received = dot_split(mid_ref[...], weight_ref[...])
        pre_ref[...] = (
            pick(own_ref[...], table)
            + pick(recv_ref[...], received)
            + edge_terms(feat_ref[...], edge_ref[...])
            + bias_ref[...]
        )

    edge_block = shape(mesh_edges, units)
    mesh_pre, down_first, up_first = call(
        mesh_first_body,
        (edge_block, edge_block, edge_block),
        16 * mesh_edges * nodes * units,
        mesh_terms,
        mesh_mid,
        receiver_weight[1],
        mesh_edge_feats.reshape(-1, mesh_edges),
        edge_weight[1],
        first_bias[1:2],
        mesh_recv,
        own_nodes[0],
        low_nodes[0],
        high_nodes[0],
    )

    def add_others(first_ref, index_refs, table_refs):
        total = first_ref[...]
        for index_ref, table_ref in zip(index_refs, table_refs):
            total = total + pick(index_ref[...], table_ref[...])
        return total

    def mesh_sent_body(*refs):
        count = len(others)
        tables = refs[:count]
        refs = refs[count:]
        refs[-2][...] = add_others(refs[0], refs[2 : 2 + count], tables)
        refs[-1][...] = add_others(refs[1], refs[2 + count : 2 + 2 * count], tables)

    down, up = call(
        mesh_sent_body,
        (edge_block, edge_block),
        8 * mesh_edges * nodes * units,
        *others,
        down_first,
        up_first,
        *low_nodes[1:],
        *high_nodes[1:],
    )
    from_high = exchange(down, ("lat",), ((-1, False),))
    from_low = exchange(up, ("lat",), ((1, False),))

    def mesh_own_body(*refs):
        count = len(others)
        refs[-1][...] = add_others(refs[0], refs[1 : 1 + count], refs[1 + count : 1 + 2 * count])

    mesh_pre = call(
        mesh_own_body,
        edge_block,
        4 * mesh_edges * nodes * units,
        mesh_pre,
        *own_nodes[1:],
        *others,
    )

    def mesh_hidden_body(pre_ref, low_ref, high_ref, hidden_ref):
        total = pre_ref[...] + low_ref[...] + high_ref[...]
        hidden_ref[...] = total / (1.0 + jnp.exp(-total))

    mesh_hidden = call(
        mesh_hidden_body, edge_block, mesh_edges * units, mesh_pre, from_low, from_high
    )
    mesh_pieces = gather_hid(mesh_hidden)
    share = width // hid_count

    def mesh_message_body(*refs):
        place_ref = refs[0]
        refs = refs[1:]
        hidden_refs, weight_refs = refs[:hid_count], refs[hid_count : 2 * hid_count]
        bias_ref, gain_ref, shift_ref, recv_ref, mid_ref = refs[2 * hid_count : -2]
        out_ref, normed_ref = refs[-2:]
        place = place_ref[0]

        def own_part(value):
            part = value[:, :share]
            for step in range(1, hid_count):
                part = jnp.where(place == step, value[:, step * share : (step + 1) * share], part)
            return part

        def store(start, step, normed):
            high, low = split(own_part(normed))
            normed_ref[start : start + step, :share] = high
            normed_ref[start : start + step, share:] = low

        normed_chunks(hidden_refs, weight_refs, bias_ref, gain_ref, shift_ref, store)
        out_ref[...] = own_part(mid_ref[...]) + aggregate(recv_ref[...], nodes, normed_ref)

    vmem = pl.BlockSpec(memory_space=pltpu.VMEM)
    mesh_out = pl.pallas_call(
        mesh_message_body,
        out_shape=shape(nodes, share),
        in_specs=[pl.BlockSpec(memory_space=pltpu.SMEM)] + [vmem] * (2 * hid_count + 5),
        out_specs=vmem,
        scratch_shapes=[pltpu.VMEM((mesh_edges, 2 * share), BF16)],
        cost_estimate=pl.CostEstimate(
            flops=8 * mesh_edges * width * width, bytes_accessed=1 << 22, transcendentals=0
        ),
    )(
        hid_index.reshape(1).astype(jnp.int32),
        *mesh_pieces,
        *out_weights[1],
        out_bias[1:2],
        norm_gain[1:2],
        norm_shift[1:2],
        mesh_recv,
        mesh_mid,
    )
    return mesh_out.reshape(1, 1, nodes, share)


def solution(mesh):
    return jax.shard_map(
        per_device,
        mesh=mesh,
        in_specs=(
            P("lat", "lon", None),
            P("lat", "lon", None, None),
            P("lat", "lon", None, None),
            P("lat", "lon", None),
            P("lat", "lon", None),
            P("lat", "lon", None, None),
            P("lat", "lon", None),
            P("lat", "lon", None),
            P(None, None, "hid"),
            P(None, None, "hid"),
            P(None, None, "hid"),
            P(None, "hid"),
            P(None, "hid", None),
            P(),
            P(),
            P(),
        ),
        out_specs=P("lat", "lon", None, "hid"),
        check_vma=False,
    )
```

time: 208 us -> 97.6 us (0.47)
  waiting for transfers between devices: 135 us -> 21.1 us
  Pallas kernels: 0 us -> 31.8 us
  matrix products: 22.1 us -> 0 us
  starting transfers between devices: 6.08 us -> 22.8 us
  between operations: 13.8 us -> 0.21 us
  other arithmetic: 12.6 us -> 6.88 us
    psum x2 -> x0, waiting for transfers between devices: 86.7 us -> none  [normalise_whole(): summed = lax.psum(partial_value, 'hid') + out_bias[section_index]]
    pallas_call x0 -> x9, Pallas kernels: none -> 31.8 us  [the longest x7 20.7 us: call(): pl.pallas_call(body, out_shape=outs, cost_estimate=pl.CostEstimate(flops=...]
    ppermute x8 -> x15, waiting for transfers between devices: 48.7 us -> 21.1 us  [the longest x9 13.4 us: gather_hid(): lax.ppermute(source, 'hid', [(i, i ^ hop) for i in range(count)])]
    dot_general x10 -> x0, matrix products: 22.1 us -> none  [the longest x6 14.2 us: matmul(): jnp.dot(left, right, precision=HIGHEST, preferred_element_type=jnp.float32)]
    ppermute x8 -> x15, starting transfers between devices: 6.03 us -> 22.8 us  [the longest x6 12 us: exchange(): return lax.ppermute(value, axes if len(axes) > 1 else axes[0], pairs)]
    gather x4 -> x0, local copies, waits for them, and re-layouts: 11.8 us -> none  [the longest x2 4.45 us: aggregate(): jnp.take(recv_terms, jnp.clip(local_node, 0, node_count - 1), axis=0)]
    squeeze x0 -> x7, local copies, waits for them, and re-layouts: none -> 6.63 us  [the longest x4 3.35 us: per_device(): piece[section]]
    concatenate x3 -> x1, other arithmetic: 6.11 us -> 0.02 us  [rim_sent(): jnp.concatenate([terms[first * cols:(first + RIM) * cols], side_got[first...]
  transfers between devices with their start and end apart: 10 -> 15, of which waited for: 8 -> 6; matrix products, arithmetic and copies ran while one was open for 5% -> 17% of each run, Pallas kernels for 0% -> 17%
where the time goes in v1:
time: 97.6 us; the launch traced here: 95.9 us
  Pallas kernels  31.8 us (33%)
  starting transfers between devices  22.8 us (23%)
  waiting for transfers between devices  21.1 us (22%)
  local copies, waits for them, and re-layouts  13.2 us (14%)
  other arithmetic  6.88 us (7%)
    pallas_call x7, Pallas kernels, call(): pl.pallas_call(body, out_shape=outs, cost_estimate=pl.CostEstimate(flops=...  20.7 us
    ppermute x9, waiting for transfers between devices, gather_hid(): lax.ppermute(source, 'hid', [(i, i ^ hop) for i in range(count)])  13.4 us
    ppermute x6, starting transfers between devices, exchange(): return lax.ppermute(value, axes if len(axes) > 1 else axes[0], pairs)  12 us
    ppermute x9, starting transfers between devices, gather_hid(): lax.ppermute(source, 'hid', [(i, i ^ hop) for i in range(count)])  10.7 us
    ppermute x6, waiting for transfers between devices, exchange(): return lax.ppermute(value, axes if len(axes) > 1 else axes[0], pairs)  7.63 us
    pallas_call x1, Pallas kernels, per_device(): pl.pallas_call(grid_message_body, out_shape=(shape(nodes, width), shape(n...  6.98 us
    pallas_call x1, Pallas kernels, per_device(): pl.pallas_call(mesh_message_body, out_shape=shape(nodes, share), in_specs...  4.09 us
    unnamed x46, local copies, waits for them, and re-layouts  3.8 us
  transfers between devices with their start and end apart: 15, of which 6 were waited for; matrix products, arithmetic and copies ran while one was open for 17% of the time, Pallas kernels for 17%

profile of v1, /device:TPU:9, one launch (start us, length us, event | category | flops | bytes accessed | tf_op | source)
XLA Modules:
  0.0 95.9 jit_solution(13782528226571478080)
XLA Ops:
  0.0 1.2 %collective-permute-start.7 = (f32[2,128,512]{2,1,0:T(8,128)}, f32[2,128,512]{2,1,0:T(8,128)S(1)}, u32[]{:S(2)}, u32[]{:S(2)}) collective-permute-start(f32[2,128,512]{2,1,0:T(8,128)} %param.28), channel_id=1, source_target_pairs={{0,2},{1,3},{2,0},{3,1},{4,6},{5,7},{6,4},{7,5},{8,10},{9,11},{10,... | collective-permute-start | bytes 1572872 | tf_op jit(solution)/shard_map/ppermute | solution.py:106
  1.2 1.0 collective-permute-start.6
  2.2 1.9 %slice_bitcast_fusion.8 = (f32[512,128]{1,0:T(8,128)}, f32[512,128]{1,0:T(8,128)}) fusion(f32[2,512,128]{2,1,0:T(8,128)} %param.25), kind=kLoop, calls=%fused_computation.8 | loop fusion | bytes 1048576 | tf_op jit(solution)/shard_map/squeeze | solution.py:319
  4.1 3.5 %shard_map.154 = (f32[1024,128]{1,0:T(8,128)}, f32[32,128]{1,0:T(8,128)}) custom-call(f32[1024,512]{1,0:T(8,128)} %bitcast.70, f32[512,128]{1,0:T(8,128)} %get-tuple-element.55.weight_ref), custom_call_target="tpu_custom_call" | custom-call | flops 402653184 | bytes 1048576 | tf_op jit(solution)/shard_map/pallas_call | solution.py:68
  7.5 1.2 %collective-permute-start = (f32[32,128]{1,0:T(8,128)}, f32[32,128]{1,0:T(8,128)S(1)}, u32[]{:S(2)}, u32[]{:S(2)}) collective-permute-start(f32[32,128]{1,0:T(8,128)} %get-tuple-element.15), channel_id=1, source_target_pairs={{0,4},{4,0},{1,5},{5,1},{2,6},{6,2},{3,7},{7,3},{8,12},{12,8},{9,1... | collective-permute-start | bytes 49160 | tf_op jit(solution)/shard_map/ppermute | solution.py:98
  8.8 0.8 slice_bitcast_fusion.6
  9.7 1.0 %fusion.13 = (f32[256,128]{1,0:T(8,128)S(1)}, f32[256,128]{1,0:T(8,128)S(1)}) fusion(f32[1024,128]{1,0:T(8,128)} %get-tuple-element.14.term_ref), kind=kLoop, calls=%fused_computation.94 | loop fusion | bytes 524288 | tf_op jit(solution)/shard_map/slice | solution.py:236
  10.7 0.8 slice_bitcast_fusion.7
  11.5 0.6 slice_bitcast_fusion.12
  12.7 0.6 subtract_bitcast_fusion.recv_ref.refs_11_
  13.9 0.7 fusion.1
  14.5 0.6 and_select_fusion.send_ref
  15.1 0.6 fusion.15
  15.7 0.6 and_select_fusion.6
  17.0 2.1 %collective-permute-start.2 = (f32[272,128]{1,0:T(8,128)S(1)}, f32[272,128]{1,0:T(8,128)S(1)}, u32[]{:S(2)}, u32[]{:S(2)}) collective-permute-start(f32[272,128]{1,0:T(8,128)S(1)} %get-tuple-element.68), channel_id=1, source_target_pairs={{8,0},{16,8},{24,16},{9,1},{17,9},{25,17},{10,2},{18,10},{26,18},{... | collective-permute-start | bytes 417800 | tf_op jit(solution)/shard_map/ppermute | solution.py:98
  19.1 3.2 %collective-permute-start.1 = (f32[272,128]{1,0:T(8,128)S(1)}, f32[272,128]{1,0:T(8,128)S(1)}, u32[]{:S(2)}, u32[]{:S(2)}) collective-permute-start(f32[272,128]{1,0:T(8,128)S(1)} %get-tuple-element.69), channel_id=1, source_target_pairs={{0,8},{8,16},{16,24},{1,9},{9,17},{17,25},{2,10},{10,18},{18,26},{... | collective-permute-start | bytes 417800 | tf_op jit(solution)/shard_map/ppermute | solution.py:98
  22.9 4.1 %shard_map.155.pre_ref = f32[1024,128]{1,0:T(8,128)} custom-call(f32[1024,128]{1,0:T(8,128)} %get-tuple-element.14.term_ref, f32[512,512]{1,0:T(8,128)} %bitcast.74, f32[512,128]{1,0:T(8,128)} %get-tuple-element.53.weight_ref, f32[4,1024]{1,0:T(4,128)} %bitcast.76, f32[4,128]{1,0:T(4,128)} %get-tuple-element.67.edge_ref, ...), custom_call_target="tpu_custom_call" | custom-call | flops 1073741824 | bytes 1048576 | tf_op jit(solution)/shard_map/pallas_call | solution.py:68
  27.0 0.6 copy-done.16
  27.7 2.6 %shard_map.156.refs_0_ = f32[1024,128]{1,0:T(8,128)} custom-call(f32[1024,128]{1,0:T(8,128)} %shard_map.155.pre_ref, f32[32,128]{1,0:T(8,128)} %copy-done.7, f32[272,128]{1,0:T(8,128)} %copy-done.15, f32[272,128]{1,0:T(8,128)} %copy-done.16, s32[1,1024]{1,0:T(1,128)} %get-tuple-element.41.send_ref), custom_call_target="tpu_custom_call" | custom-call | flops 536870912 | bytes 1048576 | tf_op jit(solution)/shard_map/pallas_call | solution.py:68
  30.5 1.1 %collective-permute-start.3 = (f32[1024,128]{1,0:T(8,128)}, f32[1024,128]{1,0:T(8,128)S(1)}, u32[]{:S(2)}, u32[]{:S(2)}) collective-permute-start(f32[1024,128]{1,0:T(8,128)} %shard_map.156.refs_0_), channel_id=1, source_target_pairs={{0,1},{1,0},{2,3},{3,2},{4,5},{5,4},{6,7},{7,6},{8,9},{9,8},{10,11... | collective-permute-start | bytes 1572872 | tf_op jit(solution)/shard_map/ppermute | solution.py:106
  31.6 0.7 slice_convert_fusion
  32.3 0.7 slice_convert_fusion.1
  33.0 0.6 and_select_fusion.4
  33.7 0.6 and_select_fusion.8.high_ref
  34.3 8.8 %collective-permute-done.4.refs_2_ = f32[1024,128]{1,0:T(8,128)S(1)} collective-permute-done((f32[1024,128]{1,0:T(8,128)}, f32[1024,128]{1,0:T(8,128)S(1)}, u32[]{:S(2)}, u32[]{:S(2)}) %collective-permute-start.4) | collective-permute-done | bytes 524320 | tf_op jit(solution)/shard_map/ppermute | solution.py:106
  43.1 1.7 %collective-permute-start.5 = (f32[1024,128]{1,0:T(8,128)S(1)}, f32[1024,128]{1,0:T(8,128)S(1)}, u32[]{:S(2)}, u32[]{:S(2)}) collective-permute-start(f32[1024,128]{1,0:T(8,128)S(1)} %collective-permute-done.4.refs_2_), channel_id=1, source_target_pairs={{0,1},{1,0},{2,3},{3,2},{4,5},{5,4},{6,7},{7,6},{8,9},{9,8},{10,11... | collective-permute-start | bytes 1572872 | tf_op jit(solution)/shard_map/ppermute | solution.py:106
  44.8 0.8 slice_bitcast_fusion.1
  45.6 0.8 slice_bitcast_fusion.2
  46.5 0.8 slice_bitcast_fusion
  47.4 0.8 copy-done.18
  48.3 7.0 %shard_map.157 = (f32[512,512]{1,0:T(8,128)}, f32[512,128]{1,0:T(8,128)}) custom-call(f32[1024,128]{1,0:T(8,128)} %shard_map.156.refs_0_, f32[1024,128]{1,0:T(8,128)} %copy-done.18, f32[1024,128]{1,0:T(8,128)} %copy-done.17, f32[1024,128]{1,0:T(8,128)} %copy-done.19, f32[128,512]{1,0:T(8,128)} %get-tuple-element.51.refs_4_, ...), custom_call_target="tpu_custom_call" | custom-call | flops 3221225472 | bytes 4194304 | tf_op jit(solution)/shard_map/pallas_call | solution.py:304
  56.1 4.2 %shard_map.158 = (f32[512,128]{1,0:T(8,128)}, f32[512,128]{1,0:T(8,128)}, f32[512,128]{1,0:T(8,128)}) custom-call(f32[512,128]{1,0:T(8,128)} %get-tuple-element.16.term_ref, f32[512,512]{1,0:T(8,128)} %get-tuple-element.17.mid_ref.refs_13_, f32[512,128]{1,0:T(8,128)} %get-tuple-element.52.weight_ref, f32[4,512]{1,0:T(4,128)} %bitcast.77, ...), custom_call_target="tpu_custom_call" | custom-call | flops 536870912 | bytes 1048576 | tf_op jit(solution)/shard_map/pallas_call | solution.py:68
  60.3 3.1 %collective-permute-done.9.refs_2_.refs_0_ = f32[512,128]{1,0:T(8,128)S(1)} collective-permute-done((f32[512,128]{1,0:T(8,128)}, f32[512,128]{1,0:T(8,128)S(1)}, u32[]{:S(2)}, u32[]{:S(2)}) %collective-permute-start.9) | collective-permute-done | bytes 262176 | tf_op jit(solution)/shard_map/ppermute | solution.py:98
  63.3 0.7 copy-done.2
  64.0 2.4 %shard_map.160 = (f32[512,128]{1,0:T(8,128)}, f32[512,128]{1,0:T(8,128)}) custom-call(f32[512,128]{1,0:T(8,128)} %copy-done.2, f32[512,128]{1,0:T(8,128)} %get-tuple-element.19.refs_1_, f32[512,128]{1,0:T(8,128)} %get-tuple-element.20.refs_2_, s32[1,512]{1,0:T(1,128)} %get-tuple-element.72.refs_3_, s32[1,512]{1,0:T(1,128)} %get-tuple-element.23.refs_4_), custom_call_target="tpu_custom_call" | custom-call | flops 268435456 | bytes 1048576 | tf_op jit(solution)/shard_map/pallas_call | solution.py:68
  66.4 3.2 %collective-permute-start.10 = (f32[512,128]{1,0:T(8,128)}, f32[512,128]{1,0:T(8,128)S(1)}, u32[]{:S(2)}, u32[]{:S(2)}) collective-permute-start(f32[512,128]{1,0:T(8,128)} %get-tuple-element.21), channel_id=1, source_target_pairs={{0,8},{8,16},{16,24},{1,9},{9,17},{17,25},{2,10},{10,18},{18,26},{... | collective-permute-start | bytes 786440 | tf_op jit(solution)/shard_map/ppermute | solution.py:98
  69.7 2.1 %collective-permute-start.11 = (f32[512,128]{1,0:T(8,128)}, f32[512,128]{1,0:T(8,128)S(1)}, u32[]{:S(2)}, u32[]{:S(2)}) collective-permute-start(f32[512,128]{1,0:T(8,128)} %get-tuple-element.22), channel_id=1, source_target_pairs={{8,0},{16,8},{24,16},{9,1},{17,9},{25,17},{10,2},{18,10},{26,18},{... | collective-permute-start | bytes 786440 | tf_op jit(solution)/shard_map/ppermute | solution.py:98
  71.7 2.1 %shard_map.159.pre_ref = f32[512,128]{1,0:T(8,128)} custom-call(f32[512,128]{1,0:T(8,128)} %get-tuple-element.18.refs_0_, s32[1,512]{1,0:T(1,128)} %get-tuple-element.29.refs_1_, f32[512,128]{1,0:T(8,128)} %copy-done.2), custom_call_target="tpu_custom_call" | custom-call | flops 134217728 | bytes 1048576 | tf_op jit(solution)/shard_map/pallas_call | solution.py:68
  73.9 1.6 %collective-permute-done.10.low_ref = f32[512,128]{1,0:T(8,128)S(1)} collective-permute-done((f32[512,128]{1,0:T(8,128)}, f32[512,128]{1,0:T(8,128)S(1)}, u32[]{:S(2)}, u32[]{:S(2)}) %collective-permute-start.10) | collective-permute-done | bytes 262176 | tf_op jit(solution)/shard_map/ppermute | solution.py:98
  75.5 2.9 %collective-permute-done.11.high_ref = f32[512,128]{1,0:T(8,128)S(1)} collective-permute-done((f32[512,128]{1,0:T(8,128)}, f32[512,128]{1,0:T(8,128)S(1)}, u32[]{:S(2)}, u32[]{:S(2)}) %collective-permute-start.11) | collective-permute-done | bytes 262176 | tf_op jit(solution)/shard_map/ppermute | solution.py:98
  78.4 0.7 copy-done.4
  79.1 1.9 %shard_map.161.refs_1_ = f32[512,128]{1,0:T(8,128)} custom-call(f32[512,128]{1,0:T(8,128)} %shard_map.159.pre_ref, f32[512,128]{1,0:T(8,128)} %copy-done.3, f32[512,128]{1,0:T(8,128)} %copy-done.4), custom_call_target="tpu_custom_call" | custom-call | flops 65536 | bytes 1048576 | tf_op jit(solution)/shard_map/pallas_call | solution.py:68
  81.3 2.3 %collective-permute-start.12 = (f32[512,128]{1,0:T(8,128)}, f32[512,128]{1,0:T(8,128)S(1)}, u32[]{:S(2)}, u32[]{:S(2)}) collective-permute-start(f32[512,128]{1,0:T(8,128)} %shard_map.161.refs_1_), channel_id=1, source_target_pairs={{0,1},{1,0},{2,3},{3,2},{4,5},{5,4},{6,7},{7,6},{8,9},{9,8},{10,11... | collective-permute-start | bytes 786440 | tf_op jit(solution)/shard_map/ppermute | solution.py:106
  83.6 3.4 %collective-permute-done.13.refs_3_ = f32[512,128]{1,0:T(8,128)S(1)} collective-permute-done((f32[512,128]{1,0:T(8,128)}, f32[512,128]{1,0:T(8,128)S(1)}, u32[]{:S(2)}, u32[]{:S(2)}) %collective-permute-start.13) | collective-permute-done | bytes 262176 | tf_op jit(solution)/shard_map/ppermute | solution.py:106
  87.0 2.9 %collective-permute-start.14 = (f32[512,128]{1,0:T(8,128)S(1)}, f32[512,128]{1,0:T(8,128)S(1)}, u32[]{:S(2)}, u32[]{:S(2)}) collective-permute-start(f32[512,128]{1,0:T(8,128)S(1)} %collective-permute-done.13.refs_3_), channel_id=1, source_target_pairs={{0,1},{1,0},{2,3},{3,2},{4,5},{5,4},{6,7},{7,6},{8,9},{9,8},{10,11... | collective-permute-start | bytes 786440 | tf_op jit(solution)/shard_map/ppermute | solution.py:106
  90.0 1.2 %collective-permute-done.14.refs_4_ = f32[512,128]{1,0:T(8,128)S(1)} collective-permute-done((f32[512,128]{1,0:T(8,128)S(1)}, f32[512,128]{1,0:T(8,128)S(1)}, u32[]{:S(2)}, u32[]{:S(2)}) %collective-permute-start.14) | collective-permute-done | bytes 262176 | tf_op jit(solution)/shard_map/ppermute | solution.py:106
  91.1 0.7 copy-done.22
  91.8 4.1 %shard_map.162 = f32[512,128]{1,0:T(8,128)} custom-call(s32[1]{0:T(128)} %bitcast.refs_0_, f32[512,128]{1,0:T(8,128)} %shard_map.161.refs_1_, f32[512,128]{1,0:T(8,128)} %copy-done.21, f32[512,128]{1,0:T(8,128)} %copy-done.20, f32[512,128]{1,0:T(8,128)} %copy-done.22, f32[128,512]{1,0:T(8,128)} %get-tuple-element.50.refs_5_, ...), custom_call_target="tpu_custom_call" | custom-call | flops 1073741824 | bytes 4194304 | tf_op jit(solution)/shard_map/pallas_call | solution.py:438
  (66 shorter events, 4.1 us)
Async XLA Ops:
  0.0 8.8 %copy-start.1 = (f32[2,128,512]{2,1,0:T(8,128)S(1)}, f32[2,128,512]{2,1,0:T(8,128)}, u32[]{:S(2)}) copy-start(f32[2,128,512]{2,1,0:T(8,128)} %param.28) | copy-start | bytes 1572868
  0.0 9.6 %copy-start.5 = (s32[1,1,512]{2,1,0:T(1,128)S(1)}, s32[1,1,512]{2,1,0:T(1,128)}, u32[]{:S(2)}) copy-start(s32[1,1,512]{2,1,0:T(1,128)} %param.22) | copy-start | bytes 6148
  0.0 33.7 %collective-permute-start.7 = (f32[2,128,512]{2,1,0:T(8,128)}, f32[2,128,512]{2,1,0:T(8,128)S(1)}, u32[]{:S(2)}, u32[]{:S(2)}) collective-permute-start(f32[2,128,512]{2,1,0:T(8,128)} %param.28), channel_id=1, source_target_pairs={{0,2},{1,3},{2,0},{3,1},{4,6},{5,7},{6,4},{7,5},{8,10},{9,11},{10,... | collective-permute-start | bytes 1572872 | tf_op jit(solution)/shard_map/ppermute | solution.py:106
  1.2 44.4 %collective-permute-start.6 = (f32[2,128,512]{2,1,0:T(8,128)}, f32[2,128,512]{2,1,0:T(8,128)S(1)}, u32[]{:S(2)}, u32[]{:S(2)}) collective-permute-start(f32[2,128,512]{2,1,0:T(8,128)} %param.28), channel_id=1, source_target_pairs={{0,1},{1,0},{2,3},{3,2},{4,5},{5,4},{6,7},{7,6},{8,9},{9,8},{10,11... | collective-permute-start | bytes 1572872 | tf_op jit(solution)/shard_map/ppermute | solution.py:106
  4.0 6.6 %copy-start = (f32[2,512,128]{2,1,0:T(8,128)S(1)}, f32[2,512,128]{2,1,0:T(8,128)}, u32[]{:S(2)}) copy-start(f32[2,512,128]{2,1,0:T(8,128)} %param.26) | copy-start | bytes 1572868
  4.0 7.5 %copy-start.8 = (f32[2,4,128]{2,1,0:T(4,128)S(1)}, f32[2,4,128]{2,1,0:T(4,128)}, u32[]{:S(2)}) copy-start(f32[2,4,128]{2,1,0:T(4,128)} %param.24) | copy-start | bytes 12292
  4.0 8.1 %copy-start.9 = (f32[2,512]{1,0:T(2,128)S(1)}, f32[2,512]{1,0:T(2,128)}, u32[]{:S(2)}) copy-start(f32[2,512]{1,0:T(2,128)} %param.29) | copy-start | bytes 12292
  4.0 8.7 %copy-start.10 = (s32[1,1,1024]{2,1,0:T(1,128)S(1)}, s32[1,1,1024]{2,1,0:T(1,128)}, u32[]{:S(2)}) copy-start(s32[1,1,1024]{2,1,0:T(1,128)} %param.20) | copy-start | bytes 12292
  4.0 9.2 %copy-start.13 = (s32[1,1,512]{2,1,0:T(1,128)S(1)}, s32[1,1,512]{2,1,0:T(1,128)}, u32[]{:S(2)}) copy-start(s32[1,1,512]{2,1,0:T(1,128)} %param.23) | copy-start | bytes 6148
  4.1 9.8 %copy-start.6 = (s32[1,1,1024]{2,1,0:T(1,128)S(1)}, s32[1,1,1024]{2,1,0:T(1,128)}, u32[]{:S(2)}) copy-start(s32[1,1,1024]{2,1,0:T(1,128)} %param.19) | copy-start | bytes 12292
  4.1 11.1 %copy-start.11 = (f32[2,512]{1,0:T(2,128)S(1)}, f32[2,512]{1,0:T(2,128)}, u32[]{:S(2)}) copy-start(f32[2,512]{1,0:T(2,128)} %param.31) | copy-start | bytes 12292
  4.1 11.1 %copy-start.12 = (f32[2,512]{1,0:T(2,128)S(1)}, f32[2,512]{1,0:T(2,128)}, u32[]{:S(2)}) copy-start(f32[2,512]{1,0:T(2,128)} %param.30) | copy-start | bytes 12292
  7.5 14.7 %copy-start.14 = (f32[2,128]{1,0:T(2,128)S(1)}, f32[2,128]{1,0:T(2,128)}, u32[]{:S(2)}) copy-start(f32[2,128]{1,0:T(2,128)} %param.27) | copy-start | bytes 3076
  7.5 9.4 %collective-permute-start = (f32[32,128]{1,0:T(8,128)}, f32[32,128]{1,0:T(8,128)S(1)}, u32[]{:S(2)}, u32[]{:S(2)}) collective-permute-start(f32[32,128]{1,0:T(8,128)} %get-tuple-element.15), channel_id=1, source_target_pairs={{0,4},{4,0},{1,5},{5,1},{2,6},{6,2},{3,7},{7,3},{8,12},{12,8},{9,1... | collective-permute-start | bytes 49160 | tf_op jit(solution)/shard_map/ppermute | solution.py:98
  16.9 10.0 %copy-start.7 = (f32[32,128]{1,0:T(8,128)}, f32[32,128]{1,0:T(8,128)S(1)}, u32[]{:S(2)}) copy-start(f32[32,128]{1,0:T(8,128)S(1)} %collective-permute-done.side_ref) | copy-start | bytes 49156
  17.0 10.0 %collective-permute-start.2 = (f32[272,128]{1,0:T(8,128)S(1)}, f32[272,128]{1,0:T(8,128)S(1)}, u32[]{:S(2)}, u32[]{:S(2)}) collective-permute-start(f32[272,128]{1,0:T(8,128)S(1)} %get-tuple-element.68), channel_id=1, source_target_pairs={{8,0},{16,8},{24,16},{9,1},{17,9},{25,17},{10,2},{18,10},{26,18},{... | collective-permute-start | bytes 417800 | tf_op jit(solution)/shard_map/ppermute | solution.py:98
  19.1 7.9 %collective-permute-start.1 = (f32[272,128]{1,0:T(8,128)S(1)}, f32[272,128]{1,0:T(8,128)S(1)}, u32[]{:S(2)}, u32[]{:S(2)}) collective-permute-start(f32[272,128]{1,0:T(8,128)S(1)} %get-tuple-element.69), channel_id=1, source_target_pairs={{0,8},{8,16},{16,24},{1,9},{9,17},{17,25},{2,10},{10,18},{18,26},{... | collective-permute-start | bytes 417800 | tf_op jit(solution)/shard_map/ppermute | solution.py:98
  26.9 0.7 copy-start.16
  27.0 0.7 copy-start.15
  30.3 12.8 %collective-permute-start.4 = (f32[1024,128]{1,0:T(8,128)}, f32[1024,128]{1,0:T(8,128)S(1)}, u32[]{:S(2)}, u32[]{:S(2)}) collective-permute-start(f32[1024,128]{1,0:T(8,128)} %shard_map.156.refs_0_), channel_id=1, source_target_pairs={{0,2},{1,3},{2,0},{3,1},{4,6},{5,7},{6,4},{7,5},{8,10},{9,11},{10,... | collective-permute-start | bytes 1572872 | tf_op jit(solution)/shard_map/ppermute | solution.py:106
  30.5 16.8 %collective-permute-start.3 = (f32[1024,128]{1,0:T(8,128)}, f32[1024,128]{1,0:T(8,128)S(1)}, u32[]{:S(2)}, u32[]{:S(2)}) collective-permute-start(f32[1024,128]{1,0:T(8,128)} %shard_map.156.refs_0_), channel_id=1, source_target_pairs={{0,1},{1,0},{2,3},{3,2},{4,5},{5,4},{6,7},{7,6},{8,9},{9,8},{10,11... | collective-permute-start | bytes 1572872 | tf_op jit(solution)/shard_map/ppermute | solution.py:106
  33.7 12.8 %collective-permute-start.8 = (f32[2,128,512]{2,1,0:T(8,128)S(1)}, f32[2,128,512]{2,1,0:T(8,128)S(1)}, u32[]{:S(2)}, u32[]{:S(2)}) collective-permute-start(f32[2,128,512]{2,1,0:T(8,128)S(1)} %collective-permute-done.7), channel_id=1, source_target_pairs={{0,1},{1,0},{2,3},{3,2},{4,5},{5,4},{6,7},{7,6},{8,9},{9,8},{10,11... | collective-permute-start | bytes 1572872 | tf_op jit(solution)/shard_map/ppermute | solution.py:106
  43.1 4.2 %copy-start.17 = (f32[1024,128]{1,0:T(8,128)}, f32[1024,128]{1,0:T(8,128)S(1)}, u32[]{:S(2)}) copy-start(f32[1024,128]{1,0:T(8,128)S(1)} %collective-permute-done.4.refs_2_) | copy-start | bytes 1572868
  43.1 4.2 %collective-permute-start.5 = (f32[1024,128]{1,0:T(8,128)S(1)}, f32[1024,128]{1,0:T(8,128)S(1)}, u32[]{:S(2)}, u32[]{:S(2)}) collective-permute-start(f32[1024,128]{1,0:T(8,128)S(1)} %collective-permute-done.4.refs_2_), channel_id=1, source_target_pairs={{0,1},{1,0},{2,3},{3,2},{4,5},{5,4},{6,7},{7,6},{8,9},{9,8},{10,11... | collective-permute-start | bytes 1572872 | tf_op jit(solution)/shard_map/ppermute | solution.py:106
  47.3 0.8 copy-start.18
  47.3 1.0 %copy-start.19 = (f32[1024,128]{1,0:T(8,128)}, f32[1024,128]{1,0:T(8,128)S(1)}, u32[]{:S(2)}) copy-start(f32[1024,128]{1,0:T(8,128)S(1)} %collective-permute-done.5.refs_3_) | copy-start | bytes 1572868
  55.3 8.0 %collective-permute-start.9 = (f32[512,128]{1,0:T(8,128)}, f32[512,128]{1,0:T(8,128)S(1)}, u32[]{:S(2)}, u32[]{:S(2)}) collective-permute-start(f32[512,128]{1,0:T(8,128)} %get-tuple-element.16.term_ref), channel_id=1, source_target_pairs={{0,4},{4,0},{1,5},{5,1},{2,6},{6,2},{3,7},{7,3},{8,12},{12,8},{9,1... | collective-permute-start | bytes 786440 | tf_op jit(solution)/shard_map/ppermute | solution.py:98
  63.3 0.7 copy-start.2
  66.4 9.0 %collective-permute-start.10 = (f32[512,128]{1,0:T(8,128)}, f32[512,128]{1,0:T(8,128)S(1)}, u32[]{:S(2)}, u32[]{:S(2)}) collective-permute-start(f32[512,128]{1,0:T(8,128)} %get-tuple-element.21), channel_id=1, source_target_pairs={{0,8},{8,16},{16,24},{1,9},{9,17},{17,25},{2,10},{10,18},{18,26},{... | collective-permute-start | bytes 786440 | tf_op jit(solution)/shard_map/ppermute | solution.py:98
  69.7 8.8 %collective-permute-start.11 = (f32[512,128]{1,0:T(8,128)}, f32[512,128]{1,0:T(8,128)S(1)}, u32[]{:S(2)}, u32[]{:S(2)}) collective-permute-start(f32[512,128]{1,0:T(8,128)} %get-tuple-element.22), channel_id=1, source_target_pairs={{8,0},{16,8},{24,16},{9,1},{17,9},{25,17},{10,2},{18,10},{26,18},{... | collective-permute-start | bytes 786440 | tf_op jit(solution)/shard_map/ppermute | solution.py:98
  75.5 2.9 %copy-start.3 = (f32[512,128]{1,0:T(8,128)}, f32[512,128]{1,0:T(8,128)S(1)}, u32[]{:S(2)}) copy-start(f32[512,128]{1,0:T(8,128)S(1)} %collective-permute-done.10.low_ref) | copy-start | bytes 786436
  78.4 0.7 copy-start.4
  81.0 6.0 %collective-permute-start.13 = (f32[512,128]{1,0:T(8,128)}, f32[512,128]{1,0:T(8,128)S(1)}, u32[]{:S(2)}, u32[]{:S(2)}) collective-permute-start(f32[512,128]{1,0:T(8,128)} %shard_map.161.refs_1_), channel_id=1, source_target_pairs={{0,2},{1,3},{2,0},{3,1},{4,6},{5,7},{6,4},{7,5},{8,10},{9,11},{10,... | collective-permute-start | bytes 786440 | tf_op jit(solution)/shard_map/ppermute | solution.py:106
  81.3 8.7 %collective-permute-start.12 = (f32[512,128]{1,0:T(8,128)}, f32[512,128]{1,0:T(8,128)S(1)}, u32[]{:S(2)}, u32[]{:S(2)}) collective-permute-start(f32[512,128]{1,0:T(8,128)} %shard_map.161.refs_1_), channel_id=1, source_target_pairs={{0,1},{1,0},{2,3},{3,2},{4,5},{5,4},{6,7},{7,6},{8,9},{9,8},{10,11... | collective-permute-start | bytes 786440 | tf_op jit(solution)/shard_map/ppermute | solution.py:106
  87.0 4.1 %copy-start.20 = (f32[512,128]{1,0:T(8,128)}, f32[512,128]{1,0:T(8,128)S(1)}, u32[]{:S(2)}) copy-start(f32[512,128]{1,0:T(8,128)S(1)} %collective-permute-done.13.refs_3_) | copy-start | bytes 786436
  87.0 4.1 %collective-permute-start.14 = (f32[512,128]{1,0:T(8,128)S(1)}, f32[512,128]{1,0:T(8,128)S(1)}, u32[]{:S(2)}, u32[]{:S(2)}) collective-permute-start(f32[512,128]{1,0:T(8,128)S(1)} %collective-permute-done.13.refs_3_), channel_id=1, source_target_pairs={{0,1},{1,0},{2,3},{3,2},{4,5},{5,4},{6,7},{7,6},{8,9},{9,8},{10,11... | collective-permute-start | bytes 786440 | tf_op jit(solution)/shard_map/ppermute | solution.py:106
  90.0 1.2 %copy-start.21 = (f32[512,128]{1,0:T(8,128)}, f32[512,128]{1,0:T(8,128)S(1)}, u32[]{:S(2)}) copy-start(f32[512,128]{1,0:T(8,128)S(1)} %collective-permute-done.12.refs_2_) | copy-start | bytes 786436
  91.1 0.7 copy-start.22

commit v2 on v1

v2 whole, which is shorter than its diff:
```python
import jax
import jax.numpy as jnp
from jax import lax
from jax.experimental import pallas as pl
from jax.experimental.pallas import tpu as pltpu
from jax.sharding import PartitionSpec as P

RIM = 2
LANES = 128
EDGE_CHUNK = 256
epsilon = 1e-05
F32 = jnp.float32
BF16 = jnp.bfloat16


def split(value):
    high = value.astype(BF16)
    low = (value - high.astype(F32)).astype(BF16)
    return high, low


def dot(left, right):
    return jnp.dot(left, right, preferred_element_type=F32)


def dot_split(left, right):
    left_high, left_low = split(left)
    right_high, right_low = split(right)
    return dot(
        jnp.concatenate([left_high, left_high, left_low], axis=1),
        jnp.concatenate([right_high, right_low, right_high], axis=0),
    )


def down_lanes(index_row):
    return jnp.transpose(jnp.broadcast_to(index_row, (LANES, index_row.shape[1])))


def onehot_rows(index_cols, count):
    lane = lax.broadcasted_iota(jnp.int32, index_cols.shape, 1)
    blocks = [
        jnp.where(index_cols == lane + start, 1.0, 0.0).astype(BF16)
        for start in range(0, count, LANES)
    ]
    return jnp.concatenate(blocks, axis=1)


def pick(index_row, table):
    width = table.shape[1]
    high, low = split(table)
    both = dot(
        onehot_rows(down_lanes(index_row), table.shape[0]), jnp.concatenate([high, low], axis=1)
    )
    return both[:, :width] + both[:, width:]


def edge_terms(feats, weight):
    return lax.dot_general(
        feats,
        weight,
        (((0,), (0,)), ((), ())),
        precision=lax.Precision.HIGHEST,
        preferred_element_type=F32,
    )


def divide(value, count):
    if count & (count - 1) == 0:
        return value >> (count.bit_length() - 1), value & (count - 1)
    return value // count, value % count


VMEM = pl.BlockSpec(memory_space=pltpu.VMEM)


def call(name, body, outs, flops, args, scratch=()):
    return pl.pallas_call(
        body,
        out_shape=outs,
        in_specs=[VMEM] * len(args),
        out_specs=jax.tree.map(lambda _: VMEM, outs),
        scratch_shapes=scratch,
        name=name,
        cost_estimate=pl.CostEstimate(flops=flops, bytes_accessed=1 << 20, transcendentals=0),
    )(*args)


def shape(*dims, dtype=F32):
    return jax.ShapeDtypeStruct(dims, dtype)


def shift(value, axis, step):
    count = lax.axis_size(axis)
    return lax.ppermute(value, axis, [(i, (i + step) % count) for i in range(count)])


def swap_lat(value, first):
    count = lax.axis_size("lat")
    pairs = [(i, i + 1) for i in range(first, count - 1, 2)]
    return lax.ppermute(value, "lat", pairs + [(high, low) for low, high in pairs])


def gather_hid(value):
    count = lax.axis_size("hid")
    pieces = [value]
    for step in range(1, count):
        source, hop = (pieces[step - 1], 1) if step % 2 else (value, step)
        pieces.append(lax.ppermute(source, "hid", [(i, i ^ hop) for i in range(count)]))
    return pieces


def layer_norm(message, gain, shift):
    centred = message - jnp.mean(message, axis=1, keepdims=True)
    spread = jnp.mean(centred * centred, axis=1, keepdims=True)
    return centred * lax.rsqrt(spread + epsilon) * gain + shift


def normed_chunks(hidden_refs, weight_ref, bias, gain, shift_row, store):
    edges = hidden_refs[0].shape[0]
    step = min(EDGE_CHUNK, edges)
    for start in range(0, edges, step):
        left = jnp.concatenate([ref[start : start + step, :] for ref in hidden_refs], axis=1)
        left_high, left_low = split(left)
        left = jnp.concatenate([left_high, left_high, left_low], axis=1)
        message = dot(left, weight_ref[...]) + bias
        store(start, step, layer_norm(message, gain, shift_row))


def aggregate(receiver_row, nodes, normed_ref):
    node = lax.broadcasted_iota(jnp.int32, (nodes, receiver_row.shape[1]), 0)
    onehot = jnp.where(node == receiver_row, 1.0, 0.0).astype(BF16)
    width = normed_ref.shape[1] // 2
    both = dot(onehot, normed_ref[...])
    return both[:, :width] + both[:, width:]


def per_device(
    grid_latent,
    mesh_latent,
    grid_edge_feats,
    grid_senders,
    grid_receivers,
    mesh_edge_feats,
    mesh_senders,
    mesh_receivers,
    edge_weight,
    sender_weight,
    receiver_weight,
    first_bias,
    out_weight,
    out_bias,
    norm_gain,
    norm_shift,
):
    lon_count = lax.axis_size("lon")
    hid_count = lax.axis_size("hid")
    rows, cols, width = grid_latent.shape
    nodes = mesh_latent.shape[2]
    units = sender_weight.shape[2]
    grid_edges = grid_senders.shape[2]
    mesh_edges = mesh_senders.shape[2]
    mesh_own = mesh_latent.reshape(nodes, width)
    cells = grid_latent.reshape(rows * cols, width)
    grid_ids = grid_senders.reshape(1, grid_edges)
    grid_to = grid_receivers.reshape(1, grid_edges)
    mesh_ids = mesh_senders.reshape(1, mesh_edges)
    mesh_to = mesh_receivers.reshape(1, mesh_edges)
    two_lon = lon_count == 2
    side_size = rows * 2 * RIM
    id_rows = mesh_edges // LANES
    lat_size = RIM * cols + RIM * 2 * RIM
    lat_rows = lat_size + id_rows + -(lat_size + id_rows) % 16

    def local(receivers):
        patch = lax.axis_index("lat") * lon_count + lax.axis_index("lon")
        return receivers - patch * nodes

    def cell_places(ids):
        lat_index = lax.axis_index("lat")
        total_lon = cols * lon_count
        row, col = divide(ids, total_lon)
        row = row - lat_index * rows
        col = divide(col - lax.axis_index("lon") * cols + RIM, total_lon)[1] - RIM
        in_rows = (row >= 0) & (row < rows)
        in_cols = (col >= 0) & (col < cols)
        own = jnp.where(in_rows & in_cols, row * cols + col, -1)
        slot = jnp.where(col < 0, col + 2 * RIM, col - cols)
        rim_row = jnp.where(row < 0, row + RIM, row - rows)
        rim = jnp.where(in_cols, rim_row * cols + col, RIM * cols + rim_row * 2 * RIM + slot)
        odd = lat_index % 2
        rim = rim + side_size + jnp.where(row < 0, 1 - odd, odd) * lat_rows
        beyond = jnp.where(in_rows, jnp.where(in_cols, -1, row * 2 * RIM + slot), rim)
        return own, beyond

    def sender_nodes(ids):
        source, node = divide(ids, nodes)
        source_lat, source_lon = divide(source, lon_count)
        here = source_lat == lax.axis_index("lat")
        offset = divide(source_lon - lax.axis_index("lon") + lon_count, lon_count)[1]
        tables = [0, 1] if two_lon else [0, lon_count - 1, 1]
        return [jnp.where(here & (offset == place), node, -1) for place in tables]

    def ids_in(rim_ref):
        rim_ids = [rim_ref[lat_size + row : lat_size + row + 1, :] for row in range(id_rows)]
        return jnp.concatenate(rim_ids, axis=1).astype(jnp.int32)

    step_rows = 2 if rows % 2 == 0 else 1

    def terms_body(cell_ref, weight_ref, term_ref, side_ref):
        term_ref[...] = dot_split(cell_ref[...], weight_ref[...])
        for row in range(step_rows):
            start = row * 2 * RIM
            side_ref[start : start + RIM, :] = term_ref[row * cols : row * cols + RIM, :]
            side_ref[start + RIM : start + 2 * RIM, :] = term_ref[
                (row + 1) * cols - RIM : (row + 1) * cols, :
            ]

    terms, sides = pl.pallas_call(
        terms_body,
        grid=(rows // step_rows,),
        in_specs=[
            pl.BlockSpec((step_rows * cols, width), lambda i: (i, 0)),
            pl.BlockSpec((None, width, units), lambda i: (0, 0, 0)),
        ],
        out_shape=(shape(rows * cols, units), shape(side_size, units)),
        out_specs=(
            pl.BlockSpec((step_rows * cols, units), lambda i: (i, 0)),
            pl.BlockSpec((step_rows * 2 * RIM, units), lambda i: (i, 0)),
        ),
        name="grid_terms",
        cost_estimate=pl.CostEstimate(
            flops=6 * rows * cols * width * units, bytes_accessed=1 << 21, transcendentals=0
        ),
    )(cells, sender_weight)
    if two_lon:
        side_got = shift(sides, "lon", 1)
    else:
        parts = sides.reshape(rows, 2, RIM, units)
        from_high = shift(parts[:, 0], "lon", -1)
        from_low = shift(parts[:, 1], "lon", 1)
        side_got = jnp.stack([from_high, from_low], axis=1).reshape(side_size, units)

    out_pieces = gather_hid(lax.optimization_barrier((out_weight, sides))[0])

    def grid_received_body(mesh_ref, weight_ref, feat_ref, edge_ref, bias_ref, recv_ref, pre_ref):
        received = dot_split(mesh_ref[...], weight_ref[0])
        pre_ref[...] = (
            pick(local(recv_ref[...]), received)
            + edge_terms(feat_ref[...], edge_ref[0])
            + bias_ref[0:1, :]
        )

    grid_pre = call(
        "grid_received",
        grid_received_body,
        shape(grid_edges, units),
        8 * grid_edges * rows * cols * units,
        (mesh_own, receiver_weight, grid_edge_feats.reshape(-1, grid_edges), edge_weight, first_bias, grid_to),
    )

    def rim_body(term_ref, side_ref, id_ref, a_ref, b_ref):
        odd = lax.axis_index("lat") % 2
        for ref, up in ((a_ref, 1 - odd), (b_ref, odd)):
            start = up * (rows - RIM)
            ref[: RIM * cols, :] = term_ref[pl.ds(pl.multiple_of(start * cols, 8), RIM * cols), :]
            ref[RIM * cols : lat_size, :] = jnp.where(
                up == 1,
                side_ref[(rows - RIM) * 2 * RIM : rows * 2 * RIM, :],
                side_ref[: RIM * 2 * RIM, :],
            )
            ids = id_ref[...].astype(F32)
            for row in range(id_rows):
                ref[lat_size + row : lat_size + row + 1, :] = ids[:, row * LANES : (row + 1) * LANES]
            ref[lat_size + id_rows :, :] = jnp.zeros((lat_rows - lat_size - id_rows, units), F32)

    rim_block = shape(lat_rows, units)
    rim_a, rim_b = call(
        "grid_rim", rim_body, (rim_block, rim_block), 1 << 20, (terms, side_got, mesh_ids)
    )
    rim_a = swap_lat(rim_a, 0)
    rim_b = swap_lat(rim_b, 1)

    def grid_own_body(pre_ref, term_ref, send_ref, out_ref):
        out_ref[...] = pre_ref[...] + pick(cell_places(send_ref[...])[0], term_ref[...])

    grid_pre = call(
        "grid_own",
        grid_own_body,
        shape(grid_edges, units),
        8 * grid_edges * rows * cols * units,
        (grid_pre, terms, grid_ids),
    )

    def grid_hidden_body(pre_ref, side_ref, a_ref, b_ref, send_ref, hidden_ref):
        pad = -(side_size + 2 * lat_rows) % LANES
        table = jnp.concatenate(
            [side_ref[...], a_ref[...], b_ref[...], jnp.zeros((pad, units), F32)], axis=0
        )
        total = pre_ref[...] + pick(cell_places(send_ref[...])[1], table)
        hidden_ref[...] = total / (1.0 + jnp.exp(-total))

    grid_hidden = call(
        "grid_hidden",
        grid_hidden_body,
        shape(grid_edges, units),
        4 * grid_edges * rows * cols * units,
        (grid_pre, side_got, rim_a, rim_b, grid_ids),
    )
    grid_pieces = gather_hid(grid_hidden)

    def weight_body(*refs):
        for section in range(2):
            whole = jnp.concatenate([ref[section] for ref in refs[:hid_count]], axis=0)
            high, low = split(whole)
            out_ref = refs[hid_count + section]
            out_ref[:width, :] = high
            out_ref[width : 2 * width, :] = low
            out_ref[2 * width :, :] = high

    weight_block = shape(3 * width, width, dtype=BF16)
    whole_weights = call(
        "weights",
        weight_body,
        (weight_block, weight_block),
        1 << 30,
        lax.optimization_barrier((*out_pieces, grid_hidden))[:hid_count],
    )

    def grid_message_body(*refs):
        hidden_refs = refs[:hid_count]
        weight_ref, bias_ref, gain_ref, shift_ref, recv_ref, mesh_ref, send_ref = refs[hid_count:-3]
        mid_ref, term_ref, normed_ref = refs[-3:]

        def store(start, step, normed):
            high, low = split(normed)
            normed_ref[start : start + step, :width] = high
            normed_ref[start : start + step, width:] = low

        normed_chunks(
            hidden_refs, weight_ref, bias_ref[0:1, :], gain_ref[0:1, :], shift_ref[0:1, :], store
        )
        middle = mesh_ref[...] + aggregate(local(recv_ref[...]), nodes, normed_ref)
        mid_ref[...] = middle
        term_ref[...] = dot_split(middle, send_ref[1])

    mesh_mid, mesh_terms = call(
        "grid_message",
        grid_message_body,
        (shape(nodes, width), shape(nodes, units)),
        12 * grid_edges * width * width,
        (*grid_pieces, whole_weights[0], out_bias, norm_gain, norm_shift, grid_to, mesh_own, sender_weight),
        (pltpu.VMEM((grid_edges, 2 * width), BF16),),
    )

    others = [shift(mesh_terms, "lon", 1)]
    if not two_lon:
        others.append(shift(mesh_terms, "lon", -1))
    table_count = len(others)

    def mesh_first_body(
        term_ref, mid_ref, weight_ref, feat_ref, edge_ref, bias_ref, recv_ref, id_ref, rim_a_ref, rim_b_ref,
        pre_ref, a_ref, b_ref,
    ):
        table = term_ref[...]
        a_ref[...] = pick(sender_nodes(ids_in(rim_a_ref))[0], table)
        b_ref[...] = pick(sender_nodes(ids_in(rim_b_ref))[0], table)
        received = dot_split(mid_ref[...], weight_ref[1])
        pre_ref[...] = (
            pick(sender_nodes(id_ref[...])[0], table)
            + pick(local(recv_ref[...]), received)
            + edge_terms(feat_ref[...], edge_ref[1])
            + bias_ref[1:2, :]
        )

    edge_block = shape(mesh_edges, units)
    mesh_pre, send_a, send_b = call(
        "mesh_first",
        mesh_first_body,
        (edge_block, edge_block, edge_block),
        16 * mesh_edges * nodes * units,
        (
            mesh_terms, mesh_mid, receiver_weight, mesh_edge_feats.reshape(-1, mesh_edges), edge_weight,
            first_bias, mesh_to, mesh_ids, rim_a, rim_b,
        ),
    )

    def add_others(first_ref, ids, table_refs):
        total = first_ref[...]
        for index_row, table_ref in zip(sender_nodes(ids)[1:], table_refs):
            total = total + pick(index_row, table_ref[...])
        return total

    def mesh_sent_body(*refs):
        tables = refs[:table_count]
        first_a, first_b, rim_a_ref, rim_b_ref, a_ref, b_ref = refs[table_count:]
        a_ref[...] = add_others(first_a, ids_in(rim_a_ref), tables)
        b_ref[...] = add_others(first_b, ids_in(rim_b_ref), tables)

    send_a, send_b = call(
        "mesh_sent",
        mesh_sent_body,
        (edge_block, edge_block),
        8 * mesh_edges * nodes * units,
        (*others, send_a, send_b, rim_a, rim_b),
    )
    got_a = swap_lat(send_a, 0)
    got_b = swap_lat(send_b, 1)

    def mesh_own_body(*refs):
        first_ref, id_ref, out_ref = refs[table_count:]
        out_ref[...] = add_others(first_ref, id_ref[...], refs[:table_count])

    mesh_pre = call(
        "mesh_own",
        mesh_own_body,
        edge_block,
        4 * mesh_edges * nodes * units,
        (*others, mesh_pre, mesh_ids),
    )
    total = mesh_pre + got_a + got_b
    mesh_pieces = gather_hid(total / (1.0 + jnp.exp(-total)))
    share = width // hid_count

    def mesh_message_body(*refs):
        hidden_refs = refs[:hid_count]
        weight_ref, bias_ref, gain_ref, shift_ref, recv_ref, mid_ref, out_ref, normed_ref = refs[hid_count:]
        place = lax.axis_index("hid")

        def own_part(value):
            part = value[:, :share]
            for step in range(1, hid_count):
                part = jnp.where(place == step, value[:, step * share : (step + 1) * share], part)
            return part

        def store(start, step, normed):
            high, low = split(own_part(normed))
            normed_ref[start : start + step, :share] = high
            normed_ref[start : start + step, share:] = low

        normed_chunks(
            hidden_refs, weight_ref, bias_ref[1:2, :], gain_ref[1:2, :], shift_ref[1:2, :], store
        )
        out_ref[...] = own_part(mid_ref[...]) + aggregate(local(recv_ref[...]), nodes, normed_ref)

    mesh_out = call(
        "mesh_message",
        mesh_message_body,
        shape(nodes, share),
        8 * mesh_edges * width * width,
        (*mesh_pieces, whole_weights[1], out_bias, norm_gain, norm_shift, mesh_to, mesh_mid),
        (pltpu.VMEM((mesh_edges, 2 * share), BF16),),
    )
    return mesh_out.reshape(1, 1, nodes, share)


def solution(mesh):
    return jax.shard_map(
        per_device,
        mesh=mesh,
        in_specs=(
            P("lat", "lon", None),
            P("lat", "lon", None, None),
            P("lat", "lon", None, None),
            P("lat", "lon", None),
            P("lat", "lon", None),
            P("lat", "lon", None, None),
            P("lat", "lon", None),
            P("lat", "lon", None),
            P(None, None, "hid"),
            P(None, None, "hid"),
            P(None, None, "hid"),
            P(None, "hid"),
            P(None, "hid", None),
            P(),
            P(),
            P(),
        ),
        out_specs=P("lat", "lon", None, "hid"),
        check_vma=False,
    )
```

time: 97.6 us -> 88.8 us (0.910); the launches traced: 95.9 us -> 88.3 us
  local copies, waits for them, and re-layouts: 13.2 us -> 5.1 us
  Pallas kernels: 31.8 us -> 39.8 us
  other arithmetic: 6.88 us -> 1.03 us
  waiting for transfers between devices: 21.1 us -> 18.7 us
    pallas_call x9 -> x11, Pallas kernels: 31.8 us -> 39.8 us  [the longest x10 35.5 us: call(): pl.pallas_call(body, out_shape=outs, in_specs=[VMEM] * len(args), out_spe...]
    squeeze x7 -> x0, local copies, waits for them, and re-layouts: 6.63 us -> none  [the longest x4 3.35 us: per_device(): piece[section]]
    select_n x7 -> x0, other arithmetic: 4.26 us -> none  [the longest x5 2.99 us: sender_nodes(): return [jnp.where(here & (offset == place), node, -1) for place in tables]]
    ppermute x9, starting transfers between devices: 10.7 us -> 14.8 us  [gather_hid(): lax.ppermute(source, 'hid', [(i, i ^ hop) for i in range(count)])]
    ppermute x6, starting transfers between devices: 12 us -> 8.88 us  [the longest x4 6.4 us: swap_lat(): lax.ppermute(value, 'lat', pairs + [(high, low) for low, high in pairs])]
    slice x5 -> x0, local copies, waits for them, and re-layouts: 2.74 us -> none  [the longest x1 0.99 us: rim_sent(): terms[first * cols:(first + RIM) * cols]]
    ppermute x9, waiting for transfers between devices: 13.4 us -> 10.9 us  [gather_hid(): lax.ppermute(source, 'hid', [(i, i ^ hop) for i in range(count)])]
    convert_element_type x3 -> x0, other arithmetic: 1.37 us -> none  [the longest x2 1.37 us: ids_of(): rim[lat_size:lat_size + id_rows].reshape(1, -1)[:, :mesh_edges]]
  transfers between devices with their start and end apart: 15 -> 15, of which waited for: 6 -> 7; matrix products, arithmetic and copies ran while one was open for 17% -> 0% of each run, Pallas kernels for 17% -> 24%
where the time goes in v2:
time: 88.8 us; the launch traced here: 88.3 us
  Pallas kernels  39.8 us (45%)
  starting transfers between devices  23.6 us (27%)
  waiting for transfers between devices  18.7 us (21%)
  local copies, waits for them, and re-layouts  5.1 us (6%)
  other arithmetic  1.03 us (1%)
    pallas_call x10, Pallas kernels, call(): pl.pallas_call(body, out_shape=outs, in_specs=[VMEM] * len(args), out_spe...  35.5 us
    ppermute x9, starting transfers between devices, gather_hid(): lax.ppermute(source, 'hid', [(i, i ^ hop) for i in range(count)])  14.8 us
    ppermute x9, waiting for transfers between devices, gather_hid(): lax.ppermute(source, 'hid', [(i, i ^ hop) for i in range(count)])  10.9 us
    ppermute x4, starting transfers between devices, swap_lat(): lax.ppermute(value, 'lat', pairs + [(high, low) for low, high in pairs])  6.4 us
    unnamed x28, local copies, waits for them, and re-layouts  5.1 us
    ppermute x4, waiting for transfers between devices, swap_lat(): lax.ppermute(value, 'lat', pairs + [(high, low) for low, high in pairs])  5.02 us
    pallas_call x1, Pallas kernels, per_device(): pl.pallas_call(terms_body, grid=(rows // step_rows,), in_specs=[pl.BlockS...  4.26 us
    ppermute x2, waiting for transfers between devices, shift(): lax.ppermute(value, axis, [(i, (i + step) % count) for i in range(count)])  2.72 us
  transfers between devices with their start and end apart: 15, of which 7 were waited for; matrix products, arithmetic and copies ran while one was open for 0% of the time, Pallas kernels for 24%

profile of v2, /device:TPU:9, one launch (start us, length us, event | category | flops | bytes accessed | tf_op | source)
XLA Modules:
  0.0 88.3 jit_solution(591315695462202453)
XLA Ops:
  0.0 4.3 %grid_terms.1 = (f32[1024,128]{1,0:T(8,128)}, f32[32,128]{1,0:T(8,128)}) custom-call(f32[1024,512]{1,0:T(8,128)} %bitcast.9, f32[2,512,128]{2,1,0:T(8,128)} %refs_10_.1), custom_call_target="tpu_custom_call" | custom-call | flops 402653184 | bytes 2097152 | tf_op jit(solution)/shard_map/grid_terms/pallas_call | solution.py:218
  4.3 1.2 %collective-permute-start = (f32[32,128]{1,0:T(8,128)}, f32[32,128]{1,0:T(8,128)S(1)}, u32[]{:S(2)}, u32[]{:S(2)}) collective-permute-start(f32[32,128]{1,0:T(8,128)} %get-tuple-element.24), channel_id=1, source_target_pairs={{0,4},{4,0},{1,5},{5,1},{2,6},{6,2},{3,7},{7,3},{8,12},{12,8},{9,1... | collective-permute-start | bytes 49160 | tf_op jit(solution)/shard_map/ppermute | solution.py:94
  5.5 1.2 %collective-permute-start.7 = (f32[2,128,512]{2,1,0:T(8,128)S(1)}, f32[2,128,512]{2,1,0:T(8,128)S(1)}, u32[]{:S(2)}, u32[]{:S(2)}) collective-permute-start(f32[2,128,512]{2,1,0:T(8,128)S(1)} %copy-done.5), channel_id=1, source_target_pairs={{0,2},{1,3},{2,0},{3,1},{4,6},{5,7},{6,4},{7,5},{8,10},{9,11},{10,... | collective-permute-start | bytes 1572872 | tf_op jit(solution)/shard_map/ppermute | solution.py:108
  6.7 0.3 collective-permute-done.side_ref
  7.1 0.6 copy-done.4
  7.7 1.8 %grid_rim.1 = (f32[272,128]{1,0:T(8,128)}, f32[272,128]{1,0:T(8,128)}) custom-call(f32[1024,128]{1,0:T(8,128)} %get-tuple-element.23.term_ref, f32[32,128]{1,0:T(8,128)} %copy-done.4, s32[1,512]{1,0:T(1,128)} %bitcast.10), custom_call_target="tpu_custom_call" | custom-call | flops 1048576 | bytes 1048576 | tf_op jit(solution)/shard_map/grid_rim/pallas_call | solution.py:77
  9.5 0.0 collective-permute-start.1
  9.5 4.5 %collective-permute-start.2 = (f32[272,128]{1,0:T(8,128)}, f32[272,128]{1,0:T(8,128)S(1)}, u32[]{:S(2)}, u32[]{:S(2)}) collective-permute-start(f32[272,128]{1,0:T(8,128)} %get-tuple-element.26), channel_id=1, source_target_pairs={{8,16},{16,8},{9,17},{17,9},{10,18},{18,10},{11,19},{19,11},{12,20... | collective-permute-start | bytes 417800 | tf_op jit(solution)/shard_map/ppermute | solution.py:100
  14.0 4.4 %grid_received.1.pre_ref = f32[1024,128]{1,0:T(8,128)} custom-call(f32[512,512]{1,0:T(8,128)} %bitcast.16, f32[2,512,128]{2,1,0:T(8,128)} %weight_ref.5, f32[4,1024]{1,0:T(4,128)} %bitcast.18, f32[2,4,128]{2,1,0:T(4,128)} %edge_ref.3, f32[2,128]{1,0:T(2,128)} %bias_ref.3, s32[1,1024]{1,0:T(1,128)} %bitcast.21), custom_call_target="tpu_custom_call" | custom-call | flops 1073741824 | bytes 1048576 | tf_op jit(solution)/shard_map/grid_received/pallas_call | solution.py:77
  18.4 2.8 %grid_own.1.pre_ref = f32[1024,128]{1,0:T(8,128)} custom-call(f32[1024,128]{1,0:T(8,128)} %grid_received.1.pre_ref, f32[1024,128]{1,0:T(8,128)} %get-tuple-element.23.term_ref, s32[1,1024]{1,0:T(1,128)} %bitcast.19), custom_call_target="tpu_custom_call" | custom-call | flops 1073741824 | bytes 1048576 | tf_op jit(solution)/shard_map/grid_own/pallas_call | solution.py:77
  21.1 0.0 collective-permute-done.1.a_ref.rim_a_ref.refs_3_
  21.1 0.0 collective-permute-done.2.b_ref.rim_b_ref.refs_4_
  21.1 0.7 copy-done.1
  21.8 0.6 copy-done.2
  22.4 2.6 %grid_hidden.1.refs_0_ = f32[1024,128]{1,0:T(8,128)} custom-call(f32[1024,128]{1,0:T(8,128)} %grid_own.1.pre_ref, f32[32,128]{1,0:T(8,128)} %copy-done.4, f32[272,128]{1,0:T(8,128)} %copy-done.1, f32[272,128]{1,0:T(8,128)} %copy-done.2, s32[1,1024]{1,0:T(1,128)} %bitcast.20), custom_call_target="tpu_custom_call" | custom-call | flops 536870912 | bytes 1048576 | tf_op jit(solution)/shard_map/grid_hidden/pallas_call | solution.py:77
  25.1 1.2 %collective-permute-start.4 = (f32[1024,128]{1,0:T(8,128)}, f32[1024,128]{1,0:T(8,128)S(1)}, u32[]{:S(2)}, u32[]{:S(2)}) collective-permute-start(f32[1024,128]{1,0:T(8,128)} %grid_hidden.1.refs_0_), channel_id=1, source_target_pairs={{0,2},{1,3},{2,0},{3,1},{4,6},{5,7},{6,4},{7,5},{8,10},{9,11},{10,... | collective-permute-start | bytes 1572872 | tf_op jit(solution)/shard_map/ppermute | solution.py:108
  26.3 2.7 %collective-permute-start.6 = (f32[2,128,512]{2,1,0:T(8,128)S(1)}, f32[2,128,512]{2,1,0:T(8,128)S(1)}, u32[]{:S(2)}, u32[]{:S(2)}) collective-permute-start(f32[2,128,512]{2,1,0:T(8,128)S(1)} %copy-done.5), channel_id=1, source_target_pairs={{0,1},{1,0},{2,3},{3,2},{4,5},{5,4},{6,7},{7,6},{8,9},{9,8},{10,11... | collective-permute-start | bytes 1572872 | tf_op jit(solution)/shard_map/ppermute | solution.py:108
  29.0 0.0 collective-permute-done.7.refs_2_
  29.0 0.1 collective-permute-start.8
  29.0 0.4 collective-permute-start.3
  29.5 6.9 %collective-permute-done.4.refs_2_ = f32[1024,128]{1,0:T(8,128)S(1)} collective-permute-done((f32[1024,128]{1,0:T(8,128)}, f32[1024,128]{1,0:T(8,128)S(1)}, u32[]{:S(2)}, u32[]{:S(2)}) %collective-permute-start.4) | collective-permute-done | bytes 524320 | tf_op jit(solution)/shard_map/ppermute | solution.py:108
  36.4 3.2 %collective-permute-start.5 = (f32[1024,128]{1,0:T(8,128)S(1)}, f32[1024,128]{1,0:T(8,128)S(1)}, u32[]{:S(2)}, u32[]{:S(2)}) collective-permute-start(f32[1024,128]{1,0:T(8,128)S(1)} %collective-permute-done.4.refs_2_), channel_id=1, source_target_pairs={{0,1},{1,0},{2,3},{3,2},{4,5},{5,4},{6,7},{7,6},{8,9},{9,8},{10,11... | collective-permute-start | bytes 1572872 | tf_op jit(solution)/shard_map/ppermute | solution.py:108
  39.6 0.0 collective-permute-done.6.refs_1_
  39.6 0.0 collective-permute-done.8.refs_3_
  39.7 0.8 copy-done.9
  40.4 3.3 %weights.1 = (bf16[1536,512]{1,0:T(8,128)(2,1)}, bf16[1536,512]{1,0:T(8,128)(2,1)}) custom-call(f32[2,128,512]{2,1,0:T(8,128)} %refs_0_, f32[2,128,512]{2,1,0:T(8,128)} %copy-done.9, f32[2,128,512]{2,1,0:T(8,128)} %copy-done.6, f32[2,128,512]{2,1,0:T(8,128)} %collective-permute-done.8.refs_3_), custom_call_target="tpu_custom_call" | custom-call | flops 1073741824 | bytes 1048576 | tf_op jit(solution)/shard_map/weights/pallas_call | solution.py:77
  43.8 0.0 collective-permute-done.3.refs_1_
  43.8 0.0 collective-permute-done.5.refs_3_
  43.8 0.8 copy-done.8
  44.6 0.2 copy-done.10
  44.8 7.2 %grid_message.1 = (f32[512,512]{1,0:T(8,128)}, f32[512,128]{1,0:T(8,128)}) custom-call(f32[1024,128]{1,0:T(8,128)} %grid_hidden.1.refs_0_, f32[1024,128]{1,0:T(8,128)} %copy-done.8, f32[1024,128]{1,0:T(8,128)} %copy-done.7, f32[1024,128]{1,0:T(8,128)} %copy-done.10, bf16[1536,512]{1,0:T(8,128)(2,1)} %get-tuple-element.32.refs_4_, f32[2,512]{1,0:T(2,128)} %refs_5_.3, ...), custom_call_target="tpu_custom_call" | custom-call | flops 3221225472 | bytes 1048576 | tf_op jit(solution)/shard_map/grid_message/pallas_call | solution.py:77
  52.0 1.2 %collective-permute-start.9 = (f32[512,128]{1,0:T(8,128)}, f32[512,128]{1,0:T(8,128)S(1)}, u32[]{:S(2)}, u32[]{:S(2)}) collective-permute-start(f32[512,128]{1,0:T(8,128)} %get-tuple-element.33.term_ref), channel_id=1, source_target_pairs={{0,4},{4,0},{1,5},{5,1},{2,6},{6,2},{3,7},{7,3},{8,12},{12,8},{9,1... | collective-permute-start | bytes 786440 | tf_op jit(solution)/shard_map/ppermute | solution.py:94
  53.2 4.4 %mesh_first.1 = (f32[512,128]{1,0:T(8,128)}, f32[512,128]{1,0:T(8,128)}, f32[512,128]{1,0:T(8,128)}) custom-call(f32[512,128]{1,0:T(8,128)} %get-tuple-element.33.term_ref, f32[512,512]{1,0:T(8,128)} %get-tuple-element.34.mid_ref.refs_9_, f32[2,512,128]{2,1,0:T(8,128)} %weight_ref.5, f32[4,512]{1,0:T(4,128)} %bitcast.13, f32[2,4,128]{2,1,0:T(4,128)} %edge_ref.3, ...), custom_call_target="tpu_custom_call" | custom-call | flops 536870912 | bytes 1048576 | tf_op jit(solution)/shard_map/mesh_first/pallas_call | solution.py:77
  57.7 2.4 %collective-permute-done.9.refs_0_ = f32[512,128]{1,0:T(8,128)S(1)} collective-permute-done((f32[512,128]{1,0:T(8,128)}, f32[512,128]{1,0:T(8,128)S(1)}, u32[]{:S(2)}, u32[]{:S(2)}) %collective-permute-start.9) | collective-permute-done | bytes 262176 | tf_op jit(solution)/shard_map/ppermute | solution.py:94
  60.0 0.7 copy-done
  60.7 2.6 %mesh_sent.1 = (f32[512,128]{1,0:T(8,128)}, f32[512,128]{1,0:T(8,128)}) custom-call(f32[512,128]{1,0:T(8,128)} %copy-done, f32[512,128]{1,0:T(8,128)} %get-tuple-element.36.refs_1_, f32[512,128]{1,0:T(8,128)} %get-tuple-element.37.refs_2_, f32[272,128]{1,0:T(8,128)} %copy-done.1, f32[272,128]{1,0:T(8,128)} %copy-done.2), custom_call_target="tpu_custom_call" | custom-call | flops 268435456 | bytes 1048576 | tf_op jit(solution)/shard_map/mesh_sent/pallas_call | solution.py:77
  63.3 1.9 %collective-permute-start.11 = (f32[512,128]{1,0:T(8,128)}, f32[512,128]{1,0:T(8,128)S(1)}, u32[]{:S(2)}, u32[]{:S(2)}) collective-permute-start(f32[512,128]{1,0:T(8,128)} %get-tuple-element.39), channel_id=1, source_target_pairs={{8,16},{16,8},{9,17},{17,9},{10,18},{18,10},{11,19},{19,11},{12,20... | collective-permute-start | bytes 786440 | tf_op jit(solution)/shard_map/ppermute | solution.py:100
  65.2 2.1 %mesh_own.1 = f32[512,128]{1,0:T(8,128)} custom-call(f32[512,128]{1,0:T(8,128)} %copy-done, f32[512,128]{1,0:T(8,128)} %get-tuple-element.35.refs_1_, s32[1,512]{1,0:T(1,128)} %bitcast.12), custom_call_target="tpu_custom_call" | custom-call | flops 134217728 | bytes 1048576 | tf_op jit(solution)/shard_map/mesh_own/pallas_call | solution.py:77
  67.3 3.1 %collective-permute-done.10 = f32[512,128]{1,0:T(8,128)S(1)} collective-permute-done((f32[512,128]{1,0:T(8,128)}, f32[512,128]{1,0:T(8,128)S(1)}, u32[]{:S(2)}, u32[]{:S(2)}) %collective-permute-start.10) | collective-permute-done | bytes 262176 | tf_op jit(solution)/shard_map/ppermute | solution.py:100
  70.5 1.9 %collective-permute-done.11 = f32[512,128]{1,0:T(8,128)S(1)} collective-permute-done((f32[512,128]{1,0:T(8,128)}, f32[512,128]{1,0:T(8,128)S(1)}, u32[]{:S(2)}, u32[]{:S(2)}) %collective-permute-start.11) | collective-permute-done | bytes 262176 | tf_op jit(solution)/shard_map/ppermute | solution.py:100
  72.3 1.0 %add_divide_fusion.refs_0_ = f32[512,128]{1,0:T(8,128)S(1)} fusion(f32[512,128]{1,0:T(8,128)S(1)} %collective-permute-done.11, f32[512,128]{1,0:T(8,128)} %mesh_own.1, f32[512,128]{1,0:T(8,128)S(1)} %collective-permute-done.10), kind=kLoop, calls=%fused_computation | loop fusion | flops 327680 | bytes 1048576 | tf_op jit(solution)/shard_map/div | solution.py:421
  73.4 1.3 %collective-permute-start.13 = (f32[512,128]{1,0:T(8,128)S(1)}, f32[512,128]{1,0:T(8,128)S(1)}, u32[]{:S(2)}, u32[]{:S(2)}) collective-permute-start(f32[512,128]{1,0:T(8,128)S(1)} %add_divide_fusion.refs_0_), channel_id=1, source_target_pairs={{0,2},{1,3},{2,0},{3,1},{4,6},{5,7},{6,4},{7,5},{8,10},{9,11},{10,... | collective-permute-start | bytes 786440 | tf_op jit(solution)/shard_map/ppermute | solution.py:108
  74.7 2.0 %collective-permute-start.12 = (f32[512,128]{1,0:T(8,128)S(1)}, f32[512,128]{1,0:T(8,128)S(1)}, u32[]{:S(2)}, u32[]{:S(2)}) collective-permute-start(f32[512,128]{1,0:T(8,128)S(1)} %add_divide_fusion.refs_0_), channel_id=1, source_target_pairs={{0,1},{1,0},{2,3},{3,2},{4,5},{5,4},{6,7},{7,6},{8,9},{9,8},{10,11... | collective-permute-start | bytes 786440 | tf_op jit(solution)/shard_map/ppermute | solution.py:108
  76.7 2.9 %collective-permute-done.13.refs_2_ = f32[512,128]{1,0:T(8,128)S(1)} collective-permute-done((f32[512,128]{1,0:T(8,128)S(1)}, f32[512,128]{1,0:T(8,128)S(1)}, u32[]{:S(2)}, u32[]{:S(2)}) %collective-permute-start.13) | collective-permute-done | bytes 262176 | tf_op jit(solution)/shard_map/ppermute | solution.py:108
  79.6 2.6 %collective-permute-start.14 = (f32[512,128]{1,0:T(8,128)S(1)}, f32[512,128]{1,0:T(8,128)S(1)}, u32[]{:S(2)}, u32[]{:S(2)}) collective-permute-start(f32[512,128]{1,0:T(8,128)S(1)} %collective-permute-done.13.refs_2_), channel_id=1, source_target_pairs={{0,1},{1,0},{2,3},{3,2},{4,5},{5,4},{6,7},{7,6},{8,9},{9,8},{10,11... | collective-permute-start | bytes 786440 | tf_op jit(solution)/shard_map/ppermute | solution.py:108
  82.2 1.2 %collective-permute-done.14.refs_3_ = f32[512,128]{1,0:T(8,128)S(1)} collective-permute-done((f32[512,128]{1,0:T(8,128)S(1)}, f32[512,128]{1,0:T(8,128)S(1)}, u32[]{:S(2)}, u32[]{:S(2)}) %collective-permute-start.14) | collective-permute-done | bytes 262176 | tf_op jit(solution)/shard_map/ppermute | solution.py:108
  83.4 0.7 copy-done.13
  84.1 4.3 %mesh_message.1 = f32[512,128]{1,0:T(8,128)} custom-call(f32[512,128]{1,0:T(8,128)} %copy-done.3, f32[512,128]{1,0:T(8,128)} %copy-done.12, f32[512,128]{1,0:T(8,128)} %copy-done.11, f32[512,128]{1,0:T(8,128)} %copy-done.13, bf16[1536,512]{1,0:T(8,128)(2,1)} %get-tuple-element.40.refs_4_, f32[2,512]{1,0:T(2,128)} %refs_5_.3, f32[2,512]{1,0:T(2,128)} %refs_6_.3, ...), custom_call_target="tpu_custom_call" | custom-call | flops 1073741824 | bytes 1048576 | tf_op jit(solution)/shard_map/mesh_message/pallas_call | solution.py:77
  (22 shorter events, 0.0 us)
Async XLA Ops:
  0.0 5.5 %copy-start.5 = (f32[2,128,512]{2,1,0:T(8,128)S(1)}, f32[2,128,512]{2,1,0:T(8,128)}, u32[]{:S(2)}) copy-start(f32[2,128,512]{2,1,0:T(8,128)} %refs_0_) | copy-start | bytes 1572868
  4.3 2.8 %collective-permute-start = (f32[32,128]{1,0:T(8,128)}, f32[32,128]{1,0:T(8,128)S(1)}, u32[]{:S(2)}, u32[]{:S(2)}) collective-permute-start(f32[32,128]{1,0:T(8,128)} %get-tuple-element.24), channel_id=1, source_target_pairs={{0,4},{4,0},{1,5},{5,1},{2,6},{6,2},{3,7},{7,3},{8,12},{12,8},{9,1... | collective-permute-start | bytes 49160 | tf_op jit(solution)/shard_map/ppermute | solution.py:94
  5.5 23.5 %collective-permute-start.7 = (f32[2,128,512]{2,1,0:T(8,128)S(1)}, f32[2,128,512]{2,1,0:T(8,128)S(1)}, u32[]{:S(2)}, u32[]{:S(2)}) collective-permute-start(f32[2,128,512]{2,1,0:T(8,128)S(1)} %copy-done.5), channel_id=1, source_target_pairs={{0,2},{1,3},{2,0},{3,1},{4,6},{5,7},{6,4},{7,5},{8,10},{9,11},{10,... | collective-permute-start | bytes 1572872 | tf_op jit(solution)/shard_map/ppermute | solution.py:108
  7.1 0.6 copy-start.4
  9.5 11.7 %collective-permute-start.1 = (f32[272,128]{1,0:T(8,128)}, f32[272,128]{1,0:T(8,128)S(1)}, u32[]{:S(2)}, u32[]{:S(2)}) collective-permute-start(f32[272,128]{1,0:T(8,128)} %get-tuple-element.25), channel_id=1, source_target_pairs={{0,8},{16,24},{8,0},{24,16},{1,9},{17,25},{9,1},{25,17},{2,10},{18... | collective-permute-start | bytes 417800 | tf_op jit(solution)/shard_map/ppermute | solution.py:100
  9.5 11.7 %collective-permute-start.2 = (f32[272,128]{1,0:T(8,128)}, f32[272,128]{1,0:T(8,128)S(1)}, u32[]{:S(2)}, u32[]{:S(2)}) collective-permute-start(f32[272,128]{1,0:T(8,128)} %get-tuple-element.26), channel_id=1, source_target_pairs={{8,16},{16,8},{9,17},{17,9},{10,18},{18,10},{11,19},{19,11},{12,20... | collective-permute-start | bytes 417800 | tf_op jit(solution)/shard_map/ppermute | solution.py:100
  21.1 0.7 copy-start.1
  21.8 0.7 copy-start.2
  25.1 11.3 %collective-permute-start.4 = (f32[1024,128]{1,0:T(8,128)}, f32[1024,128]{1,0:T(8,128)S(1)}, u32[]{:S(2)}, u32[]{:S(2)}) collective-permute-start(f32[1024,128]{1,0:T(8,128)} %grid_hidden.1.refs_0_), channel_id=1, source_target_pairs={{0,2},{1,3},{2,0},{3,1},{4,6},{5,7},{6,4},{7,5},{8,10},{9,11},{10,... | collective-permute-start | bytes 1572872 | tf_op jit(solution)/shard_map/ppermute | solution.py:108
  26.3 13.3 %collective-permute-start.6 = (f32[2,128,512]{2,1,0:T(8,128)S(1)}, f32[2,128,512]{2,1,0:T(8,128)S(1)}, u32[]{:S(2)}, u32[]{:S(2)}) collective-permute-start(f32[2,128,512]{2,1,0:T(8,128)S(1)} %copy-done.5), channel_id=1, source_target_pairs={{0,1},{1,0},{2,3},{3,2},{4,5},{5,4},{6,7},{7,6},{8,9},{9,8},{10,11... | collective-permute-start | bytes 1572872 | tf_op jit(solution)/shard_map/ppermute | solution.py:108
  29.0 10.7 %copy-start.6 = (f32[2,128,512]{2,1,0:T(8,128)}, f32[2,128,512]{2,1,0:T(8,128)S(1)}, u32[]{:S(2)}) copy-start(f32[2,128,512]{2,1,0:T(8,128)S(1)} %collective-permute-done.7.refs_2_) | copy-start | bytes 1572868
  29.0 10.7 %collective-permute-start.8 = (f32[2,128,512]{2,1,0:T(8,128)S(1)}, f32[2,128,512]{2,1,0:T(8,128)}, u32[]{:S(2)}, u32[]{:S(2)}) collective-permute-start(f32[2,128,512]{2,1,0:T(8,128)S(1)} %collective-permute-done.7.refs_2_), channel_id=1, source_target_pairs={{0,1},{1,0},{2,3},{3,2},{4,5},{5,4},{6,7},{7,6},{8,9},{9,8},{10,11... | collective-permute-start | bytes 1572872 | tf_op jit(solution)/shard_map/ppermute | solution.py:108
  29.0 14.7 %collective-permute-start.3 = (f32[1024,128]{1,0:T(8,128)}, f32[1024,128]{1,0:T(8,128)S(1)}, u32[]{:S(2)}, u32[]{:S(2)}) collective-permute-start(f32[1024,128]{1,0:T(8,128)} %grid_hidden.1.refs_0_), channel_id=1, source_target_pairs={{0,1},{1,0},{2,3},{3,2},{4,5},{5,4},{6,7},{7,6},{8,9},{9,8},{10,11... | collective-permute-start | bytes 1572872 | tf_op jit(solution)/shard_map/ppermute | solution.py:108
  36.4 7.4 %copy-start.7 = (f32[1024,128]{1,0:T(8,128)}, f32[1024,128]{1,0:T(8,128)S(1)}, u32[]{:S(2)}) copy-start(f32[1024,128]{1,0:T(8,128)S(1)} %collective-permute-done.4.refs_2_) | copy-start | bytes 1572868
  36.4 7.4 %collective-permute-start.5 = (f32[1024,128]{1,0:T(8,128)S(1)}, f32[1024,128]{1,0:T(8,128)S(1)}, u32[]{:S(2)}, u32[]{:S(2)}) collective-permute-start(f32[1024,128]{1,0:T(8,128)S(1)} %collective-permute-done.4.refs_2_), channel_id=1, source_target_pairs={{0,1},{1,0},{2,3},{3,2},{4,5},{5,4},{6,7},{7,6},{8,9},{9,8},{10,11... | collective-permute-start | bytes 1572872 | tf_op jit(solution)/shard_map/ppermute | solution.py:108
  39.6 0.8 copy-start.9
  43.8 0.8 copy-start.8
  43.8 1.0 %copy-start.10 = (f32[1024,128]{1,0:T(8,128)}, f32[1024,128]{1,0:T(8,128)S(1)}, u32[]{:S(2)}) copy-start(f32[1024,128]{1,0:T(8,128)S(1)} %collective-permute-done.5.refs_3_) | copy-start | bytes 1572868
  52.0 8.0 %collective-permute-start.9 = (f32[512,128]{1,0:T(8,128)}, f32[512,128]{1,0:T(8,128)S(1)}, u32[]{:S(2)}, u32[]{:S(2)}) collective-permute-start(f32[512,128]{1,0:T(8,128)} %get-tuple-element.33.term_ref), channel_id=1, source_target_pairs={{0,4},{4,0},{1,5},{5,1},{2,6},{6,2},{3,7},{7,3},{8,12},{12,8},{9,1... | collective-permute-start | bytes 786440 | tf_op jit(solution)/shard_map/ppermute | solution.py:94
  60.0 0.7 copy-start
  63.3 7.2 %collective-permute-start.10 = (f32[512,128]{1,0:T(8,128)}, f32[512,128]{1,0:T(8,128)S(1)}, u32[]{:S(2)}, u32[]{:S(2)}) collective-permute-start(f32[512,128]{1,0:T(8,128)} %get-tuple-element.38), channel_id=1, source_target_pairs={{0,8},{16,24},{8,0},{24,16},{1,9},{17,25},{9,1},{25,17},{2,10},{18... | collective-permute-start | bytes 786440 | tf_op jit(solution)/shard_map/ppermute | solution.py:100
  63.3 9.1 %collective-permute-start.11 = (f32[512,128]{1,0:T(8,128)}, f32[512,128]{1,0:T(8,128)S(1)}, u32[]{:S(2)}, u32[]{:S(2)}) collective-permute-start(f32[512,128]{1,0:T(8,128)} %get-tuple-element.39), channel_id=1, source_target_pairs={{8,16},{16,8},{9,17},{17,9},{10,18},{18,10},{11,19},{19,11},{12,20... | collective-permute-start | bytes 786440 | tf_op jit(solution)/shard_map/ppermute | solution.py:100
  73.4 10.0 %copy-start.3 = (f32[512,128]{1,0:T(8,128)}, f32[512,128]{1,0:T(8,128)S(1)}, u32[]{:S(2)}) copy-start(f32[512,128]{1,0:T(8,128)S(1)} %add_divide_fusion.refs_0_) | copy-start | bytes 786436
  73.4 6.2 %collective-permute-start.13 = (f32[512,128]{1,0:T(8,128)S(1)}, f32[512,128]{1,0:T(8,128)S(1)}, u32[]{:S(2)}, u32[]{:S(2)}) collective-permute-start(f32[512,128]{1,0:T(8,128)S(1)} %add_divide_fusion.refs_0_), channel_id=1, source_target_pairs={{0,2},{1,3},{2,0},{3,1},{4,6},{5,7},{6,4},{7,5},{8,10},{9,11},{10,... | collective-permute-start | bytes 786440 | tf_op jit(solution)/shard_map/ppermute | solution.py:108
  74.7 7.5 %collective-permute-start.12 = (f32[512,128]{1,0:T(8,128)S(1)}, f32[512,128]{1,0:T(8,128)S(1)}, u32[]{:S(2)}, u32[]{:S(2)}) collective-permute-start(f32[512,128]{1,0:T(8,128)S(1)} %add_divide_fusion.refs_0_), channel_id=1, source_target_pairs={{0,1},{1,0},{2,3},{3,2},{4,5},{5,4},{6,7},{7,6},{8,9},{9,8},{10,11... | collective-permute-start | bytes 786440 | tf_op jit(solution)/shard_map/ppermute | solution.py:108
  79.6 3.8 %copy-start.11 = (f32[512,128]{1,0:T(8,128)}, f32[512,128]{1,0:T(8,128)S(1)}, u32[]{:S(2)}) copy-start(f32[512,128]{1,0:T(8,128)S(1)} %collective-permute-done.13.refs_2_) | copy-start | bytes 786436
  79.6 3.8 %collective-permute-start.14 = (f32[512,128]{1,0:T(8,128)S(1)}, f32[512,128]{1,0:T(8,128)S(1)}, u32[]{:S(2)}, u32[]{:S(2)}) collective-permute-start(f32[512,128]{1,0:T(8,128)S(1)} %collective-permute-done.13.refs_2_), channel_id=1, source_target_pairs={{0,1},{1,0},{2,3},{3,2},{4,5},{5,4},{6,7},{7,6},{8,9},{9,8},{10,11... | collective-permute-start | bytes 786440 | tf_op jit(solution)/shard_map/ppermute | solution.py:108
  82.2 1.2 %copy-start.12 = (f32[512,128]{1,0:T(8,128)}, f32[512,128]{1,0:T(8,128)S(1)}, u32[]{:S(2)}) copy-start(f32[512,128]{1,0:T(8,128)S(1)} %collective-permute-done.12.refs_1_) | copy-start | bytes 786436
  83.3 0.7 copy-start.13

commit v3 on v2

--- a/solution.py
+++ b/solution.py
@@ -8,6 +8,7 @@
 RIM = 2
 LANES = 128
 EDGE_CHUNK = 256
+KERNEL_VMEM = 24 << 20
 epsilon = 1e-05
 F32 = jnp.float32
 BF16 = jnp.bfloat16
@@ -81,6 +82,7 @@
         out_specs=jax.tree.map(lambda _: VMEM, outs),
         scratch_shapes=scratch,
         name=name,
+        compiler_params=pltpu.CompilerParams(vmem_limit_bytes=KERNEL_VMEM),
         cost_estimate=pl.CostEstimate(flops=flops, bytes_accessed=1 << 20, transcendentals=0),
     )(*args)
 
@@ -228,6 +230,7 @@
             pl.BlockSpec((step_rows * 2 * RIM, units), lambda i: (i, 0)),
         ),
         name="grid_terms",
+        compiler_params=pltpu.CompilerParams(vmem_limit_bytes=KERNEL_VMEM),
         cost_estimate=pl.CostEstimate(
             flops=6 * rows * cols * width * units, bytes_accessed=1 << 21, transcendentals=0
         ),

time: 88.8 us -> 66.9 us (0.75)
  Pallas kernels: 39.8 us -> 14.7 us
  waiting for transfers between devices: 18.7 us -> 22.6 us
  starting transfers between devices: 23.6 us -> 26.3 us
  local copies, waits for them, and re-layouts: 5.1 us -> 2.71 us
  other arithmetic: 1.03 us -> 0.08 us
    pallas_call x10, Pallas kernels: 35.5 us -> 13.2 us  [call(): pl.pallas_call(body, out_shape=outs, in_specs=[VMEM] * len(args), out_spe...]
    pallas_call x1, Pallas kernels: 4.26 us -> 1.49 us  [per_device(): pl.pallas_call(terms_body, grid=(rows // step_rows,), in_specs=[pl.BlockS...]
    ppermute x4, starting transfers between devices: 6.4 us -> 9.11 us  [swap_lat(): lax.ppermute(value, 'lat', pairs + [(high, low) for low, high in pairs])]
    ppermute x2, waiting for transfers between devices: 2.72 us -> 5.27 us  [shift(): lax.ppermute(value, axis, [(i, (i + step) % count) for i in range(count)])]
    unnamed x28 -> x34, local copies, waits for them, and re-layouts: 5.1 us -> 2.71 us
    ppermute x9, waiting for transfers between devices: 10.9 us -> 12.5 us  [gather_hid(): lax.ppermute(source, 'hid', [(i, i ^ hop) for i in range(count)])]
    div x1, other arithmetic: 1.03 us -> 0.08 us  [per_device(): mesh_pieces = gather_hid(total / (1.0 + jnp.exp(-total)))]
  transfers between devices with their start and end apart: 15 -> 15, of which waited for: 7 -> 8; matrix products, arithmetic and copies ran while one was open for 0% -> 0% of each run, Pallas kernels for 24% -> 10%
where the time goes in v3:
time: 66.9 us; the launch traced here: 66.7 us
  starting transfers between devices  26.3 us (39%)
  waiting for transfers between devices  22.6 us (34%)
  Pallas kernels  14.7 us (22%)
  local copies, waits for them, and re-layouts  2.71 us (4%)
    ppermute x9, starting transfers between devices, gather_hid(): lax.ppermute(source, 'hid', [(i, i ^ hop) for i in range(count)])  15.6 us
    pallas_call x10, Pallas kernels, call(): pl.pallas_call(body, out_shape=outs, in_specs=[VMEM] * len(args), out_spe...  13.2 us
    ppermute x9, waiting for transfers between devices, gather_hid(): lax.ppermute(source, 'hid', [(i, i ^ hop) for i in range(count)])  12.5 us
    ppermute x4, starting transfers between devices, swap_lat(): lax.ppermute(value, 'lat', pairs + [(high, low) for low, high in pairs])  9.11 us
    ppermute x2, waiting for transfers between devices, shift(): lax.ppermute(value, axis, [(i, (i + step) % count) for i in range(count)])  5.27 us
    ppermute x4, waiting for transfers between devices, swap_lat(): lax.ppermute(value, 'lat', pairs + [(high, low) for low, high in pairs])  4.79 us
    unnamed x34, local copies, waits for them, and re-layouts  2.71 us
    ppermute x2, starting transfers between devices, shift(): lax.ppermute(value, axis, [(i, (i + step) % count) for i in range(count)])  1.6 us
  transfers between devices with their start and end apart: 15, of which 8 were waited for; matrix products, arithmetic and copies ran while one was open for 0% of the time, Pallas kernels for 10%

profile of v3, /device:TPU:9, one launch (start us, length us, event | category | flops | bytes accessed | tf_op | source)
XLA Modules:
  0.0 66.7 jit_solution(17703655860287841314)
XLA Ops:
  0.0 1.6 %copy-done = f32[8,128,512]{2,1,0:T(8,128)S(1)} copy-done((f32[8,128,512]{2,1,0:T(8,128)S(1)}, f32[8,128,512]{2,1,0:T(8,128)}, u32[]{:S(2)}) %copy-start) | copy-done | bytes 2097176
  1.6 1.0 %copy-done.1 = f32[2,512,128]{2,1,0:T(8,128)S(1)} copy-done((f32[2,512,128]{2,1,0:T(8,128)S(1)}, f32[2,512,128]{2,1,0:T(8,128)}, u32[]{:S(2)}) %copy-start.1) | copy-done | bytes 524312
  2.7 1.5 %grid_terms.1 = (f32[1024,128]{1,0:T(8,128)S(1)}, f32[32,128]{1,0:T(8,128)S(1)}) custom-call(f32[1024,512]{1,0:T(8,128)S(1)} %bitcast.9, f32[2,512,128]{2,1,0:T(8,128)S(1)} %copy-done.1), custom_call_target="tpu_custom_call" | custom-call | flops 402653184 | bytes 2097152 | tf_op jit(solution)/shard_map/grid_terms/pallas_call | solution.py:220
  4.2 1.3 %collective-permute-start = (f32[32,128]{1,0:T(8,128)S(1)}, f32[32,128]{1,0:T(8,128)S(1)}, u32[]{:S(2)}, u32[]{:S(2)}) collective-permute-start(f32[32,128]{1,0:T(8,128)S(1)} %get-tuple-element.24), channel_id=1, source_target_pairs={{0,4},{4,0},{1,5},{5,1},{2,6},{6,2},{3,7},{7,3},{8,12},{12,8},{9,1... | collective-permute-start | bytes 49160 | tf_op jit(solution)/shard_map/ppermute | solution.py:96
  5.5 1.2 %collective-permute-start.7 = (f32[2,128,512]{2,1,0:T(8,128)S(1)}, f32[2,128,512]{2,1,0:T(8,128)S(1)}, u32[]{:S(2)}, u32[]{:S(2)}) collective-permute-start(f32[2,128,512]{2,1,0:T(8,128)S(1)} %copy-done.10), channel_id=1, source_target_pairs={{0,2},{1,3},{2,0},{3,1},{4,6},{5,7},{6,4},{7,5},{8,10},{9,11},{10,... | collective-permute-start | bytes 1572872 | tf_op jit(solution)/shard_map/ppermute | solution.py:110
  6.7 0.1 collective-permute-done.side_ref
  6.9 0.1 collective-permute-start.1
  7.0 4.4 %collective-permute-start.2 = (f32[272,128]{1,0:T(8,128)S(1)}, f32[272,128]{1,0:T(8,128)S(1)}, u32[]{:S(2)}, u32[]{:S(2)}) collective-permute-start(f32[272,128]{1,0:T(8,128)S(1)} %get-tuple-element.26), channel_id=1, source_target_pairs={{8,16},{16,8},{9,17},{17,9},{10,18},{18,10},{11,19},{19,11},{12,20... | collective-permute-start | bytes 417800 | tf_op jit(solution)/shard_map/ppermute | solution.py:102
  11.5 0.0 copy-start.12
  11.5 2.2 %grid_received.1.pre_ref = f32[1024,128]{1,0:T(8,128)S(1)} custom-call(f32[512,512]{1,0:T(8,128)S(1)} %bitcast.16, f32[2,512,128]{2,1,0:T(8,128)S(1)} %copy-done.3, f32[4,1024]{1,0:T(4,128)S(1)} %bitcast.18, f32[2,4,128]{2,1,0:T(4,128)S(1)} %copy-done.6, f32[2,128]{1,0:T(2,128)S(1)} %copy-done.8, s32[1,1024]{1,0:T(1,128)S(1)} %bitcast.21), custom_call_target="tpu_custom_call" | custom-call | flops 1073741824 | bytes 1048576 | tf_op jit(solution)/shard_map/grid_received/pallas_call | solution.py:78
  13.7 0.8 %grid_own.1.pre_ref = f32[1024,128]{1,0:T(8,128)S(1)} custom-call(f32[1024,128]{1,0:T(8,128)S(1)} %grid_received.1.pre_ref, f32[1024,128]{1,0:T(8,128)S(1)} %get-tuple-element.23.term_ref, s32[1,1024]{1,0:T(1,128)S(1)} %bitcast.19), custom_call_target="tpu_custom_call" | custom-call | flops 1073741824 | bytes 1048576 | tf_op jit(solution)/shard_map/grid_own/pallas_call | solution.py:78
  14.5 0.0 collective-permute-done.1.a_ref.rim_a_ref.refs_3_
  14.5 0.7 grid_hidden.1.refs_0_
  15.2 0.0 copy-start.2
  15.2 0.0 copy-start.14
  15.2 0.0 copy-start.15
  15.2 0.0 copy-start.16
  15.2 1.3 %collective-permute-start.4 = (f32[1024,128]{1,0:T(8,128)S(1)}, f32[1024,128]{1,0:T(8,128)S(1)}, u32[]{:S(2)}, u32[]{:S(2)}) collective-permute-start(f32[1024,128]{1,0:T(8,128)S(1)} %grid_hidden.1.refs_0_), channel_id=1, source_target_pairs={{0,2},{1,3},{2,0},{3,1},{4,6},{5,7},{6,4},{7,5},{8,10},{9,11},{10,... | collective-permute-start | bytes 1572872 | tf_op jit(solution)/shard_map/ppermute | solution.py:110
  16.5 2.7 %collective-permute-start.6 = (f32[2,128,512]{2,1,0:T(8,128)S(1)}, f32[2,128,512]{2,1,0:T(8,128)S(1)}, u32[]{:S(2)}, u32[]{:S(2)}) collective-permute-start(f32[2,128,512]{2,1,0:T(8,128)S(1)} %copy-done.10), channel_id=1, source_target_pairs={{0,1},{1,0},{2,3},{3,2},{4,5},{5,4},{6,7},{7,6},{8,9},{9,8},{10,11... | collective-permute-start | bytes 1572872 | tf_op jit(solution)/shard_map/ppermute | solution.py:110
  19.2 2.1 %collective-permute-start.8 = (f32[2,128,512]{2,1,0:T(8,128)S(1)}, f32[2,128,512]{2,1,0:T(8,128)S(1)}, u32[]{:S(2)}, u32[]{:S(2)}) collective-permute-start(f32[2,128,512]{2,1,0:T(8,128)S(1)} %collective-permute-done.7.refs_2_), channel_id=1, source_target_pairs={{0,1},{1,0},{2,3},{3,2},{4,5},{5,4},{6,7},{7,6},{8,9},{9,8},{10,11... | collective-permute-start | bytes 1572872 | tf_op jit(solution)/shard_map/ppermute | solution.py:110
  21.2 0.0 collective-permute-start.3
  21.2 8.0 %collective-permute-done.4.refs_2_ = f32[1024,128]{1,0:T(8,128)S(1)} collective-permute-done((f32[1024,128]{1,0:T(8,128)S(1)}, f32[1024,128]{1,0:T(8,128)S(1)}, u32[]{:S(2)}, u32[]{:S(2)}) %collective-permute-start.4) | collective-permute-done | bytes 524320 | tf_op jit(solution)/shard_map/ppermute | solution.py:110
  29.3 1.8 %collective-permute-start.5 = (f32[1024,128]{1,0:T(8,128)S(1)}, f32[1024,128]{1,0:T(8,128)S(1)}, u32[]{:S(2)}, u32[]{:S(2)}) collective-permute-start(f32[1024,128]{1,0:T(8,128)S(1)} %collective-permute-done.4.refs_2_), channel_id=1, source_target_pairs={{0,1},{1,0},{2,3},{3,2},{4,5},{5,4},{6,7},{7,6},{8,9},{9,8},{10,11... | collective-permute-start | bytes 1572872 | tf_op jit(solution)/shard_map/ppermute | solution.py:110
  31.1 0.0 collective-permute-done.6.refs_1_
  31.1 0.0 collective-permute-done.8.refs_3_
  31.1 0.3 weights.1
  31.4 0.0 collective-permute-done.3.refs_1_
  31.4 1.2 %collective-permute-done.5.refs_3_ = f32[1024,128]{1,0:T(8,128)S(1)} collective-permute-done((f32[1024,128]{1,0:T(8,128)S(1)}, f32[1024,128]{1,0:T(8,128)S(1)}, u32[]{:S(2)}, u32[]{:S(2)}) %collective-permute-start.5) | collective-permute-done | bytes 524320 | tf_op jit(solution)/shard_map/ppermute | solution.py:110
  32.6 0.0 copy-start.5
  32.6 0.0 copy-start.7
  32.6 4.0 %grid_message.1 = (f32[512,512]{1,0:T(8,128)S(1)}, f32[512,128]{1,0:T(8,128)S(1)}) custom-call(f32[1024,128]{1,0:T(8,128)S(1)} %grid_hidden.1.refs_0_, f32[1024,128]{1,0:T(8,128)S(1)} %collective-permute-done.3.refs_1_, f32[1024,128]{1,0:T(8,128)S(1)} %collective-permute-done.4.refs_2_, f32[1024,128]{1,0:T(8,128)S(1)} %collective-permute-done.5.refs_3_, ...), custom_call_target="tpu_custom_call" | custom-call | flops 3221225472 | bytes 1048576 | tf_op jit(solution)/shard_map/grid_message/pallas_call | solution.py:78
  36.7 0.3 collective-permute-start.9
  37.0 2.1 %mesh_first.1 = (f32[512,128]{1,0:T(8,128)S(1)}, f32[512,128]{1,0:T(8,128)S(1)}, f32[512,128]{1,0:T(8,128)S(1)}) custom-call(f32[512,128]{1,0:T(8,128)S(1)} %get-tuple-element.33.term_ref, f32[512,512]{1,0:T(8,128)S(1)} %get-tuple-element.34.mid_ref.refs_9_, f32[2,512,128]{2,1,0:T(8,128)S(1)} %copy-done.3, f32[4,512]{1,0:T(4,128)S(1)} %bitcast.13, ...), custom_call_target="tpu_custom_call" | custom-call | flops 536870912 | bytes 1048576 | tf_op jit(solution)/shard_map/mesh_first/pallas_call | solution.py:78
  39.1 5.1 %collective-permute-done.9.refs_0_ = f32[512,128]{1,0:T(8,128)S(1)} collective-permute-done((f32[512,128]{1,0:T(8,128)S(1)}, f32[512,128]{1,0:T(8,128)S(1)}, u32[]{:S(2)}, u32[]{:S(2)}) %collective-permute-start.9) | collective-permute-done | bytes 262176 | tf_op jit(solution)/shard_map/ppermute | solution.py:96
  44.2 0.5 mesh_sent.1
  44.8 0.2 collective-permute-start.10
  45.0 4.3 %collective-permute-start.11 = (f32[512,128]{1,0:T(8,128)S(1)}, f32[512,128]{1,0:T(8,128)S(1)}, u32[]{:S(2)}, u32[]{:S(2)}) collective-permute-start(f32[512,128]{1,0:T(8,128)S(1)} %get-tuple-element.39), channel_id=1, source_target_pairs={{8,16},{16,8},{9,17},{17,9},{10,18},{18,10},{11,19},{19,11},{12,20... | collective-permute-start | bytes 786440 | tf_op jit(solution)/shard_map/ppermute | solution.py:102
  49.3 0.4 mesh_own.1
  49.7 1.8 %collective-permute-done.10 = f32[512,128]{1,0:T(8,128)S(1)} collective-permute-done((f32[512,128]{1,0:T(8,128)S(1)}, f32[512,128]{1,0:T(8,128)S(1)}, u32[]{:S(2)}, u32[]{:S(2)}) %collective-permute-start.10) | collective-permute-done | bytes 262176 | tf_op jit(solution)/shard_map/ppermute | solution.py:102
  51.4 3.0 %collective-permute-done.11 = f32[512,128]{1,0:T(8,128)S(1)} collective-permute-done((f32[512,128]{1,0:T(8,128)S(1)}, f32[512,128]{1,0:T(8,128)S(1)}, u32[]{:S(2)}, u32[]{:S(2)}) %collective-permute-start.11) | collective-permute-done | bytes 262176 | tf_op jit(solution)/shard_map/ppermute | solution.py:102
  54.5 0.1 add_divide_fusion.refs_0_
  54.6 1.3 %collective-permute-start.13 = (f32[512,128]{1,0:T(8,128)S(1)}, f32[512,128]{1,0:T(8,128)S(1)}, u32[]{:S(2)}, u32[]{:S(2)}) collective-permute-start(f32[512,128]{1,0:T(8,128)S(1)} %add_divide_fusion.refs_0_), channel_id=1, source_target_pairs={{0,2},{1,3},{2,0},{3,1},{4,6},{5,7},{6,4},{7,5},{8,10},{9,11},{10,... | collective-permute-start | bytes 786440 | tf_op jit(solution)/shard_map/ppermute | solution.py:110
  55.8 2.4 %collective-permute-start.12 = (f32[512,128]{1,0:T(8,128)S(1)}, f32[512,128]{1,0:T(8,128)S(1)}, u32[]{:S(2)}, u32[]{:S(2)}) collective-permute-start(f32[512,128]{1,0:T(8,128)S(1)} %add_divide_fusion.refs_0_), channel_id=1, source_target_pairs={{0,1},{1,0},{2,3},{3,2},{4,5},{5,4},{6,7},{7,6},{8,9},{9,8},{10,11... | collective-permute-start | bytes 786440 | tf_op jit(solution)/shard_map/ppermute | solution.py:110
  58.2 2.2 %collective-permute-done.13.refs_2_ = f32[512,128]{1,0:T(8,128)S(1)} collective-permute-done((f32[512,128]{1,0:T(8,128)S(1)}, f32[512,128]{1,0:T(8,128)S(1)}, u32[]{:S(2)}, u32[]{:S(2)}) %collective-permute-start.13) | collective-permute-done | bytes 262176 | tf_op jit(solution)/shard_map/ppermute | solution.py:110
  60.4 3.0 %collective-permute-start.14 = (f32[512,128]{1,0:T(8,128)S(1)}, f32[512,128]{1,0:T(8,128)S(1)}, u32[]{:S(2)}, u32[]{:S(2)}) collective-permute-start(f32[512,128]{1,0:T(8,128)S(1)} %collective-permute-done.13.refs_2_), channel_id=1, source_target_pairs={{0,1},{1,0},{2,3},{3,2},{4,5},{5,4},{6,7},{7,6},{8,9},{9,8},{10,11... | collective-permute-start | bytes 786440 | tf_op jit(solution)/shard_map/ppermute | solution.py:110
  63.3 0.0 collective-permute-done.12.refs_1_
  63.3 1.2 %collective-permute-done.14.refs_3_ = f32[512,128]{1,0:T(8,128)S(1)} collective-permute-done((f32[512,128]{1,0:T(8,128)S(1)}, f32[512,128]{1,0:T(8,128)S(1)}, u32[]{:S(2)}, u32[]{:S(2)}) %collective-permute-start.14) | collective-permute-done | bytes 262176 | tf_op jit(solution)/shard_map/ppermute | solution.py:110
  64.5 2.2 %mesh_message.1 = f32[512,128]{1,0:T(8,128)} custom-call(f32[512,128]{1,0:T(8,128)S(1)} %add_divide_fusion.refs_0_, f32[512,128]{1,0:T(8,128)S(1)} %collective-permute-done.12.refs_1_, f32[512,128]{1,0:T(8,128)S(1)} %collective-permute-done.13.refs_2_, f32[512,128]{1,0:T(8,128)S(1)} %collective-permute-done.14.refs_3_, ...), custom_call_target="tpu_custom_call" | custom-call | flops 1073741824 | bytes 1048576 | tf_op jit(solution)/shard_map/mesh_message/pallas_call | solution.py:78
  (28 shorter events, 0.1 us)
Async XLA Ops:
  0.0 1.6 %copy-start = (f32[8,128,512]{2,1,0:T(8,128)S(1)}, f32[8,128,512]{2,1,0:T(8,128)}, u32[]{:S(2)}) copy-start(f32[8,128,512]{2,1,0:T(8,128)} %param.16) | copy-start | bytes 6291460
  1.6 1.0 %copy-start.1 = (f32[2,512,128]{2,1,0:T(8,128)S(1)}, f32[2,512,128]{2,1,0:T(8,128)}, u32[]{:S(2)}) copy-start(f32[2,512,128]{2,1,0:T(8,128)} %refs_10_.1) | copy-start | bytes 1572868
  2.6 2.9 %copy-start.10 = (f32[2,128,512]{2,1,0:T(8,128)S(1)}, f32[2,128,512]{2,1,0:T(8,128)}, u32[]{:S(2)}) copy-start(f32[2,128,512]{2,1,0:T(8,128)} %refs_0_) | copy-start | bytes 1572868
  2.6 4.2 %copy-start.4 = (s32[1,1,512]{2,1,0:T(1,128)S(1)}, s32[1,1,512]{2,1,0:T(1,128)}, u32[]{:S(2)}) copy-start(s32[1,1,512]{2,1,0:T(1,128)} %param.22) | copy-start | bytes 6148
  2.6 8.8 %copy-start.3 = (f32[2,512,128]{2,1,0:T(8,128)S(1)}, f32[2,512,128]{2,1,0:T(8,128)}, u32[]{:S(2)}) copy-start(f32[2,512,128]{2,1,0:T(8,128)} %weight_ref.5) | copy-start | bytes 1572868
  2.6 8.8 %copy-start.6 = (f32[2,4,128]{2,1,0:T(4,128)S(1)}, f32[2,4,128]{2,1,0:T(4,128)}, u32[]{:S(2)}) copy-start(f32[2,4,128]{2,1,0:T(4,128)} %edge_ref.3) | copy-start | bytes 12292
  2.6 8.8 %copy-start.8 = (f32[2,128]{1,0:T(2,128)S(1)}, f32[2,128]{1,0:T(2,128)}, u32[]{:S(2)}) copy-start(f32[2,128]{1,0:T(2,128)} %bias_ref.3) | copy-start | bytes 3076
  2.7 8.8 %copy-start.9 = (f32[1,1,512,512]{3,2,1,0:T(8,128)S(1)}, f32[1,1,512,512]{3,2,1,0:T(8,128)}, u32[]{:S(2)}) copy-start(f32[1,1,512,512]{3,2,1,0:T(8,128)} %param.17) | copy-start | bytes 3145732
  2.7 8.8 %copy-start.11 = (f32[1,1,4,1024]{3,2,1,0:T(4,128)S(1)}, f32[1,1,4,1024]{3,2,1,0:T(4,128)}, u32[]{:S(2)}) copy-start(f32[1,1,4,1024]{3,2,1,0:T(4,128)} %param.18) | copy-start | bytes 49156
  2.7 8.8 %copy-start.13 = (s32[1,1,1024]{2,1,0:T(1,128)S(1)}, s32[1,1,1024]{2,1,0:T(1,128)}, u32[]{:S(2)}) copy-start(s32[1,1,1024]{2,1,0:T(1,128)} %param.20) | copy-start | bytes 12292
  4.2 2.7 %collective-permute-start = (f32[32,128]{1,0:T(8,128)S(1)}, f32[32,128]{1,0:T(8,128)S(1)}, u32[]{:S(2)}, u32[]{:S(2)}) collective-permute-start(f32[32,128]{1,0:T(8,128)S(1)} %get-tuple-element.24), channel_id=1, source_target_pairs={{0,4},{4,0},{1,5},{5,1},{2,6},{6,2},{3,7},{7,3},{8,12},{12,8},{9,1... | collective-permute-start | bytes 49160 | tf_op jit(solution)/shard_map/ppermute | solution.py:96
  5.5 13.7 %collective-permute-start.7 = (f32[2,128,512]{2,1,0:T(8,128)S(1)}, f32[2,128,512]{2,1,0:T(8,128)S(1)}, u32[]{:S(2)}, u32[]{:S(2)}) collective-permute-start(f32[2,128,512]{2,1,0:T(8,128)S(1)} %copy-done.10), channel_id=1, source_target_pairs={{0,2},{1,3},{2,0},{3,1},{4,6},{5,7},{6,4},{7,5},{8,10},{9,11},{10,... | collective-permute-start | bytes 1572872 | tf_op jit(solution)/shard_map/ppermute | solution.py:110
  6.9 7.6 %collective-permute-start.1 = (f32[272,128]{1,0:T(8,128)S(1)}, f32[272,128]{1,0:T(8,128)S(1)}, u32[]{:S(2)}, u32[]{:S(2)}) collective-permute-start(f32[272,128]{1,0:T(8,128)S(1)} %get-tuple-element.25), channel_id=1, source_target_pairs={{0,8},{16,24},{8,0},{24,16},{1,9},{17,25},{9,1},{25,17},{2,10},{18... | collective-permute-start | bytes 417800 | tf_op jit(solution)/shard_map/ppermute | solution.py:102
  7.0 7.5 %collective-permute-start.2 = (f32[272,128]{1,0:T(8,128)S(1)}, f32[272,128]{1,0:T(8,128)S(1)}, u32[]{:S(2)}, u32[]{:S(2)}) collective-permute-start(f32[272,128]{1,0:T(8,128)S(1)} %get-tuple-element.26), channel_id=1, source_target_pairs={{8,16},{16,8},{9,17},{17,9},{10,18},{18,10},{11,19},{19,11},{12,20... | collective-permute-start | bytes 417800 | tf_op jit(solution)/shard_map/ppermute | solution.py:102
  11.5 2.2 %copy-start.12 = (s32[1,1,1024]{2,1,0:T(1,128)S(1)}, s32[1,1,1024]{2,1,0:T(1,128)}, u32[]{:S(2)}) copy-start(s32[1,1,1024]{2,1,0:T(1,128)} %param.19) | copy-start | bytes 12292
  15.2 17.4 %copy-start.2 = (f32[2,512,128]{2,1,0:T(8,128)S(1)}, f32[2,512,128]{2,1,0:T(8,128)}, u32[]{:S(2)}) copy-start(f32[2,512,128]{2,1,0:T(8,128)} %refs_10_.1) | copy-start | bytes 1572868
  15.2 17.4 %copy-start.14 = (f32[2,512]{1,0:T(2,128)S(1)}, f32[2,512]{1,0:T(2,128)}, u32[]{:S(2)}) copy-start(f32[2,512]{1,0:T(2,128)} %refs_5_.3) | copy-start | bytes 12292
  15.2 17.4 %copy-start.15 = (f32[2,512]{1,0:T(2,128)S(1)}, f32[2,512]{1,0:T(2,128)}, u32[]{:S(2)}) copy-start(f32[2,512]{1,0:T(2,128)} %refs_6_.3) | copy-start | bytes 12292
  15.2 17.4 %copy-start.16 = (f32[2,512]{1,0:T(2,128)S(1)}, f32[2,512]{1,0:T(2,128)}, u32[]{:S(2)}) copy-start(f32[2,512]{1,0:T(2,128)} %refs_7_.3) | copy-start | bytes 12292
  15.2 14.0 %collective-permute-start.4 = (f32[1024,128]{1,0:T(8,128)S(1)}, f32[1024,128]{1,0:T(8,128)S(1)}, u32[]{:S(2)}, u32[]{:S(2)}) collective-permute-start(f32[1024,128]{1,0:T(8,128)S(1)} %grid_hidden.1.refs_0_), channel_id=1, source_target_pairs={{0,2},{1,3},{2,0},{3,1},{4,6},{5,7},{6,4},{7,5},{8,10},{9,11},{10,... | collective-permute-start | bytes 1572872 | tf_op jit(solution)/shard_map/ppermute | solution.py:110
  16.5 14.6 %collective-permute-start.6 = (f32[2,128,512]{2,1,0:T(8,128)S(1)}, f32[2,128,512]{2,1,0:T(8,128)S(1)}, u32[]{:S(2)}, u32[]{:S(2)}) collective-permute-start(f32[2,128,512]{2,1,0:T(8,128)S(1)} %copy-done.10), channel_id=1, source_target_pairs={{0,1},{1,0},{2,3},{3,2},{4,5},{5,4},{6,7},{7,6},{8,9},{9,8},{10,11... | collective-permute-start | bytes 1572872 | tf_op jit(solution)/shard_map/ppermute | solution.py:110
  19.2 11.9 %collective-permute-start.8 = (f32[2,128,512]{2,1,0:T(8,128)S(1)}, f32[2,128,512]{2,1,0:T(8,128)S(1)}, u32[]{:S(2)}, u32[]{:S(2)}) collective-permute-start(f32[2,128,512]{2,1,0:T(8,128)S(1)} %collective-permute-done.7.refs_2_), channel_id=1, source_target_pairs={{0,1},{1,0},{2,3},{3,2},{4,5},{5,4},{6,7},{7,6},{8,9},{9,8},{10,11... | collective-permute-start | bytes 1572872 | tf_op jit(solution)/shard_map/ppermute | solution.py:110
  21.2 10.2 %collective-permute-start.3 = (f32[1024,128]{1,0:T(8,128)S(1)}, f32[1024,128]{1,0:T(8,128)S(1)}, u32[]{:S(2)}, u32[]{:S(2)}) collective-permute-start(f32[1024,128]{1,0:T(8,128)S(1)} %grid_hidden.1.refs_0_), channel_id=1, source_target_pairs={{0,1},{1,0},{2,3},{3,2},{4,5},{5,4},{6,7},{7,6},{8,9},{9,8},{10,11... | collective-permute-start | bytes 1572872 | tf_op jit(solution)/shard_map/ppermute | solution.py:110
  29.3 3.3 %collective-permute-start.5 = (f32[1024,128]{1,0:T(8,128)S(1)}, f32[1024,128]{1,0:T(8,128)S(1)}, u32[]{:S(2)}, u32[]{:S(2)}) collective-permute-start(f32[1024,128]{1,0:T(8,128)S(1)} %collective-permute-done.4.refs_2_), channel_id=1, source_target_pairs={{0,1},{1,0},{2,3},{3,2},{4,5},{5,4},{6,7},{7,6},{8,9},{9,8},{10,11... | collective-permute-start | bytes 1572872 | tf_op jit(solution)/shard_map/ppermute | solution.py:110
  32.6 4.3 %copy-start.5 = (f32[1,1,4,512]{3,2,1,0:T(4,128)S(1)}, f32[1,1,4,512]{3,2,1,0:T(4,128)}, u32[]{:S(2)}) copy-start(f32[1,1,4,512]{3,2,1,0:T(4,128)} %param.21) | copy-start | bytes 24580
  32.6 4.3 %copy-start.7 = (s32[1,1,512]{2,1,0:T(1,128)S(1)}, s32[1,1,512]{2,1,0:T(1,128)}, u32[]{:S(2)}) copy-start(s32[1,1,512]{2,1,0:T(1,128)} %param.23) | copy-start | bytes 6148
  36.7 7.5 %collective-permute-start.9 = (f32[512,128]{1,0:T(8,128)S(1)}, f32[512,128]{1,0:T(8,128)S(1)}, u32[]{:S(2)}, u32[]{:S(2)}) collective-permute-start(f32[512,128]{1,0:T(8,128)S(1)} %get-tuple-element.33.term_ref), channel_id=1, source_target_pairs={{0,4},{4,0},{1,5},{5,1},{2,6},{6,2},{3,7},{7,3},{8,12},{12,8},{9,1... | collective-permute-start | bytes 786440 | tf_op jit(solution)/shard_map/ppermute | solution.py:96
  44.8 6.7 %collective-permute-start.10 = (f32[512,128]{1,0:T(8,128)S(1)}, f32[512,128]{1,0:T(8,128)S(1)}, u32[]{:S(2)}, u32[]{:S(2)}) collective-permute-start(f32[512,128]{1,0:T(8,128)S(1)} %get-tuple-element.38), channel_id=1, source_target_pairs={{0,8},{16,24},{8,0},{24,16},{1,9},{17,25},{9,1},{25,17},{2,10},{18... | collective-permute-start | bytes 786440 | tf_op jit(solution)/shard_map/ppermute | solution.py:102
  45.0 9.5 %collective-permute-start.11 = (f32[512,128]{1,0:T(8,128)S(1)}, f32[512,128]{1,0:T(8,128)S(1)}, u32[]{:S(2)}, u32[]{:S(2)}) collective-permute-start(f32[512,128]{1,0:T(8,128)S(1)} %get-tuple-element.39), channel_id=1, source_target_pairs={{8,16},{16,8},{9,17},{17,9},{10,18},{18,10},{11,19},{19,11},{12,20... | collective-permute-start | bytes 786440 | tf_op jit(solution)/shard_map/ppermute | solution.py:102
  54.6 5.8 %collective-permute-start.13 = (f32[512,128]{1,0:T(8,128)S(1)}, f32[512,128]{1,0:T(8,128)S(1)}, u32[]{:S(2)}, u32[]{:S(2)}) collective-permute-start(f32[512,128]{1,0:T(8,128)S(1)} %add_divide_fusion.refs_0_), channel_id=1, source_target_pairs={{0,2},{1,3},{2,0},{3,1},{4,6},{5,7},{6,4},{7,5},{8,10},{9,11},{10,... | collective-permute-start | bytes 786440 | tf_op jit(solution)/shard_map/ppermute | solution.py:110
  55.8 7.5 %collective-permute-start.12 = (f32[512,128]{1,0:T(8,128)S(1)}, f32[512,128]{1,0:T(8,128)S(1)}, u32[]{:S(2)}, u32[]{:S(2)}) collective-permute-start(f32[512,128]{1,0:T(8,128)S(1)} %add_divide_fusion.refs_0_), channel_id=1, source_target_pairs={{0,1},{1,0},{2,3},{3,2},{4,5},{5,4},{6,7},{7,6},{8,9},{9,8},{10,11... | collective-permute-start | bytes 786440 | tf_op jit(solution)/shard_map/ppermute | solution.py:110
  60.4 4.1 %collective-permute-start.14 = (f32[512,128]{1,0:T(8,128)S(1)}, f32[512,128]{1,0:T(8,128)S(1)}, u32[]{:S(2)}, u32[]{:S(2)}) collective-permute-start(f32[512,128]{1,0:T(8,128)S(1)} %collective-permute-done.13.refs_2_), channel_id=1, source_target_pairs={{0,1},{1,0},{2,3},{3,2},{4,5},{5,4},{6,7},{7,6},{8,9},{9,8},{10,11... | collective-permute-start | bytes 786440 | tf_op jit(solution)/shard_map/ppermute | solution.py:110

commit v4 on v3

--- a/solution.py
+++ b/solution.py
@@ -74,14 +74,13 @@
 VMEM = pl.BlockSpec(memory_space=pltpu.VMEM)
 
 
-def call(name, body, outs, flops, args, scratch=()):
+def call(body, outs, flops, args, scratch=()):
     return pl.pallas_call(
         body,
         out_shape=outs,
         in_specs=[VMEM] * len(args),
         out_specs=jax.tree.map(lambda _: VMEM, outs),
         scratch_shapes=scratch,
-        name=name,
         compiler_params=pltpu.CompilerParams(vmem_limit_bytes=KERNEL_VMEM),
         cost_estimate=pl.CostEstimate(flops=flops, bytes_accessed=1 << 20, transcendentals=0),
     )(*args)
@@ -100,6 +99,31 @@
     count = lax.axis_size("lat")
     pairs = [(i, i + 1) for i in range(first, count - 1, 2)]
     return lax.ppermute(value, "lat", pairs + [(high, low) for low, high in pairs])
+
+
+def by_role(value, lon_parity, lon_step, lat_first):
+    lat_count, lon_count = lax.axis_size("lat"), lax.axis_size("lon")
+    hid_count = lax.axis_size("hid")
+    pairs = []
+    for lat in range(lat_count):
+        for lon in range(lon_count):
+            for hid in range(hid_count):
+                to_lat, to_lon = lat, lon
+                if hid % 2 == lon_parity:
+                    if lon_step is None:
+                        continue
+                    to_lon = (lon + lon_step) % lon_count
+                else:
+                    to_lat = lat_first + ((lat - lat_first) ^ 1)
+                    if lat < lat_first or to_lat >= lat_count:
+                        continue
+                pairs.append(
+                    (
+                        (lat * lon_count + lon) * hid_count + hid,
+                        (to_lat * lon_count + to_lon) * hid_count + hid,
+                    )
+                )
+    return lax.ppermute(value, ("lat", "lon", "hid"), pairs)
 
 
 def gather_hid(value):
@@ -128,11 +152,11 @@
         store(start, step, layer_norm(message, gain, shift_row))
 
 
-def aggregate(receiver_row, nodes, normed_ref):
+def aggregate(receiver_row, nodes, normed):
     node = lax.broadcasted_iota(jnp.int32, (nodes, receiver_row.shape[1]), 0)
     onehot = jnp.where(node == receiver_row, 1.0, 0.0).astype(BF16)
-    width = normed_ref.shape[1] // 2
-    both = dot(onehot, normed_ref[...])
+    width = normed.shape[1] // 2
+    both = dot(onehot, normed)
     return both[:, :width] + both[:, width:]
 
 
@@ -168,8 +192,9 @@
     mesh_ids = mesh_senders.reshape(1, mesh_edges)
     mesh_to = mesh_receivers.reshape(1, mesh_edges)
     two_lon = lon_count == 2
+    id_rows = mesh_edges // LANES
     side_size = rows * 2 * RIM
-    id_rows = mesh_edges // LANES
+    side_rows = side_size + id_rows + -(side_size + id_rows) % 8
     lat_size = RIM * cols + RIM * 2 * RIM
     lat_rows = lat_size + id_rows + -(lat_size + id_rows) % 16
 
@@ -194,122 +219,167 @@
         beyond = jnp.where(in_rows, jnp.where(in_cols, -1, row * 2 * RIM + slot), rim)
         return own, beyond
 
+    def lat_partners():
+        lat_index = lax.axis_index("lat")
+        turn = 1 - 2 * (lat_index % 2)
+        return lat_index + turn, lat_index - turn
+
     def sender_nodes(ids):
         source, node = divide(ids, nodes)
         source_lat, source_lon = divide(source, lon_count)
-        here = source_lat == lax.axis_index("lat")
         offset = divide(source_lon - lax.axis_index("lon") + lon_count, lon_count)[1]
-        tables = [0, 1] if two_lon else [0, lon_count - 1, 1]
-        return [jnp.where(here & (offset == place), node, -1) for place in tables]
-
-    def ids_in(rim_ref):
-        rim_ids = [rim_ref[lat_size + row : lat_size + row + 1, :] for row in range(id_rows)]
-        return jnp.concatenate(rim_ids, axis=1).astype(jnp.int32)
-
-    step_rows = 2 if rows % 2 == 0 else 1
-
-    def terms_body(cell_ref, weight_ref, term_ref, side_ref):
-        term_ref[...] = dot_split(cell_ref[...], weight_ref[...])
-        for row in range(step_rows):
+        tag = source_lat * lon_count + offset
+        own = lax.axis_index("lat") * lon_count
+        odd = lax.axis_index("hid") % 2 == 1
+        first, second = lat_partners()
+        first = jnp.where(odd, first * lon_count, own + (1 if two_lon else lon_count - 1))
+        second = jnp.where(odd, second * lon_count, -1 if two_lon else own + 1)
+        return [jnp.where(tag == place, node, -1) for place in (own, first, second)]
+
+    def choose_ids(lat_ref, lat_start, lon_ref):
+        odd = lax.axis_index("hid") % 2 == 1
+        return jnp.where(odd, ids_in(lon_ref, side_size), ids_in(lat_ref, lat_start))
+
+    def ids_in(ref, start):
+        rows_of = [ref[start + row : start + row + 1, :] for row in range(id_rows)]
+        return jnp.concatenate(rows_of, axis=1).astype(jnp.int32)
+
+    def put_ids(ref, start, id_ref):
+        ids = id_ref[...].astype(F32)
+        for row in range(id_rows):
+            ref[start + row : start + row + 1, :] = ids[:, row * LANES : (row + 1) * LANES]
+        end = start + id_rows
+        if end < ref.shape[0]:
+            ref[end:, :] = jnp.zeros((ref.shape[0] - end, units), F32)
+
+    def side_table(low_ref, high_ref):
+        if two_lon:
+            return low_ref[:side_size, :]
+        slot = lax.broadcasted_iota(jnp.int32, (side_size, units), 0) % (2 * RIM)
+        return jnp.where(slot < RIM, high_ref[:side_size, :], low_ref[:side_size, :])
+
+    out_pieces = gather_hid(out_weight)
+
+    chunk = rows * cols // 4
+
+    def terms_body(
+        cell_ref, weight_ref, id_ref, term_ref, side_ref, cell_vmem, weight_vmem, id_vmem, sems
+    ):
+        loads = [
+            pltpu.make_async_copy(weight_ref.at[0], weight_vmem, sems.at[0]),
+            pltpu.make_async_copy(id_ref, id_vmem, sems.at[1]),
+        ]
+        for step in range(4):
+            part = pl.ds(step * chunk, chunk)
+            loads.append(
+                pltpu.make_async_copy(cell_ref.at[part], cell_vmem.at[part], sems.at[step + 2])
+            )
+        for load in loads:
+            load.start()
+        loads[0].wait()
+        for step in range(4):
+            loads[step + 2].wait()
+            start = step * chunk
+            term_ref[start : start + chunk, :] = dot_split(
+                cell_vmem[start : start + chunk, :], weight_vmem[...]
+            )
+        loads[1].wait()
+        put_ids(side_ref, side_size, id_vmem)
+        for row in range(rows):
             start = row * 2 * RIM
             side_ref[start : start + RIM, :] = term_ref[row * cols : row * cols + RIM, :]
             side_ref[start + RIM : start + 2 * RIM, :] = term_ref[
                 (row + 1) * cols - RIM : (row + 1) * cols, :
             ]
 
+    hbm = pl.BlockSpec(memory_space=pltpu.HBM)
     terms, sides = pl.pallas_call(
         terms_body,
-        grid=(rows // step_rows,),
-        in_specs=[
-            pl.BlockSpec((step_rows * cols, width), lambda i: (i, 0)),
-            pl.BlockSpec((None, width, units), lambda i: (0, 0, 0)),
+        out_shape=(shape(rows * cols, units), shape(side_rows, units)),
+        in_specs=[hbm, hbm, hbm],
+        out_specs=(VMEM, VMEM),
+        scratch_shapes=[
+            pltpu.VMEM((rows * cols, width), F32),
+            pltpu.VMEM((width, units), F32),
+            pltpu.VMEM((1, mesh_edges), jnp.int32),
+            pltpu.SemaphoreType.DMA((6,)),
         ],
-        out_shape=(shape(rows * cols, units), shape(side_size, units)),
-        out_specs=(
-            pl.BlockSpec((step_rows * cols, units), lambda i: (i, 0)),
-            pl.BlockSpec((step_rows * 2 * RIM, units), lambda i: (i, 0)),
-        ),
         name="grid_terms",
         compiler_params=pltpu.CompilerParams(vmem_limit_bytes=KERNEL_VMEM),
         cost_estimate=pl.CostEstimate(
             flops=6 * rows * cols * width * units, bytes_accessed=1 << 21, transcendentals=0
         ),
-    )(cells, sender_weight)
-    if two_lon:
-        side_got = shift(sides, "lon", 1)
-    else:
-        parts = sides.reshape(rows, 2, RIM, units)
-        from_high = shift(parts[:, 0], "lon", -1)
-        from_low = shift(parts[:, 1], "lon", 1)
-        side_got = jnp.stack([from_high, from_low], axis=1).reshape(side_size, units)
-
-    out_pieces = gather_hid(lax.optimization_barrier((out_weight, sides))[0])
-
-    def grid_received_body(mesh_ref, weight_ref, feat_ref, edge_ref, bias_ref, recv_ref, pre_ref):
-        received = dot_split(mesh_ref[...], weight_ref[0])
-        pre_ref[...] = (
-            pick(local(recv_ref[...]), received)
+    )(
+        pltpu.with_memory_space_constraint(cells, pltpu.HBM),
+        pltpu.with_memory_space_constraint(sender_weight, pltpu.HBM),
+        pltpu.with_memory_space_constraint(mesh_ids, pltpu.HBM),
+    )
+    side_low = shift(sides, "lon", 1)
+    side_high = side_low if two_lon else shift(sides, "lon", -1)
+
+    def grid_own_body(term_ref, feat_ref, edge_ref, bias_ref, send_ref, out_ref):
+        out_ref[...] = (
+            pick(cell_places(send_ref[...])[0], term_ref[...])
             + edge_terms(feat_ref[...], edge_ref[0])
             + bias_ref[0:1, :]
         )
 
     grid_pre = call(
-        "grid_received",
+        grid_own_body,
+        shape(grid_edges, units),
+        8 * grid_edges * rows * cols * units,
+        (terms, grid_edge_feats.reshape(-1, grid_edges), edge_weight, first_bias, grid_ids),
+    )
+
+    def grid_received_body(pre_ref, mesh_ref, weight_ref, recv_ref, out_ref):
+        received = dot_split(mesh_ref[...], weight_ref[0])
+        out_ref[...] = pre_ref[...] + pick(local(recv_ref[...]), received)
+
+    grid_pre = call(
         grid_received_body,
         shape(grid_edges, units),
         8 * grid_edges * rows * cols * units,
-        (mesh_own, receiver_weight, grid_edge_feats.reshape(-1, grid_edges), edge_weight, first_bias, grid_to),
-    )
-
-    def rim_body(term_ref, side_ref, id_ref, a_ref, b_ref):
+        (grid_pre, mesh_own, receiver_weight, grid_to),
+    )
+
+    def rim_body(term_ref, low_ref, high_ref, id_ref, a_ref, b_ref):
         odd = lax.axis_index("lat") % 2
+        table = side_table(low_ref, high_ref)
         for ref, up in ((a_ref, 1 - odd), (b_ref, odd)):
             start = up * (rows - RIM)
             ref[: RIM * cols, :] = term_ref[pl.ds(pl.multiple_of(start * cols, 8), RIM * cols), :]
             ref[RIM * cols : lat_size, :] = jnp.where(
-                up == 1,
-                side_ref[(rows - RIM) * 2 * RIM : rows * 2 * RIM, :],
-                side_ref[: RIM * 2 * RIM, :],
+                up == 1, table[(rows - RIM) * 2 * RIM :, :], table[: RIM * 2 * RIM, :]
             )
-            ids = id_ref[...].astype(F32)
-            for row in range(id_rows):
-                ref[lat_size + row : lat_size + row + 1, :] = ids[:, row * LANES : (row + 1) * LANES]
-            ref[lat_size + id_rows :, :] = jnp.zeros((lat_rows - lat_size - id_rows, units), F32)
+            put_ids(ref, lat_size, id_ref)
 
     rim_block = shape(lat_rows, units)
     rim_a, rim_b = call(
-        "grid_rim", rim_body, (rim_block, rim_block), 1 << 20, (terms, side_got, mesh_ids)
+        rim_body, (rim_block, rim_block), 1 << 20, (terms, side_low, side_high, mesh_ids)
     )
     rim_a = swap_lat(rim_a, 0)
     rim_b = swap_lat(rim_b, 1)
 
-    def grid_own_body(pre_ref, term_ref, send_ref, out_ref):
-        out_ref[...] = pre_ref[...] + pick(cell_places(send_ref[...])[0], term_ref[...])
-
-    grid_pre = call(
-        "grid_own",
-        grid_own_body,
-        shape(grid_edges, units),
-        8 * grid_edges * rows * cols * units,
-        (grid_pre, terms, grid_ids),
-    )
-
-    def grid_hidden_body(pre_ref, side_ref, a_ref, b_ref, send_ref, hidden_ref):
+    halves = [shape(grid_edges // 2, units)] * 2
+
+    def grid_hidden_body(pre_ref, low_ref, high_ref, a_ref, b_ref, send_ref, *hidden_refs):
         pad = -(side_size + 2 * lat_rows) % LANES
         table = jnp.concatenate(
-            [side_ref[...], a_ref[...], b_ref[...], jnp.zeros((pad, units), F32)], axis=0
+            [side_table(low_ref, high_ref), a_ref[...], b_ref[...], jnp.zeros((pad, units), F32)],
+            axis=0,
         )
         total = pre_ref[...] + pick(cell_places(send_ref[...])[1], table)
-        hidden_ref[...] = total / (1.0 + jnp.exp(-total))
+        total = total / (1.0 + jnp.exp(-total))
+        for half, ref in enumerate(hidden_refs):
+            ref[...] = total[half * ref.shape[0] : (half + 1) * ref.shape[0], :]
 
     grid_hidden = call(
-        "grid_hidden",
         grid_hidden_body,
-        shape(grid_edges, units),
+        tuple(halves),
         4 * grid_edges * rows * cols * units,
-        (grid_pre, side_got, rim_a, rim_b, grid_ids),
-    )
-    grid_pieces = gather_hid(grid_hidden)
+        (grid_pre, side_low, side_high, rim_a, rim_b, grid_ids),
+    )
+    grid_pieces = [gather_hid(part) for part in grid_hidden]
 
     def weight_body(*refs):
         for section in range(2):
@@ -321,18 +391,11 @@
             out_ref[2 * width :, :] = high
 
     weight_block = shape(3 * width, width, dtype=BF16)
-    whole_weights = call(
-        "weights",
-        weight_body,
-        (weight_block, weight_block),
-        1 << 30,
-        lax.optimization_barrier((*out_pieces, grid_hidden))[:hid_count],
-    )
+    grid_weight, mesh_weight = call(weight_body, (weight_block, weight_block), 1 << 28, out_pieces)
 
     def grid_message_body(*refs):
         hidden_refs = refs[:hid_count]
-        weight_ref, bias_ref, gain_ref, shift_ref, recv_ref, mesh_ref, send_ref = refs[hid_count:-3]
-        mid_ref, term_ref, normed_ref = refs[-3:]
+        weight_ref, bias_ref, gain_ref, shift_ref, normed_ref = refs[hid_count:]
 
         def store(start, step, normed):
             high, low = split(normed)
@@ -342,31 +405,41 @@
         normed_chunks(
             hidden_refs, weight_ref, bias_ref[0:1, :], gain_ref[0:1, :], shift_ref[0:1, :], store
         )
-        middle = mesh_ref[...] + aggregate(local(recv_ref[...]), nodes, normed_ref)
+
+    normed_parts = [
+        call(
+            grid_message_body,
+            shape(grid_edges // 2, 2 * width, dtype=BF16),
+            4 * grid_edges * width * width,
+            (*pieces, grid_weight, out_bias, norm_gain, norm_shift),
+        )
+        for pieces in grid_pieces
+    ]
+
+    def grid_sum_body(first_ref, second_ref, recv_ref, mesh_ref, send_ref, mid_ref, term_ref):
+        normed = jnp.concatenate([first_ref[...], second_ref[...]], axis=0)
+        middle = mesh_ref[...] + aggregate(local(recv_ref[...]), nodes, normed)
         mid_ref[...] = middle
         term_ref[...] = dot_split(middle, send_ref[1])
 
     mesh_mid, mesh_terms = call(
-        "grid_message",
-        grid_message_body,
+        grid_sum_body,
         (shape(nodes, width), shape(nodes, units)),
-        12 * grid_edges * width * width,
-        (*grid_pieces, whole_weights[0], out_bias, norm_gain, norm_shift, grid_to, mesh_own, sender_weight),
-        (pltpu.VMEM((grid_edges, 2 * width), BF16),),
-    )
-
-    others = [shift(mesh_terms, "lon", 1)]
-    if not two_lon:
-        others.append(shift(mesh_terms, "lon", -1))
-    table_count = len(others)
+        4 * grid_edges * width * width,
+        (*normed_parts, grid_to, mesh_own, sender_weight),
+    )
+
+    back = None if two_lon else -1
+    table_a = by_role(mesh_terms, 0, 1, 0)
+    table_b = by_role(mesh_terms, 0, back, 1)
 
     def mesh_first_body(
-        term_ref, mid_ref, weight_ref, feat_ref, edge_ref, bias_ref, recv_ref, id_ref, rim_a_ref, rim_b_ref,
-        pre_ref, a_ref, b_ref,
+        term_ref, mid_ref, weight_ref, feat_ref, edge_ref, bias_ref, recv_ref, id_ref,
+        rim_a_ref, rim_b_ref, low_ref, high_ref, pre_ref, a_ref, b_ref,
     ):
         table = term_ref[...]
-        a_ref[...] = pick(sender_nodes(ids_in(rim_a_ref))[0], table)
-        b_ref[...] = pick(sender_nodes(ids_in(rim_b_ref))[0], table)
+        a_ref[...] = pick(sender_nodes(choose_ids(rim_a_ref, lat_size, high_ref))[0], table)
+        b_ref[...] = pick(sender_nodes(choose_ids(rim_b_ref, lat_size, low_ref))[0], table)
         received = dot_split(mid_ref[...], weight_ref[1])
         pre_ref[...] = (
             pick(sender_nodes(id_ref[...])[0], table)
@@ -377,13 +450,12 @@
 
     edge_block = shape(mesh_edges, units)
     mesh_pre, send_a, send_b = call(
-        "mesh_first",
         mesh_first_body,
         (edge_block, edge_block, edge_block),
         16 * mesh_edges * nodes * units,
         (
             mesh_terms, mesh_mid, receiver_weight, mesh_edge_feats.reshape(-1, mesh_edges), edge_weight,
-            first_bias, mesh_to, mesh_ids, rim_a, rim_b,
+            first_bias, mesh_to, mesh_ids, rim_a, rim_b, side_low, side_high,
         ),
     )
 
@@ -393,32 +465,30 @@
             total = total + pick(index_row, table_ref[...])
         return total
 
-    def mesh_sent_body(*refs):
-        tables = refs[:table_count]
-        first_a, first_b, rim_a_ref, rim_b_ref, a_ref, b_ref = refs[table_count:]
-        a_ref[...] = add_others(first_a, ids_in(rim_a_ref), tables)
-        b_ref[...] = add_others(first_b, ids_in(rim_b_ref), tables)
+    def mesh_sent_body(
+        table_a_ref, table_b_ref, first_a, first_b, rim_a_ref, rim_b_ref, low_ref, high_ref, a_ref, b_ref
+    ):
+        tables = (table_a_ref, table_b_ref)
+        a_ref[...] = add_others(first_a, choose_ids(rim_a_ref, lat_size, high_ref), tables)
+        b_ref[...] = add_others(first_b, choose_ids(rim_b_ref, lat_size, low_ref), tables)
 
     send_a, send_b = call(
-        "mesh_sent",
         mesh_sent_body,
         (edge_block, edge_block),
-        8 * mesh_edges * nodes * units,
-        (*others, send_a, send_b, rim_a, rim_b),
-    )
-    got_a = swap_lat(send_a, 0)
-    got_b = swap_lat(send_b, 1)
-
-    def mesh_own_body(*refs):
-        first_ref, id_ref, out_ref = refs[table_count:]
-        out_ref[...] = add_others(first_ref, id_ref[...], refs[:table_count])
+        16 * mesh_edges * nodes * units,
+        (table_a, table_b, send_a, send_b, rim_a, rim_b, side_low, side_high),
+    )
+    got_a = by_role(send_a, 1, 1, 0)
+    got_b = by_role(send_b, 1, back, 1)
+
+    def mesh_own_body(table_a_ref, table_b_ref, first_ref, id_ref, out_ref):
+        out_ref[...] = add_others(first_ref, id_ref[...], (table_a_ref, table_b_ref))
 
     mesh_pre = call(
-        "mesh_own",
         mesh_own_body,
         edge_block,
-        4 * mesh_edges * nodes * units,
-        (*others, mesh_pre, mesh_ids),
+        8 * mesh_edges * nodes * units,
+        (table_a, table_b, mesh_pre, mesh_ids),
     )
     total = mesh_pre + got_a + got_b
     mesh_pieces = gather_hid(total / (1.0 + jnp.exp(-total)))
@@ -443,14 +513,13 @@
         normed_chunks(
             hidden_refs, weight_ref, bias_ref[1:2, :], gain_ref[1:2, :], shift_ref[1:2, :], store
         )
-        out_ref[...] = own_part(mid_ref[...]) + aggregate(local(recv_ref[...]), nodes, normed_ref)
+        out_ref[...] = own_part(mid_ref[...]) + aggregate(local(recv_ref[...]), nodes, normed_ref[...])
 
     mesh_out = call(
-        "mesh_message",
         mesh_message_body,
         shape(nodes, share),
         8 * mesh_edges * width * width,
-        (*mesh_pieces, whole_weights[1], out_bias, norm_gain, norm_shift, mesh_to, mesh_mid),
+        (*mesh_pieces, mesh_weight, out_bias, norm_gain, norm_shift, mesh_to, mesh_mid),
         (pltpu.VMEM((mesh_edges, 2 * share), BF16),),
     )
     return mesh_out.reshape(1, 1, nodes, share)

time: 66.9 us -> 63.8 us (0.954)
  waiting for transfers between devices: 22.6 us -> 19.5 us
  Pallas kernels: 14.7 us -> 17.2 us
  local copies, waits for them, and re-layouts: 2.71 us -> 0.21 us
    ppermute x0 -> x4, waiting for transfers between devices: none -> 5.66 us  [by_role(): return lax.ppermute(value, ('lat', 'lon', 'hid'), pairs)]
    ppermute x2 -> x1, waiting for transfers between devices: 5.27 us -> 0.45 us  [shift(): lax.ppermute(value, axis, [(i, (i + step) % count) for i in range(count)])]
    ppermute x4 -> x2, waiting for transfers between devices: 4.79 us -> 0.01 us  [swap_lat(): lax.ppermute(value, 'lat', pairs + [(high, low) for low, high in pairs])]
    ppermute x4 -> x2, starting transfers between devices: 9.11 us -> 4.55 us  [swap_lat(): lax.ppermute(value, 'lat', pairs + [(high, low) for low, high in pairs])]
    ppermute x0 -> x4, starting transfers between devices: none -> 4.39 us  [by_role(): return lax.ppermute(value, ('lat', 'lon', 'hid'), pairs)]
    unnamed x34 -> x30, local copies, waits for them, and re-layouts: 2.71 us -> 0.21 us
    pallas_call x10 -> x12, Pallas kernels: 13.2 us -> 14.5 us  [call(): pl.pallas_call(body, out_shape=outs, in_specs=[VMEM] * len(args), out_spe...]
    pallas_call x1, Pallas kernels: 1.49 us -> 2.68 us  [per_device(): pl.pallas_call(terms_body, out_shape=(shape(rows * cols, units), shape(si...]
  transfers between devices with their start and end apart: 15 -> 19, of which waited for: 8 -> 8; matrix products, arithmetic and copies ran while one was open for 0% -> 0% of each run, Pallas kernels for 10% -> 16%
where the time goes in v4:
time: 63.8 us; the launch traced here: 63.6 us
  starting transfers between devices  26.3 us (41%)
  waiting for transfers between devices  19.5 us (31%)
  Pallas kernels  17.2 us (27%)
    ppermute x12, starting transfers between devices, gather_hid(): lax.ppermute(source, 'hid', [(i, i ^ hop) for i in range(count)])  16.1 us
    pallas_call x12, Pallas kernels, call(): pl.pallas_call(body, out_shape=outs, in_specs=[VMEM] * len(args), out_spe...  14.5 us
    ppermute x12, waiting for transfers between devices, gather_hid(): lax.ppermute(source, 'hid', [(i, i ^ hop) for i in range(count)])  13.3 us
    ppermute x4, waiting for transfers between devices, by_role(): return lax.ppermute(value, ('lat', 'lon', 'hid'), pairs)  5.66 us
    ppermute x2, starting transfers between devices, swap_lat(): lax.ppermute(value, 'lat', pairs + [(high, low) for low, high in pairs])  4.55 us
    ppermute x4, starting transfers between devices, by_role(): return lax.ppermute(value, ('lat', 'lon', 'hid'), pairs)  4.39 us
    pallas_call x1, Pallas kernels, per_device(): pl.pallas_call(terms_body, out_shape=(shape(rows * cols, units), shape(si...  2.68 us
    ppermute x1, starting transfers between devices, shift(): lax.ppermute(value, axis, [(i, (i + step) % count) for i in range(count)])  1.3 us
  transfers between devices with their start and end apart: 19, of which 8 were waited for; matrix products, arithmetic and copies ran while one was open for 0% of the time, Pallas kernels for 16%

profile of v4, /device:TPU:9, one launch (start us, length us, event | category | flops | bytes accessed | tf_op | source)
XLA Modules:
  0.0 63.6 jit_solution(16723967661980817470)
XLA Ops:
  0.0 1.2 %collective-permute-start.7 = (f32[2,128,512]{2,1,0:T(8,128)}, f32[2,128,512]{2,1,0:T(8,128)S(1)}, u32[]{:S(2)}, u32[]{:S(2)}) collective-permute-start(f32[2,128,512]{2,1,0:T(8,128)} %refs_0_.1), channel_id=1, source_target_pairs={{0,2},{1,3},{2,0},{3,1},{4,6},{5,7},{6,4},{7,5},{8,10},{9,11},{10,... | collective-permute-start | bytes 1572872 | tf_op jit(solution)/shard_map/ppermute | solution.py:134
  1.2 2.7 %grid_terms.1 = (f32[1024,128]{1,0:T(8,128)S(1)}, f32[40,128]{1,0:T(8,128)S(1)}) custom-call(f32[1024,512]{1,0:T(8,128)} %bitcast.23, f32[2,512,128]{2,1,0:T(8,128)} %send_ref.1, s32[1,512]{1,0:T(1,128)} %bitcast.9), custom_call_target="tpu_custom_call" | custom-call | flops 402653184 | bytes 2097152 | tf_op jit(solution)/shard_map/grid_terms/pallas_call | solution.py:296
  3.9 1.3 %collective-permute-start = (f32[40,128]{1,0:T(8,128)S(1)}, f32[40,128]{1,0:T(8,128)S(1)}, u32[]{:S(2)}, u32[]{:S(2)}) collective-permute-start(f32[40,128]{1,0:T(8,128)S(1)} %get-tuple-element.21), channel_id=1, source_target_pairs={{0,4},{4,0},{1,5},{5,1},{2,6},{6,2},{3,7},{7,3},{8,12},{12,8},{9,1... | collective-permute-start | bytes 61448 | tf_op jit(solution)/shard_map/ppermute | solution.py:95
  5.2 1.2 %collective-permute-start.6 = (f32[2,128,512]{2,1,0:T(8,128)S(1)}, f32[2,128,512]{2,1,0:T(8,128)S(1)}, u32[]{:S(2)}, u32[]{:S(2)}) collective-permute-start(f32[2,128,512]{2,1,0:T(8,128)S(1)} %copy-done), channel_id=1, source_target_pairs={{0,1},{1,0},{2,3},{3,2},{4,5},{5,4},{6,7},{7,6},{8,9},{9,8},{10,11... | collective-permute-start | bytes 1572872 | tf_op jit(solution)/shard_map/ppermute | solution.py:134
  6.5 0.4 collective-permute-done.low_ref.high_ref
  6.9 0.2 collective-permute-start.1
  7.2 4.3 %collective-permute-start.2 = (f32[272,128]{1,0:T(8,128)S(1)}, f32[272,128]{1,0:T(8,128)S(1)}, u32[]{:S(2)}, u32[]{:S(2)}) collective-permute-start(f32[272,128]{1,0:T(8,128)S(1)} %get-tuple-element.23), channel_id=1, source_target_pairs={{8,16},{16,8},{9,17},{17,9},{10,18},{18,10},{11,19},{19,11},{12,20... | collective-permute-start | bytes 417800 | tf_op jit(solution)/shard_map/ppermute | solution.py:101
  11.5 0.0 copy-start.2
  11.6 0.0 copy-start.8
  11.6 0.0 copy-start.11
  11.6 1.2 %shard_map.154.pre_ref = f32[1024,128]{1,0:T(8,128)S(1)} custom-call(f32[1024,128]{1,0:T(8,128)S(1)} %get-tuple-element.20.term_ref, f32[4,1024]{1,0:T(4,128)S(1)} %bitcast.18, f32[2,4,128]{2,1,0:T(4,128)S(1)} %copy-done.5, f32[2,128]{1,0:T(2,128)S(1)} %copy-done.7, s32[1,1024]{1,0:T(1,128)S(1)} %bitcast.19), custom_call_target="tpu_custom_call" | custom-call | flops 1073741824 | bytes 1048576 | tf_op jit(solution)/shard_map/pallas_call | solution.py:78
  12.8 0.1 copy-done.8
  12.9 1.4 %shard_map.155.pre_ref = f32[1024,128]{1,0:T(8,128)S(1)} custom-call(f32[1024,128]{1,0:T(8,128)S(1)} %shard_map.154.pre_ref, f32[512,512]{1,0:T(8,128)S(1)} %bitcast.16, f32[2,512,128]{2,1,0:T(8,128)S(1)} %copy-done.2, s32[1,1024]{1,0:T(1,128)S(1)} %bitcast.21), custom_call_target="tpu_custom_call" | custom-call | flops 1073741824 | bytes 1048576 | tf_op jit(solution)/shard_map/pallas_call | solution.py:78
  14.4 0.0 copy-start.12
  14.4 0.0 copy-start.13
  14.4 0.0 copy-start.14
  14.4 2.4 %collective-permute-start.8 = (f32[2,128,512]{2,1,0:T(8,128)S(1)}, f32[2,128,512]{2,1,0:T(8,128)S(1)}, u32[]{:S(2)}, u32[]{:S(2)}) collective-permute-start(f32[2,128,512]{2,1,0:T(8,128)S(1)} %collective-permute-done.7.refs_2_), channel_id=1, source_target_pairs={{0,1},{1,0},{2,3},{3,2},{4,5},{5,4},{6,7},{7,6},{8,9},{9,8},{10,11... | collective-permute-start | bytes 1572872 | tf_op jit(solution)/shard_map/ppermute | solution.py:134
  16.9 0.7 %shard_map.157 = (f32[512,128]{1,0:T(8,128)S(1)}, f32[512,128]{1,0:T(8,128)S(1)}) custom-call(f32[1024,128]{1,0:T(8,128)S(1)} %shard_map.155.pre_ref, f32[40,128]{1,0:T(8,128)S(1)} %collective-permute-done.low_ref.high_ref, f32[40,128]{1,0:T(8,128)S(1)} %collective-permute-done.low_ref.high_ref, f32[272,128]{1,0:T(8,128)S(1)} %collective-permute-done.1.a_ref.rim_a_ref, ...), custom_call_target="tpu_custom_call" | custom-call | flops 536870912 | bytes 1048576 | tf_op jit(solution)/shard_map/pallas_call | solution.py:78
  17.5 0.3 collective-permute-start.10
  17.9 1.2 %collective-permute-start.4 = (f32[512,128]{1,0:T(8,128)S(1)}, f32[512,128]{1,0:T(8,128)S(1)}, u32[]{:S(2)}, u32[]{:S(2)}) collective-permute-start(f32[512,128]{1,0:T(8,128)S(1)} %get-tuple-element.24.refs_0_), channel_id=1, source_target_pairs={{0,2},{1,3},{2,0},{3,1},{4,6},{5,7},{6,4},{7,5},{8,10},{9,11},{10,... | collective-permute-start | bytes 786440 | tf_op jit(solution)/shard_map/ppermute | solution.py:134
  19.1 0.6 collective-permute-start.9
  19.7 5.8 %collective-permute-done.10.refs_2_ = f32[512,128]{1,0:T(8,128)S(1)} collective-permute-done((f32[512,128]{1,0:T(8,128)S(1)}, f32[512,128]{1,0:T(8,128)S(1)}, u32[]{:S(2)}, u32[]{:S(2)}) %collective-permute-start.10) | collective-permute-done | bytes 262176 | tf_op jit(solution)/shard_map/ppermute | solution.py:134
  25.4 1.4 %collective-permute-start.11 = (f32[512,128]{1,0:T(8,128)S(1)}, f32[512,128]{1,0:T(8,128)S(1)}, u32[]{:S(2)}, u32[]{:S(2)}) collective-permute-start(f32[512,128]{1,0:T(8,128)S(1)} %collective-permute-done.10.refs_2_), channel_id=1, source_target_pairs={{0,1},{1,0},{2,3},{3,2},{4,5},{5,4},{6,7},{7,6},{8,9},{9,8},{10,11... | collective-permute-start | bytes 786440 | tf_op jit(solution)/shard_map/ppermute | solution.py:134
  26.8 4.2 %collective-permute-done.4.refs_2_ = f32[512,128]{1,0:T(8,128)S(1)} collective-permute-done((f32[512,128]{1,0:T(8,128)S(1)}, f32[512,128]{1,0:T(8,128)S(1)}, u32[]{:S(2)}, u32[]{:S(2)}) %collective-permute-start.4) | collective-permute-done | bytes 262176 | tf_op jit(solution)/shard_map/ppermute | solution.py:134
  31.0 0.9 %collective-permute-start.3 = (f32[512,128]{1,0:T(8,128)S(1)}, f32[512,128]{1,0:T(8,128)S(1)}, u32[]{:S(2)}, u32[]{:S(2)}) collective-permute-start(f32[512,128]{1,0:T(8,128)S(1)} %get-tuple-element.24.refs_0_), channel_id=1, source_target_pairs={{0,1},{1,0},{2,3},{3,2},{4,5},{5,4},{6,7},{7,6},{8,9},{9,8},{10,11... | collective-permute-start | bytes 786440 | tf_op jit(solution)/shard_map/ppermute | solution.py:134
  31.9 0.0 collective-permute-start.5
  31.9 0.4 shard_map.158
  32.4 1.3 %shard_map.160.second_ref = bf16[512,1024]{1,0:T(8,128)(2,1)S(1)} custom-call(f32[512,128]{1,0:T(8,128)S(1)} %get-tuple-element.26.refs_0_, f32[512,128]{1,0:T(8,128)S(1)} %collective-permute-done.9.refs_1_, f32[512,128]{1,0:T(8,128)S(1)} %collective-permute-done.10.refs_2_, f32[512,128]{1,0:T(8,128)S(1)} %collective-permute-done.11.refs_3_, ...), custom_call_target="tpu_custom_call" | custom-call | flops 1073741824 | bytes 1048576 | tf_op jit(solution)/shard_map/pallas_call | solution.py:78
  33.7 0.0 copy-start.1
  33.7 1.3 %shard_map.159.first_ref = bf16[512,1024]{1,0:T(8,128)(2,1)S(1)} custom-call(f32[512,128]{1,0:T(8,128)S(1)} %get-tuple-element.24.refs_0_, f32[512,128]{1,0:T(8,128)S(1)} %collective-permute-done.3.refs_1_, f32[512,128]{1,0:T(8,128)S(1)} %collective-permute-done.4.refs_2_, f32[512,128]{1,0:T(8,128)S(1)} %collective-permute-done.5.refs_3_, ...), custom_call_target="tpu_custom_call" | custom-call | flops 1073741824 | bytes 1048576 | tf_op jit(solution)/shard_map/pallas_call | solution.py:78
  35.1 2.3 %shard_map.161 = (f32[512,512]{1,0:T(8,128)S(1)}, f32[512,128]{1,0:T(8,128)S(1)}) custom-call(bf16[512,1024]{1,0:T(8,128)(2,1)S(1)} %shard_map.159.first_ref, bf16[512,1024]{1,0:T(8,128)(2,1)S(1)} %shard_map.160.second_ref, s32[1,1024]{1,0:T(1,128)S(1)} %bitcast.22, f32[512,512]{1,0:T(8,128)S(1)} %bitcast.17, f32[2,512,128]{2,1,0:T(8,128)S(1)} %copy-done.1), custom_call_target="tpu_custom_call" | custom-call | flops 1073741824 | bytes 1048576 | tf_op jit(solution)/shard_map/pallas_call | solution.py:78
  37.5 0.1 collective-permute-start.12
  37.5 2.4 %collective-permute-start.13 = (f32[512,128]{1,0:T(8,128)S(1)}, f32[512,128]{1,0:T(8,128)S(1)}, u32[]{:S(2)}, u32[]{:S(2)}) collective-permute-start(f32[512,128]{1,0:T(8,128)S(1)} %get-tuple-element.27.term_ref), channel_id=1, source_target_pairs={{9,17},{11,19},{13,21},{15,23},{17,9},{19,11},{21,13},{23,15}} | collective-permute-start | bytes 786440 | tf_op jit(solution)/shard_map/ppermute | solution.py:126
  39.9 2.1 %shard_map.162 = (f32[512,128]{1,0:T(8,128)S(1)}, f32[512,128]{1,0:T(8,128)S(1)}, f32[512,128]{1,0:T(8,128)S(1)}) custom-call(f32[512,128]{1,0:T(8,128)S(1)} %get-tuple-element.27.term_ref, f32[512,512]{1,0:T(8,128)S(1)} %get-tuple-element.28.mid_ref.refs_9_, f32[2,512,128]{2,1,0:T(8,128)S(1)} %copy-done.2, f32[4,512]{1,0:T(4,128)S(1)} %bitcast.13, ...), custom_call_target="tpu_custom_call" | custom-call | flops 536870912 | bytes 1048576 | tf_op jit(solution)/shard_map/pallas_call | solution.py:78
  42.0 1.0 %collective-permute-done.12.table_a_ref = f32[512,128]{1,0:T(8,128)S(1)} collective-permute-done((f32[512,128]{1,0:T(8,128)S(1)}, f32[512,128]{1,0:T(8,128)S(1)}, u32[]{:S(2)}, u32[]{:S(2)}) %collective-permute-start.12) | collective-permute-done | bytes 262176 | tf_op jit(solution)/shard_map/ppermute | solution.py:126
  43.0 1.6 %collective-permute-done.13.table_b_ref = f32[512,128]{1,0:T(8,128)S(1)} collective-permute-done((f32[512,128]{1,0:T(8,128)S(1)}, f32[512,128]{1,0:T(8,128)S(1)}, u32[]{:S(2)}, u32[]{:S(2)}) %collective-permute-start.13) | collective-permute-done | bytes 262176 | tf_op jit(solution)/shard_map/ppermute | solution.py:126
  44.7 0.9 %shard_map.164 = (f32[512,128]{1,0:T(8,128)S(1)}, f32[512,128]{1,0:T(8,128)S(1)}) custom-call(f32[512,128]{1,0:T(8,128)S(1)} %collective-permute-done.12.table_a_ref, f32[512,128]{1,0:T(8,128)S(1)} %collective-permute-done.13.table_b_ref, f32[512,128]{1,0:T(8,128)S(1)} %get-tuple-element.30.first_a, f32[512,128]{1,0:T(8,128)S(1)} %get-tuple-element.31.first_b, ...), custom_call_target="tpu_custom_call" | custom-call | flops 536870912 | bytes 1048576 | tf_op jit(solution)/shard_map/pallas_call | solution.py:78
  45.6 1.3 %collective-permute-start.14 = (f32[512,128]{1,0:T(8,128)S(1)}, f32[512,128]{1,0:T(8,128)S(1)}, u32[]{:S(2)}, u32[]{:S(2)}) collective-permute-start(f32[512,128]{1,0:T(8,128)S(1)} %get-tuple-element.32), channel_id=1, source_target_pairs={{0,8},{1,5},{2,10},{3,7},{4,12},{5,1},{6,14},{7,3},{8,0},{9,13},{1... | collective-permute-start | bytes 786440 | tf_op jit(solution)/shard_map/ppermute | solution.py:126
  46.9 0.7 %collective-permute-start.15 = (f32[512,128]{1,0:T(8,128)S(1)}, f32[512,128]{1,0:T(8,128)S(1)}, u32[]{:S(2)}, u32[]{:S(2)}) collective-permute-start(f32[512,128]{1,0:T(8,128)S(1)} %get-tuple-element.33), channel_id=1, source_target_pairs={{8,16},{10,18},{12,20},{14,22},{16,8},{18,10},{20,12},{22,14}} | collective-permute-start | bytes 786440 | tf_op jit(solution)/shard_map/ppermute | solution.py:126
  47.6 0.6 shard_map.163
  48.1 3.1 %collective-permute-done.14 = f32[512,128]{1,0:T(8,128)S(1)} collective-permute-done((f32[512,128]{1,0:T(8,128)S(1)}, f32[512,128]{1,0:T(8,128)S(1)}, u32[]{:S(2)}, u32[]{:S(2)}) %collective-permute-start.14) | collective-permute-done | bytes 262176 | tf_op jit(solution)/shard_map/ppermute | solution.py:126
  51.2 0.1 add_divide_fusion.refs_0_
  51.3 0.3 collective-permute-start.17
  51.6 2.8 %collective-permute-start.16 = (f32[512,128]{1,0:T(8,128)S(1)}, f32[512,128]{1,0:T(8,128)S(1)}, u32[]{:S(2)}, u32[]{:S(2)}) collective-permute-start(f32[512,128]{1,0:T(8,128)S(1)} %add_divide_fusion.refs_0_), channel_id=1, source_target_pairs={{0,1},{1,0},{2,3},{3,2},{4,5},{5,4},{6,7},{7,6},{8,9},{9,8},{10,11... | collective-permute-start | bytes 786440 | tf_op jit(solution)/shard_map/ppermute | solution.py:134
  54.4 2.2 %collective-permute-done.17.refs_2_ = f32[512,128]{1,0:T(8,128)S(1)} collective-permute-done((f32[512,128]{1,0:T(8,128)S(1)}, f32[512,128]{1,0:T(8,128)S(1)}, u32[]{:S(2)}, u32[]{:S(2)}) %collective-permute-start.17) | collective-permute-done | bytes 262176 | tf_op jit(solution)/shard_map/ppermute | solution.py:134
  56.6 3.7 %collective-permute-start.18 = (f32[512,128]{1,0:T(8,128)S(1)}, f32[512,128]{1,0:T(8,128)S(1)}, u32[]{:S(2)}, u32[]{:S(2)}) collective-permute-start(f32[512,128]{1,0:T(8,128)S(1)} %collective-permute-done.17.refs_2_), channel_id=1, source_target_pairs={{0,1},{1,0},{2,3},{3,2},{4,5},{5,4},{6,7},{7,6},{8,9},{9,8},{10,11... | collective-permute-start | bytes 786440 | tf_op jit(solution)/shard_map/ppermute | solution.py:134
  60.2 1.2 %collective-permute-done.18.refs_3_ = f32[512,128]{1,0:T(8,128)S(1)} collective-permute-done((f32[512,128]{1,0:T(8,128)S(1)}, f32[512,128]{1,0:T(8,128)S(1)}, u32[]{:S(2)}, u32[]{:S(2)}) %collective-permute-start.18) | collective-permute-done | bytes 262176 | tf_op jit(solution)/shard_map/ppermute | solution.py:134
  61.4 2.3 %shard_map.165 = f32[512,128]{1,0:T(8,128)} custom-call(f32[512,128]{1,0:T(8,128)S(1)} %add_divide_fusion.refs_0_, f32[512,128]{1,0:T(8,128)S(1)} %collective-permute-done.16.refs_1_, f32[512,128]{1,0:T(8,128)S(1)} %collective-permute-done.17.refs_2_, f32[512,128]{1,0:T(8,128)S(1)} %collective-permute-done.18.refs_3_, ...), custom_call_target="tpu_custom_call" | custom-call | flops 1073741824 | bytes 1048576 | tf_op jit(solution)/shard_map/pallas_call | solution.py:78
  (34 shorter events, 0.1 us)
Async XLA Ops:
  0.0 5.2 %copy-start = (f32[2,128,512]{2,1,0:T(8,128)S(1)}, f32[2,128,512]{2,1,0:T(8,128)}, u32[]{:S(2)}) copy-start(f32[2,128,512]{2,1,0:T(8,128)} %refs_0_.1) | copy-start | bytes 1572868
  0.0 6.9 %copy-start.3 = (s32[1,1,512]{2,1,0:T(1,128)S(1)}, s32[1,1,512]{2,1,0:T(1,128)}, u32[]{:S(2)}) copy-start(s32[1,1,512]{2,1,0:T(1,128)} %param.22) | copy-start | bytes 6148
  0.0 14.4 %collective-permute-start.7 = (f32[2,128,512]{2,1,0:T(8,128)}, f32[2,128,512]{2,1,0:T(8,128)S(1)}, u32[]{:S(2)}, u32[]{:S(2)}) collective-permute-start(f32[2,128,512]{2,1,0:T(8,128)} %refs_0_.1), channel_id=1, source_target_pairs={{0,2},{1,3},{2,0},{3,1},{4,6},{5,7},{6,4},{7,5},{8,10},{9,11},{10,... | collective-permute-start | bytes 1572872 | tf_op jit(solution)/shard_map/ppermute | solution.py:134
  1.2 10.3 %copy-start.5 = (f32[2,4,128]{2,1,0:T(4,128)S(1)}, f32[2,4,128]{2,1,0:T(4,128)}, u32[]{:S(2)}) copy-start(f32[2,4,128]{2,1,0:T(4,128)} %edge_ref.3) | copy-start | bytes 12292
  1.2 10.3 %copy-start.7 = (f32[2,128]{1,0:T(2,128)S(1)}, f32[2,128]{1,0:T(2,128)}, u32[]{:S(2)}) copy-start(f32[2,128]{1,0:T(2,128)} %bias_ref.3) | copy-start | bytes 3076
  1.2 10.3 %copy-start.9 = (f32[1,1,4,1024]{3,2,1,0:T(4,128)S(1)}, f32[1,1,4,1024]{3,2,1,0:T(4,128)}, u32[]{:S(2)}) copy-start(f32[1,1,4,1024]{3,2,1,0:T(4,128)} %param.18) | copy-start | bytes 49156
  1.2 10.3 %copy-start.10 = (s32[1,1,1024]{2,1,0:T(1,128)S(1)}, s32[1,1,1024]{2,1,0:T(1,128)}, u32[]{:S(2)}) copy-start(s32[1,1,1024]{2,1,0:T(1,128)} %param.19) | copy-start | bytes 12292
  3.9 3.0 %collective-permute-start = (f32[40,128]{1,0:T(8,128)S(1)}, f32[40,128]{1,0:T(8,128)S(1)}, u32[]{:S(2)}, u32[]{:S(2)}) collective-permute-start(f32[40,128]{1,0:T(8,128)S(1)} %get-tuple-element.21), channel_id=1, source_target_pairs={{0,4},{4,0},{1,5},{5,1},{2,6},{6,2},{3,7},{7,3},{8,12},{12,8},{9,1... | collective-permute-start | bytes 61448 | tf_op jit(solution)/shard_map/ppermute | solution.py:95
  5.2 26.7 %collective-permute-start.6 = (f32[2,128,512]{2,1,0:T(8,128)S(1)}, f32[2,128,512]{2,1,0:T(8,128)S(1)}, u32[]{:S(2)}, u32[]{:S(2)}) collective-permute-start(f32[2,128,512]{2,1,0:T(8,128)S(1)} %copy-done), channel_id=1, source_target_pairs={{0,1},{1,0},{2,3},{3,2},{4,5},{5,4},{6,7},{7,6},{8,9},{9,8},{10,11... | collective-permute-start | bytes 1572872 | tf_op jit(solution)/shard_map/ppermute | solution.py:134
  6.9 9.9 %collective-permute-start.1 = (f32[272,128]{1,0:T(8,128)S(1)}, f32[272,128]{1,0:T(8,128)S(1)}, u32[]{:S(2)}, u32[]{:S(2)}) collective-permute-start(f32[272,128]{1,0:T(8,128)S(1)} %get-tuple-element.22), channel_id=1, source_target_pairs={{0,8},{16,24},{8,0},{24,16},{1,9},{17,25},{9,1},{25,17},{2,10},{18... | collective-permute-start | bytes 417800 | tf_op jit(solution)/shard_map/ppermute | solution.py:101
  7.2 9.7 %collective-permute-start.2 = (f32[272,128]{1,0:T(8,128)S(1)}, f32[272,128]{1,0:T(8,128)S(1)}, u32[]{:S(2)}, u32[]{:S(2)}) collective-permute-start(f32[272,128]{1,0:T(8,128)S(1)} %get-tuple-element.23), channel_id=1, source_target_pairs={{8,16},{16,8},{9,17},{17,9},{10,18},{18,10},{11,19},{19,11},{12,20... | collective-permute-start | bytes 417800 | tf_op jit(solution)/shard_map/ppermute | solution.py:101
  11.5 1.3 %copy-start.2 = (f32[2,512,128]{2,1,0:T(8,128)S(1)}, f32[2,512,128]{2,1,0:T(8,128)}, u32[]{:S(2)}) copy-start(f32[2,512,128]{2,1,0:T(8,128)} %weight_ref.5) | copy-start | bytes 1572868
  11.6 1.4 %copy-start.8 = (f32[1,1,512,512]{3,2,1,0:T(8,128)S(1)}, f32[1,1,512,512]{3,2,1,0:T(8,128)}, u32[]{:S(2)}) copy-start(f32[1,1,512,512]{3,2,1,0:T(8,128)} %param.17) | copy-start | bytes 3145732
  11.6 1.4 %copy-start.11 = (s32[1,1,1024]{2,1,0:T(1,128)S(1)}, s32[1,1,1024]{2,1,0:T(1,128)}, u32[]{:S(2)}) copy-start(s32[1,1,1024]{2,1,0:T(1,128)} %param.20) | copy-start | bytes 12292
  14.4 18.0 %copy-start.12 = (f32[2,512]{1,0:T(2,128)S(1)}, f32[2,512]{1,0:T(2,128)}, u32[]{:S(2)}) copy-start(f32[2,512]{1,0:T(2,128)} %refs_5_.5) | copy-start | bytes 12292
  14.4 18.0 %copy-start.13 = (f32[2,512]{1,0:T(2,128)S(1)}, f32[2,512]{1,0:T(2,128)}, u32[]{:S(2)}) copy-start(f32[2,512]{1,0:T(2,128)} %refs_6_.5) | copy-start | bytes 12292
  14.4 18.0 %copy-start.14 = (f32[2,512]{1,0:T(2,128)S(1)}, f32[2,512]{1,0:T(2,128)}, u32[]{:S(2)}) copy-start(f32[2,512]{1,0:T(2,128)} %refs_7_.5) | copy-start | bytes 12292
  14.4 17.5 %collective-permute-start.8 = (f32[2,128,512]{2,1,0:T(8,128)S(1)}, f32[2,128,512]{2,1,0:T(8,128)S(1)}, u32[]{:S(2)}, u32[]{:S(2)}) collective-permute-start(f32[2,128,512]{2,1,0:T(8,128)S(1)} %collective-permute-done.7.refs_2_), channel_id=1, source_target_pairs={{0,1},{1,0},{2,3},{3,2},{4,5},{5,4},{6,7},{7,6},{8,9},{9,8},{10,11... | collective-permute-start | bytes 1572872 | tf_op jit(solution)/shard_map/ppermute | solution.py:134
  17.5 7.9 %collective-permute-start.10 = (f32[512,128]{1,0:T(8,128)S(1)}, f32[512,128]{1,0:T(8,128)S(1)}, u32[]{:S(2)}, u32[]{:S(2)}) collective-permute-start(f32[512,128]{1,0:T(8,128)S(1)} %get-tuple-element.26.refs_0_), channel_id=1, source_target_pairs={{0,2},{1,3},{2,0},{3,1},{4,6},{5,7},{6,4},{7,5},{8,10},{9,11},{10,... | collective-permute-start | bytes 786440 | tf_op jit(solution)/shard_map/ppermute | solution.py:134
  17.9 13.2 %collective-permute-start.4 = (f32[512,128]{1,0:T(8,128)S(1)}, f32[512,128]{1,0:T(8,128)S(1)}, u32[]{:S(2)}, u32[]{:S(2)}) collective-permute-start(f32[512,128]{1,0:T(8,128)S(1)} %get-tuple-element.24.refs_0_), channel_id=1, source_target_pairs={{0,2},{1,3},{2,0},{3,1},{4,6},{5,7},{6,4},{7,5},{8,10},{9,11},{10,... | collective-permute-start | bytes 786440 | tf_op jit(solution)/shard_map/ppermute | solution.py:134
  19.1 13.3 %collective-permute-start.9 = (f32[512,128]{1,0:T(8,128)S(1)}, f32[512,128]{1,0:T(8,128)S(1)}, u32[]{:S(2)}, u32[]{:S(2)}) collective-permute-start(f32[512,128]{1,0:T(8,128)S(1)} %get-tuple-element.26.refs_0_), channel_id=1, source_target_pairs={{0,1},{1,0},{2,3},{3,2},{4,5},{5,4},{6,7},{7,6},{8,9},{9,8},{10,11... | collective-permute-start | bytes 786440 | tf_op jit(solution)/shard_map/ppermute | solution.py:134
  25.4 6.9 %collective-permute-start.11 = (f32[512,128]{1,0:T(8,128)S(1)}, f32[512,128]{1,0:T(8,128)S(1)}, u32[]{:S(2)}, u32[]{:S(2)}) collective-permute-start(f32[512,128]{1,0:T(8,128)S(1)} %collective-permute-done.10.refs_2_), channel_id=1, source_target_pairs={{0,1},{1,0},{2,3},{3,2},{4,5},{5,4},{6,7},{7,6},{8,9},{9,8},{10,11... | collective-permute-start | bytes 786440 | tf_op jit(solution)/shard_map/ppermute | solution.py:134
  31.0 2.7 %collective-permute-start.3 = (f32[512,128]{1,0:T(8,128)S(1)}, f32[512,128]{1,0:T(8,128)S(1)}, u32[]{:S(2)}, u32[]{:S(2)}) collective-permute-start(f32[512,128]{1,0:T(8,128)S(1)} %get-tuple-element.24.refs_0_), channel_id=1, source_target_pairs={{0,1},{1,0},{2,3},{3,2},{4,5},{5,4},{6,7},{7,6},{8,9},{9,8},{10,11... | collective-permute-start | bytes 786440 | tf_op jit(solution)/shard_map/ppermute | solution.py:134
  31.9 1.8 %collective-permute-start.5 = (f32[512,128]{1,0:T(8,128)S(1)}, f32[512,128]{1,0:T(8,128)S(1)}, u32[]{:S(2)}, u32[]{:S(2)}) collective-permute-start(f32[512,128]{1,0:T(8,128)S(1)} %collective-permute-done.4.refs_2_), channel_id=1, source_target_pairs={{0,1},{1,0},{2,3},{3,2},{4,5},{5,4},{6,7},{7,6},{8,9},{9,8},{10,11... | collective-permute-start | bytes 786440 | tf_op jit(solution)/shard_map/ppermute | solution.py:134
  33.7 1.4 %copy-start.1 = (f32[2,512,128]{2,1,0:T(8,128)S(1)}, f32[2,512,128]{2,1,0:T(8,128)}, u32[]{:S(2)}) copy-start(f32[2,512,128]{2,1,0:T(8,128)} %send_ref.1) | copy-start | bytes 1572868
  35.1 4.8 %copy-start.4 = (f32[1,1,4,512]{3,2,1,0:T(4,128)S(1)}, f32[1,1,4,512]{3,2,1,0:T(4,128)}, u32[]{:S(2)}) copy-start(f32[1,1,4,512]{3,2,1,0:T(4,128)} %param.21) | copy-start | bytes 24580
  35.1 4.8 %copy-start.6 = (s32[1,1,512]{2,1,0:T(1,128)S(1)}, s32[1,1,512]{2,1,0:T(1,128)}, u32[]{:S(2)}) copy-start(s32[1,1,512]{2,1,0:T(1,128)} %param.23) | copy-start | bytes 6148
  37.5 5.6 %collective-permute-start.12 = (f32[512,128]{1,0:T(8,128)S(1)}, f32[512,128]{1,0:T(8,128)S(1)}, u32[]{:S(2)}, u32[]{:S(2)}) collective-permute-start(f32[512,128]{1,0:T(8,128)S(1)} %get-tuple-element.27.term_ref), channel_id=1, source_target_pairs={{0,4},{1,9},{2,6},{3,11},{4,0},{5,13},{6,2},{7,15},{8,12},{9,1},{1... | collective-permute-start | bytes 786440 | tf_op jit(solution)/shard_map/ppermute | solution.py:126
  37.5 7.1 %collective-permute-start.13 = (f32[512,128]{1,0:T(8,128)S(1)}, f32[512,128]{1,0:T(8,128)S(1)}, u32[]{:S(2)}, u32[]{:S(2)}) collective-permute-start(f32[512,128]{1,0:T(8,128)S(1)} %get-tuple-element.27.term_ref), channel_id=1, source_target_pairs={{9,17},{11,19},{13,21},{15,23},{17,9},{19,11},{21,13},{23,15}} | collective-permute-start | bytes 786440 | tf_op jit(solution)/shard_map/ppermute | solution.py:126
  45.6 5.6 %collective-permute-start.14 = (f32[512,128]{1,0:T(8,128)S(1)}, f32[512,128]{1,0:T(8,128)S(1)}, u32[]{:S(2)}, u32[]{:S(2)}) collective-permute-start(f32[512,128]{1,0:T(8,128)S(1)} %get-tuple-element.32), channel_id=1, source_target_pairs={{0,8},{1,5},{2,10},{3,7},{4,12},{5,1},{6,14},{7,3},{8,0},{9,13},{1... | collective-permute-start | bytes 786440 | tf_op jit(solution)/shard_map/ppermute | solution.py:126
  46.9 4.3 %collective-permute-start.15 = (f32[512,128]{1,0:T(8,128)S(1)}, f32[512,128]{1,0:T(8,128)S(1)}, u32[]{:S(2)}, u32[]{:S(2)}) collective-permute-start(f32[512,128]{1,0:T(8,128)S(1)} %get-tuple-element.33), channel_id=1, source_target_pairs={{8,16},{10,18},{12,20},{14,22},{16,8},{18,10},{20,12},{22,14}} | collective-permute-start | bytes 786440 | tf_op jit(solution)/shard_map/ppermute | solution.py:126
  51.3 5.3 %collective-permute-start.17 = (f32[512,128]{1,0:T(8,128)S(1)}, f32[512,128]{1,0:T(8,128)S(1)}, u32[]{:S(2)}, u32[]{:S(2)}) collective-permute-start(f32[512,128]{1,0:T(8,128)S(1)} %add_divide_fusion.refs_0_), channel_id=1, source_target_pairs={{0,2},{1,3},{2,0},{3,1},{4,6},{5,7},{6,4},{7,5},{8,10},{9,11},{10,... | collective-permute-start | bytes 786440 | tf_op jit(solution)/shard_map/ppermute | solution.py:134
  51.6 8.6 %collective-permute-start.16 = (f32[512,128]{1,0:T(8,128)S(1)}, f32[512,128]{1,0:T(8,128)S(1)}, u32[]{:S(2)}, u32[]{:S(2)}) collective-permute-start(f32[512,128]{1,0:T(8,128)S(1)} %add_divide_fusion.refs_0_), channel_id=1, source_target_pairs={{0,1},{1,0},{2,3},{3,2},{4,5},{5,4},{6,7},{7,6},{8,9},{9,8},{10,11... | collective-permute-start | bytes 786440 | tf_op jit(solution)/shard_map/ppermute | solution.py:134
  56.6 4.8 %collective-permute-start.18 = (f32[512,128]{1,0:T(8,128)S(1)}, f32[512,128]{1,0:T(8,128)S(1)}, u32[]{:S(2)}, u32[]{:S(2)}) collective-permute-start(f32[512,128]{1,0:T(8,128)S(1)} %collective-permute-done.17.refs_2_), channel_id=1, source_target_pairs={{0,1},{1,0},{2,3},{3,2},{4,5},{5,4},{6,7},{7,6},{8,9},{9,8},{10,11... | collective-permute-start | bytes 786440 | tf_op jit(solution)/shard_map/ppermute | solution.py:134

commit v5 on v4

--- a/solution.py
+++ b/solution.py
@@ -95,35 +95,47 @@
     return lax.ppermute(value, axis, [(i, (i + step) % count) for i in range(count)])
 
 
+def exchange(value, target_of):
+    sizes = [lax.axis_size(axis) for axis in ("lat", "lon", "hid")]
+    places = [
+        (lat, lon, hid) for lat in range(sizes[0]) for lon in range(sizes[1]) for hid in range(sizes[2])
+    ]
+    targets = {place: target_of(*place) for place in places}
+    idle = {place for place, target in targets.items() if target is None}
+    for hop in (1, 2):
+        for lat, lon, hid in sorted(idle):
+            other = (lat, lon, hid ^ hop)
+            if (lat, lon, hid) in idle and other in idle:
+                targets[lat, lon, hid], targets[other] = other, (lat, lon, hid)
+                idle -= {(lat, lon, hid), other}
+    numbers = {place: number for number, place in enumerate(places)}
+    pairs = [(numbers[source], numbers[target]) for source, target in targets.items() if target]
+    return lax.ppermute(value, ("lat", "lon", "hid"), pairs)
+
+
+def lat_partner(lat, first):
+    other = first + ((lat - first) ^ 1)
+    return other if lat >= first and other < lax.axis_size("lat") else None
+
+
 def swap_lat(value, first):
-    count = lax.axis_size("lat")
-    pairs = [(i, i + 1) for i in range(first, count - 1, 2)]
-    return lax.ppermute(value, "lat", pairs + [(high, low) for low, high in pairs])
+    def target(lat, lon, hid):
+        other = lat_partner(lat, first)
+        return None if other is None else (other, lon, hid)
+
+    return exchange(value, target)
 
 
 def by_role(value, lon_parity, lon_step, lat_first):
-    lat_count, lon_count = lax.axis_size("lat"), lax.axis_size("lon")
-    hid_count = lax.axis_size("hid")
-    pairs = []
-    for lat in range(lat_count):
-        for lon in range(lon_count):
-            for hid in range(hid_count):
-                to_lat, to_lon = lat, lon
-                if hid % 2 == lon_parity:
-                    if lon_step is None:
-                        continue
-                    to_lon = (lon + lon_step) % lon_count
-                else:
-                    to_lat = lat_first + ((lat - lat_first) ^ 1)
-                    if lat < lat_first or to_lat >= lat_count:
-                        continue
-                pairs.append(
-                    (
-                        (lat * lon_count + lon) * hid_count + hid,
-                        (to_lat * lon_count + to_lon) * hid_count + hid,
-                    )
-                )
-    return lax.ppermute(value, ("lat", "lon", "hid"), pairs)
+    lon_count = lax.axis_size("lon")
+
+    def target(lat, lon, hid):
+        if hid % 2 == lon_parity:
+            return None if lon_step is None else (lat, (lon + lon_step) % lon_count, hid)
+        other = lat_partner(lat, lat_first)
+        return None if other is None else (other, lon, hid)
+
+    return exchange(value, target)
 
 
 def gather_hid(value):
@@ -236,9 +248,13 @@
         second = jnp.where(odd, second * lon_count, -1 if two_lon else own + 1)
         return [jnp.where(tag == place, node, -1) for place in (own, first, second)]
 
-    def choose_ids(lat_ref, lat_start, lon_ref):
+    def choose_ids(way, lat_ref, lon_ref):
         odd = lax.axis_index("hid") % 2 == 1
-        return jnp.where(odd, ids_in(lon_ref, side_size), ids_in(lat_ref, lat_start))
+        partner = lat_partners()[way]
+        along_lat = jnp.where((partner >= 0) & (partner < lax.axis_size("lat")), 1, 0)
+        valid = jnp.where(odd, 0 if two_lon and way == 1 else 1, along_lat)
+        ids = jnp.where(odd, ids_in(lon_ref, side_size), ids_in(lat_ref, lat_size))
+        return jnp.where(valid == 1, ids, -4 * nodes * lon_count)
 
     def ids_in(ref, start):
         rows_of = [ref[start + row : start + row + 1, :] for row in range(id_rows)]
@@ -354,9 +370,7 @@
             put_ids(ref, lat_size, id_ref)
 
     rim_block = shape(lat_rows, units)
-    rim_a, rim_b = call(
-        rim_body, (rim_block, rim_block), 1 << 20, (terms, side_low, side_high, mesh_ids)
-    )
+    rim_a, rim_b = call(rim_body, (rim_block, rim_block), 1 << 20, (terms, side_low, side_high, mesh_ids))
     rim_a = swap_lat(rim_a, 0)
     rim_b = swap_lat(rim_b, 1)
 
@@ -393,9 +407,11 @@
     weight_block = shape(3 * width, width, dtype=BF16)
     grid_weight, mesh_weight = call(weight_body, (weight_block, weight_block), 1 << 28, out_pieces)
 
-    def grid_message_body(*refs):
+    half_edges = grid_edges // 2
+
+    def half_sum(half, refs, normed_ref):
         hidden_refs = refs[:hid_count]
-        weight_ref, bias_ref, gain_ref, shift_ref, normed_ref = refs[hid_count:]
+        weight_ref, bias_ref, gain_ref, shift_ref, recv_ref = refs[hid_count : hid_count + 5]
 
         def store(start, step, normed):
             high, low = split(normed)
@@ -405,28 +421,34 @@
         normed_chunks(
             hidden_refs, weight_ref, bias_ref[0:1, :], gain_ref[0:1, :], shift_ref[0:1, :], store
         )
-
-    normed_parts = [
-        call(
-            grid_message_body,
-            shape(grid_edges // 2, 2 * width, dtype=BF16),
-            4 * grid_edges * width * width,
-            (*pieces, grid_weight, out_bias, norm_gain, norm_shift),
-        )
-        for pieces in grid_pieces
-    ]
-
-    def grid_sum_body(first_ref, second_ref, recv_ref, mesh_ref, send_ref, mid_ref, term_ref):
-        normed = jnp.concatenate([first_ref[...], second_ref[...]], axis=0)
-        middle = mesh_ref[...] + aggregate(local(recv_ref[...]), nodes, normed)
+        receivers = recv_ref[:, half * half_edges : (half + 1) * half_edges]
+        return aggregate(local(receivers), nodes, normed_ref[...])
+
+    def grid_first_half_body(*refs):
+        mesh_ref, sum_ref, normed_ref = refs[-3:]
+        sum_ref[...] = mesh_ref[...] + half_sum(0, refs, normed_ref)
+
+    def grid_second_half_body(*refs):
+        first_ref, send_ref, mid_ref, term_ref, normed_ref = refs[-5:]
+        middle = first_ref[...] + half_sum(1, refs, normed_ref)
         mid_ref[...] = middle
         term_ref[...] = dot_split(middle, send_ref[1])
 
+    normed_scratch = (pltpu.VMEM((half_edges, 2 * width), BF16),)
+    shared = (grid_weight, out_bias, norm_gain, norm_shift, grid_to)
+    first_sum = call(
+        grid_first_half_body,
+        shape(nodes, width),
+        5 * grid_edges * width * width,
+        (*grid_pieces[0], *shared, mesh_own),
+        normed_scratch,
+    )
     mesh_mid, mesh_terms = call(
-        grid_sum_body,
+        grid_second_half_body,
         (shape(nodes, width), shape(nodes, units)),
-        4 * grid_edges * width * width,
-        (*normed_parts, grid_to, mesh_own, sender_weight),
+        6 * grid_edges * width * width,
+        (*grid_pieces[1], *shared, first_sum, sender_weight),
+        normed_scratch,
     )
 
     back = None if two_lon else -1
@@ -438,8 +460,8 @@
         rim_a_ref, rim_b_ref, low_ref, high_ref, pre_ref, a_ref, b_ref,
     ):
         table = term_ref[...]
-        a_ref[...] = pick(sender_nodes(choose_ids(rim_a_ref, lat_size, high_ref))[0], table)
-        b_ref[...] = pick(sender_nodes(choose_ids(rim_b_ref, lat_size, low_ref))[0], table)
+        a_ref[...] = pick(sender_nodes(choose_ids(0, rim_a_ref, high_ref))[0], table)
+        b_ref[...] = pick(sender_nodes(choose_ids(1, rim_b_ref, low_ref))[0], table)
         received = dot_split(mid_ref[...], weight_ref[1])
         pre_ref[...] = (
             pick(sender_nodes(id_ref[...])[0], table)
@@ -469,8 +491,8 @@
         table_a_ref, table_b_ref, first_a, first_b, rim_a_ref, rim_b_ref, low_ref, high_ref, a_ref, b_ref
     ):
         tables = (table_a_ref, table_b_ref)
-        a_ref[...] = add_others(first_a, choose_ids(rim_a_ref, lat_size, high_ref), tables)
-        b_ref[...] = add_others(first_b, choose_ids(rim_b_ref, lat_size, low_ref), tables)
+        a_ref[...] = add_others(first_a, choose_ids(0, rim_a_ref, high_ref), tables)
+        b_ref[...] = add_others(first_b, choose_ids(1, rim_b_ref, low_ref), tables)
 
     send_a, send_b = call(
         mesh_sent_body,
@@ -484,12 +506,7 @@
     def mesh_own_body(table_a_ref, table_b_ref, first_ref, id_ref, out_ref):
         out_ref[...] = add_others(first_ref, id_ref[...], (table_a_ref, table_b_ref))
 
-    mesh_pre = call(
-        mesh_own_body,
-        edge_block,
-        8 * mesh_edges * nodes * units,
-        (table_a, table_b, mesh_pre, mesh_ids),
-    )
+    mesh_pre = call(mesh_own_body, edge_block, 8 * mesh_edges * nodes * units, (table_a, table_b, mesh_pre, mesh_ids))
     total = mesh_pre + got_a + got_b
     mesh_pieces = gather_hid(total / (1.0 + jnp.exp(-total)))
     share = width // hid_count

time: 63.8 us -> 61.8 us (0.969)
  starting transfers between devices: 26.3 us -> 23.3 us
  waiting for transfers between devices: 19.5 us -> 20.8 us
    ppermute x12, starting transfers between devices: 16.1 us -> 14.6 us  [gather_hid(): lax.ppermute(source, 'hid', [(i, i ^ hop) for i in range(count)])]
    ppermute x6, starting transfers between devices: 8.94 us -> 7.46 us  [exchange(): return lax.ppermute(value, ('lat', 'lon', 'hid'), pairs)]
    ppermute x12, waiting for transfers between devices: 13.3 us -> 14.7 us  [gather_hid(): lax.ppermute(source, 'hid', [(i, i ^ hop) for i in range(count)])]
    pallas_call x12 -> x11, Pallas kernels: 14.5 us -> 14.1 us  [call(): pl.pallas_call(body, out_shape=outs, in_specs=[VMEM] * len(args), out_spe...]
  transfers between devices with their start and end apart: 19 -> 19, of which waited for: 8 -> 10; matrix products, arithmetic and copies ran while one was open for 0% -> 0% of each run, Pallas kernels for 16% -> 18%
where the time goes in v5:
time: 61.8 us; the launch traced here: 61.5 us
  starting transfers between devices  23.3 us (38%)
  waiting for transfers between devices  20.8 us (34%)
  Pallas kernels  16.8 us (27%)
    ppermute x12, waiting for transfers between devices, gather_hid(): lax.ppermute(source, 'hid', [(i, i ^ hop) for i in range(count)])  14.7 us
    ppermute x12, starting transfers between devices, gather_hid(): lax.ppermute(source, 'hid', [(i, i ^ hop) for i in range(count)])  14.6 us
    pallas_call x11, Pallas kernels, call(): pl.pallas_call(body, out_shape=outs, in_specs=[VMEM] * len(args), out_spe...  14.1 us
    ppermute x6, starting transfers between devices, exchange(): return lax.ppermute(value, ('lat', 'lon', 'hid'), pairs)  7.46 us
    ppermute x6, waiting for transfers between devices, exchange(): return lax.ppermute(value, ('lat', 'lon', 'hid'), pairs)  5.67 us
    pallas_call x1, Pallas kernels, per_device(): pl.pallas_call(terms_body, out_shape=(shape(rows * cols, units), shape(si...  2.68 us
    ppermute x1, starting transfers between devices, shift(): lax.ppermute(value, axis, [(i, (i + step) % count) for i in range(count)])  1.31 us
  transfers between devices with their start and end apart: 19, of which 10 were waited for; matrix products, arithmetic and copies ran while one was open for 0% of the time, Pallas kernels for 18%

profile of v5, /device:TPU:9, one launch (start us, length us, event | category | flops | bytes accessed | tf_op | source)
XLA Modules:
  0.0 61.5 jit_solution(10888129250316937314)
XLA Ops:
  0.0 1.2 %collective-permute-start.7 = (f32[2,128,512]{2,1,0:T(8,128)}, f32[2,128,512]{2,1,0:T(8,128)S(1)}, u32[]{:S(2)}, u32[]{:S(2)}) collective-permute-start(f32[2,128,512]{2,1,0:T(8,128)} %refs_0_.1), channel_id=1, source_target_pairs={{0,2},{1,3},{2,0},{3,1},{4,6},{5,7},{6,4},{7,5},{8,10},{9,11},{10,... | collective-permute-start | bytes 1572872 | tf_op jit(solution)/shard_map/ppermute | solution.py:146
  1.2 2.7 %grid_terms.1 = (f32[1024,128]{1,0:T(8,128)S(1)}, f32[40,128]{1,0:T(8,128)S(1)}) custom-call(f32[1024,512]{1,0:T(8,128)} %bitcast.24, f32[2,512,128]{2,1,0:T(8,128)} %refs_10_.1, s32[1,512]{1,0:T(1,128)} %bitcast.9), custom_call_target="tpu_custom_call" | custom-call | flops 402653184 | bytes 2097152 | tf_op jit(solution)/shard_map/grid_terms/pallas_call | solution.py:312
  3.9 1.3 %collective-permute-start = (f32[40,128]{1,0:T(8,128)S(1)}, f32[40,128]{1,0:T(8,128)S(1)}, u32[]{:S(2)}, u32[]{:S(2)}) collective-permute-start(f32[40,128]{1,0:T(8,128)S(1)} %get-tuple-element.21), channel_id=1, source_target_pairs={{0,4},{4,0},{1,5},{5,1},{2,6},{6,2},{3,7},{7,3},{8,12},{12,8},{9,1... | collective-permute-start | bytes 61448 | tf_op jit(solution)/shard_map/ppermute | solution.py:95
  5.2 1.2 %collective-permute-start.6 = (f32[2,128,512]{2,1,0:T(8,128)S(1)}, f32[2,128,512]{2,1,0:T(8,128)S(1)}, u32[]{:S(2)}, u32[]{:S(2)}) collective-permute-start(f32[2,128,512]{2,1,0:T(8,128)S(1)} %copy-done), channel_id=1, source_target_pairs={{0,1},{1,0},{2,3},{3,2},{4,5},{5,4},{6,7},{7,6},{8,9},{9,8},{10,11... | collective-permute-start | bytes 1572872 | tf_op jit(solution)/shard_map/ppermute | solution.py:146
  6.5 0.4 collective-permute-done.low_ref.high_ref
  6.9 0.2 collective-permute-start.1
  7.2 2.4 %collective-permute-start.2 = (f32[272,128]{1,0:T(8,128)S(1)}, f32[272,128]{1,0:T(8,128)S(1)}, u32[]{:S(2)}, u32[]{:S(2)}) collective-permute-start(f32[272,128]{1,0:T(8,128)S(1)} %get-tuple-element.23), channel_id=1, source_target_pairs={{0,1},{1,0},{2,3},{3,2},{4,5},{5,4},{6,7},{7,6},{8,16},{9,17},{10,... | collective-permute-start | bytes 417800 | tf_op jit(solution)/shard_map/ppermute | solution.py:113
  9.6 0.0 copy-start.2
  9.6 0.0 copy-start.8
  9.6 0.0 copy-start.11
  9.7 1.2 %shard_map.154.pre_ref = f32[1024,128]{1,0:T(8,128)S(1)} custom-call(f32[1024,128]{1,0:T(8,128)S(1)} %get-tuple-element.20.term_ref, f32[4,1024]{1,0:T(4,128)S(1)} %bitcast.18, f32[2,4,128]{2,1,0:T(4,128)S(1)} %copy-done.5, f32[2,128]{1,0:T(2,128)S(1)} %copy-done.7, s32[1,1024]{1,0:T(1,128)S(1)} %bitcast.19), custom_call_target="tpu_custom_call" | custom-call | flops 1073741824 | bytes 1048576 | tf_op jit(solution)/shard_map/pallas_call | solution.py:78
  10.9 0.1 copy-done.8
  11.0 1.4 %shard_map.155.pre_ref = f32[1024,128]{1,0:T(8,128)S(1)} custom-call(f32[1024,128]{1,0:T(8,128)S(1)} %shard_map.154.pre_ref, f32[512,512]{1,0:T(8,128)S(1)} %bitcast.16, f32[2,512,128]{2,1,0:T(8,128)S(1)} %copy-done.2, s32[1,1024]{1,0:T(1,128)S(1)} %bitcast.21), custom_call_target="tpu_custom_call" | custom-call | flops 1073741824 | bytes 1048576 | tf_op jit(solution)/shard_map/pallas_call | solution.py:78
  12.4 0.0 copy-start.12
  12.5 0.0 copy-start.13
  12.5 0.0 copy-start.14
  12.5 0.5 collective-permute-done.7.refs_2_
  13.0 1.9 %collective-permute-start.8 = (f32[2,128,512]{2,1,0:T(8,128)S(1)}, f32[2,128,512]{2,1,0:T(8,128)S(1)}, u32[]{:S(2)}, u32[]{:S(2)}) collective-permute-start(f32[2,128,512]{2,1,0:T(8,128)S(1)} %collective-permute-done.7.refs_2_), channel_id=1, source_target_pairs={{0,1},{1,0},{2,3},{3,2},{4,5},{5,4},{6,7},{7,6},{8,9},{9,8},{10,11... | collective-permute-start | bytes 1572872 | tf_op jit(solution)/shard_map/ppermute | solution.py:146
  14.9 0.7 %shard_map.157 = (f32[512,128]{1,0:T(8,128)S(1)}, f32[512,128]{1,0:T(8,128)S(1)}) custom-call(f32[1024,128]{1,0:T(8,128)S(1)} %shard_map.155.pre_ref, f32[40,128]{1,0:T(8,128)S(1)} %collective-permute-done.low_ref.high_ref, f32[40,128]{1,0:T(8,128)S(1)} %collective-permute-done.low_ref.high_ref, f32[272,128]{1,0:T(8,128)S(1)} %collective-permute-done.1.a_ref.rim_a_ref, ...), custom_call_target="tpu_custom_call" | custom-call | flops 536870912 | bytes 1048576 | tf_op jit(solution)/shard_map/pallas_call | solution.py:78
  15.6 0.9 %collective-permute-start.10 = (f32[512,128]{1,0:T(8,128)S(1)}, f32[512,128]{1,0:T(8,128)S(1)}, u32[]{:S(2)}, u32[]{:S(2)}) collective-permute-start(f32[512,128]{1,0:T(8,128)S(1)} %get-tuple-element.26.refs_0_), channel_id=1, source_target_pairs={{0,2},{1,3},{2,0},{3,1},{4,6},{5,7},{6,4},{7,5},{8,10},{9,11},{10,... | collective-permute-start | bytes 786440 | tf_op jit(solution)/shard_map/ppermute | solution.py:146
  16.5 0.6 %collective-permute-start.4 = (f32[512,128]{1,0:T(8,128)S(1)}, f32[512,128]{1,0:T(8,128)S(1)}, u32[]{:S(2)}, u32[]{:S(2)}) collective-permute-start(f32[512,128]{1,0:T(8,128)S(1)} %get-tuple-element.24.refs_0_), channel_id=1, source_target_pairs={{0,2},{1,3},{2,0},{3,1},{4,6},{5,7},{6,4},{7,5},{8,10},{9,11},{10,... | collective-permute-start | bytes 786440 | tf_op jit(solution)/shard_map/ppermute | solution.py:146
  17.1 0.6 %collective-permute-start.9 = (f32[512,128]{1,0:T(8,128)S(1)}, f32[512,128]{1,0:T(8,128)S(1)}, u32[]{:S(2)}, u32[]{:S(2)}) collective-permute-start(f32[512,128]{1,0:T(8,128)S(1)} %get-tuple-element.26.refs_0_), channel_id=1, source_target_pairs={{0,1},{1,0},{2,3},{3,2},{4,5},{5,4},{6,7},{7,6},{8,9},{9,8},{10,11... | collective-permute-start | bytes 786440 | tf_op jit(solution)/shard_map/ppermute | solution.py:146
  17.8 5.7 %collective-permute-done.10.refs_2_ = f32[512,128]{1,0:T(8,128)S(1)} collective-permute-done((f32[512,128]{1,0:T(8,128)S(1)}, f32[512,128]{1,0:T(8,128)S(1)}, u32[]{:S(2)}, u32[]{:S(2)}) %collective-permute-start.10) | collective-permute-done | bytes 262176 | tf_op jit(solution)/shard_map/ppermute | solution.py:146
  23.5 1.5 %collective-permute-start.11 = (f32[512,128]{1,0:T(8,128)S(1)}, f32[512,128]{1,0:T(8,128)S(1)}, u32[]{:S(2)}, u32[]{:S(2)}) collective-permute-start(f32[512,128]{1,0:T(8,128)S(1)} %collective-permute-done.10.refs_2_), channel_id=1, source_target_pairs={{0,1},{1,0},{2,3},{3,2},{4,5},{5,4},{6,7},{7,6},{8,9},{9,8},{10,11... | collective-permute-start | bytes 786440 | tf_op jit(solution)/shard_map/ppermute | solution.py:146
  24.9 4.2 %collective-permute-done.4.refs_2_ = f32[512,128]{1,0:T(8,128)S(1)} collective-permute-done((f32[512,128]{1,0:T(8,128)S(1)}, f32[512,128]{1,0:T(8,128)S(1)}, u32[]{:S(2)}, u32[]{:S(2)}) %collective-permute-start.4) | collective-permute-done | bytes 262176 | tf_op jit(solution)/shard_map/ppermute | solution.py:146
  29.1 0.9 %collective-permute-start.3 = (f32[512,128]{1,0:T(8,128)S(1)}, f32[512,128]{1,0:T(8,128)S(1)}, u32[]{:S(2)}, u32[]{:S(2)}) collective-permute-start(f32[512,128]{1,0:T(8,128)S(1)} %get-tuple-element.24.refs_0_), channel_id=1, source_target_pairs={{0,1},{1,0},{2,3},{3,2},{4,5},{5,4},{6,7},{7,6},{8,9},{9,8},{10,11... | collective-permute-start | bytes 786440 | tf_op jit(solution)/shard_map/ppermute | solution.py:146
  30.0 0.0 collective-permute-start.5
  30.0 0.3 shard_map.158
  30.4 1.8 %shard_map.159.refs_9_ = f32[512,512]{1,0:T(8,128)S(1)} custom-call(f32[512,128]{1,0:T(8,128)S(1)} %get-tuple-element.26.refs_0_, f32[512,128]{1,0:T(8,128)S(1)} %collective-permute-done.9.refs_1_, f32[512,128]{1,0:T(8,128)S(1)} %collective-permute-done.10.refs_2_, f32[512,128]{1,0:T(8,128)S(1)} %collective-permute-done.11.refs_3_, ...), custom_call_target="tpu_custom_call" | custom-call | flops 1342177280 | bytes 1048576 | tf_op jit(solution)/shard_map/pallas_call | solution.py:78
  32.3 2.9 %shard_map.160 = (f32[512,512]{1,0:T(8,128)S(1)}, f32[512,128]{1,0:T(8,128)S(1)}) custom-call(f32[512,128]{1,0:T(8,128)S(1)} %get-tuple-element.24.refs_0_, f32[512,128]{1,0:T(8,128)S(1)} %collective-permute-done.3.refs_1_, f32[512,128]{1,0:T(8,128)S(1)} %collective-permute-done.4.refs_2_, f32[512,128]{1,0:T(8,128)S(1)} %collective-permute-done.5.refs_3_, ...), custom_call_target="tpu_custom_call" | custom-call | flops 1610612736 | bytes 1048576 | tf_op jit(solution)/shard_map/pallas_call | solution.py:78
  35.1 0.1 collective-permute-start.12
  35.2 2.2 %collective-permute-start.13 = (f32[512,128]{1,0:T(8,128)S(1)}, f32[512,128]{1,0:T(8,128)S(1)}, u32[]{:S(2)}, u32[]{:S(2)}) collective-permute-start(f32[512,128]{1,0:T(8,128)S(1)} %get-tuple-element.27.term_ref), channel_id=1, source_target_pairs={{0,1},{1,0},{2,3},{3,2},{4,5},{5,4},{6,7},{7,6},{8,10},{9,17},{10,... | collective-permute-start | bytes 786440 | tf_op jit(solution)/shard_map/ppermute | solution.py:113
  37.4 2.1 %shard_map.161 = (f32[512,128]{1,0:T(8,128)S(1)}, f32[512,128]{1,0:T(8,128)S(1)}, f32[512,128]{1,0:T(8,128)S(1)}) custom-call(f32[512,128]{1,0:T(8,128)S(1)} %get-tuple-element.27.term_ref, f32[512,512]{1,0:T(8,128)S(1)} %get-tuple-element.28.mid_ref.refs_9_, f32[2,512,128]{2,1,0:T(8,128)S(1)} %copy-done.2, f32[4,512]{1,0:T(4,128)S(1)} %bitcast.13, ...), custom_call_target="tpu_custom_call" | custom-call | flops 536870912 | bytes 1048576 | tf_op jit(solution)/shard_map/pallas_call | solution.py:78
  39.6 1.2 %collective-permute-done.12.table_a_ref = f32[512,128]{1,0:T(8,128)S(1)} collective-permute-done((f32[512,128]{1,0:T(8,128)S(1)}, f32[512,128]{1,0:T(8,128)S(1)}, u32[]{:S(2)}, u32[]{:S(2)}) %collective-permute-start.12) | collective-permute-done | bytes 262176 | tf_op jit(solution)/shard_map/ppermute | solution.py:113
  40.7 0.8 %collective-permute-done.13.table_b_ref = f32[512,128]{1,0:T(8,128)S(1)} collective-permute-done((f32[512,128]{1,0:T(8,128)S(1)}, f32[512,128]{1,0:T(8,128)S(1)}, u32[]{:S(2)}, u32[]{:S(2)}) %collective-permute-start.13) | collective-permute-done | bytes 262176 | tf_op jit(solution)/shard_map/ppermute | solution.py:113
  41.5 0.9 %shard_map.163 = (f32[512,128]{1,0:T(8,128)S(1)}, f32[512,128]{1,0:T(8,128)S(1)}) custom-call(f32[512,128]{1,0:T(8,128)S(1)} %collective-permute-done.12.table_a_ref, f32[512,128]{1,0:T(8,128)S(1)} %collective-permute-done.13.table_b_ref, f32[512,128]{1,0:T(8,128)S(1)} %get-tuple-element.30.first_a, f32[512,128]{1,0:T(8,128)S(1)} %get-tuple-element.31.first_b, ...), custom_call_target="tpu_custom_call" | custom-call | flops 536870912 | bytes 1048576 | tf_op jit(solution)/shard_map/pallas_call | solution.py:78
  42.4 1.3 %collective-permute-start.14 = (f32[512,128]{1,0:T(8,128)S(1)}, f32[512,128]{1,0:T(8,128)S(1)}, u32[]{:S(2)}, u32[]{:S(2)}) collective-permute-start(f32[512,128]{1,0:T(8,128)S(1)} %get-tuple-element.32), channel_id=1, source_target_pairs={{0,8},{1,5},{2,10},{3,7},{4,12},{5,1},{6,14},{7,3},{8,0},{9,13},{1... | collective-permute-start | bytes 786440 | tf_op jit(solution)/shard_map/ppermute | solution.py:113
  43.7 1.2 %collective-permute-start.15 = (f32[512,128]{1,0:T(8,128)S(1)}, f32[512,128]{1,0:T(8,128)S(1)}, u32[]{:S(2)}, u32[]{:S(2)}) collective-permute-start(f32[512,128]{1,0:T(8,128)S(1)} %get-tuple-element.33), channel_id=1, source_target_pairs={{0,1},{1,0},{2,3},{3,2},{4,5},{5,4},{6,7},{7,6},{8,16},{9,11},{10,... | collective-permute-start | bytes 786440 | tf_op jit(solution)/shard_map/ppermute | solution.py:113
  45.0 0.5 shard_map.162
  45.5 2.5 %collective-permute-done.14 = f32[512,128]{1,0:T(8,128)S(1)} collective-permute-done((f32[512,128]{1,0:T(8,128)S(1)}, f32[512,128]{1,0:T(8,128)S(1)}, u32[]{:S(2)}, u32[]{:S(2)}) %collective-permute-start.14) | collective-permute-done | bytes 262176 | tf_op jit(solution)/shard_map/ppermute | solution.py:113
  48.0 1.2 %collective-permute-done.15 = f32[512,128]{1,0:T(8,128)S(1)} collective-permute-done((f32[512,128]{1,0:T(8,128)S(1)}, f32[512,128]{1,0:T(8,128)S(1)}, u32[]{:S(2)}, u32[]{:S(2)}) %collective-permute-start.15) | collective-permute-done | bytes 262176 | tf_op jit(solution)/shard_map/ppermute | solution.py:113
  49.3 0.1 add_divide_fusion.refs_0_
  49.3 1.3 %collective-permute-start.17 = (f32[512,128]{1,0:T(8,128)S(1)}, f32[512,128]{1,0:T(8,128)S(1)}, u32[]{:S(2)}, u32[]{:S(2)}) collective-permute-start(f32[512,128]{1,0:T(8,128)S(1)} %add_divide_fusion.refs_0_), channel_id=1, source_target_pairs={{0,2},{1,3},{2,0},{3,1},{4,6},{5,7},{6,4},{7,5},{8,10},{9,11},{10,... | collective-permute-start | bytes 786440 | tf_op jit(solution)/shard_map/ppermute | solution.py:146
  50.6 1.7 %collective-permute-start.16 = (f32[512,128]{1,0:T(8,128)S(1)}, f32[512,128]{1,0:T(8,128)S(1)}, u32[]{:S(2)}, u32[]{:S(2)}) collective-permute-start(f32[512,128]{1,0:T(8,128)S(1)} %add_divide_fusion.refs_0_), channel_id=1, source_target_pairs={{0,1},{1,0},{2,3},{3,2},{4,5},{5,4},{6,7},{7,6},{8,9},{9,8},{10,11... | collective-permute-start | bytes 786440 | tf_op jit(solution)/shard_map/ppermute | solution.py:146
  52.3 3.1 %collective-permute-done.17.refs_2_ = f32[512,128]{1,0:T(8,128)S(1)} collective-permute-done((f32[512,128]{1,0:T(8,128)S(1)}, f32[512,128]{1,0:T(8,128)S(1)}, u32[]{:S(2)}, u32[]{:S(2)}) %collective-permute-start.17) | collective-permute-done | bytes 262176 | tf_op jit(solution)/shard_map/ppermute | solution.py:146
  55.5 2.7 %collective-permute-start.18 = (f32[512,128]{1,0:T(8,128)S(1)}, f32[512,128]{1,0:T(8,128)S(1)}, u32[]{:S(2)}, u32[]{:S(2)}) collective-permute-start(f32[512,128]{1,0:T(8,128)S(1)} %collective-permute-done.17.refs_2_), channel_id=1, source_target_pairs={{0,1},{1,0},{2,3},{3,2},{4,5},{5,4},{6,7},{7,6},{8,9},{9,8},{10,11... | collective-permute-start | bytes 786440 | tf_op jit(solution)/shard_map/ppermute | solution.py:146
  58.1 1.2 %collective-permute-done.18.refs_3_ = f32[512,128]{1,0:T(8,128)S(1)} collective-permute-done((f32[512,128]{1,0:T(8,128)S(1)}, f32[512,128]{1,0:T(8,128)S(1)}, u32[]{:S(2)}, u32[]{:S(2)}) %collective-permute-start.18) | collective-permute-done | bytes 262176 | tf_op jit(solution)/shard_map/ppermute | solution.py:146
  59.3 2.2 %shard_map.164 = f32[512,128]{1,0:T(8,128)} custom-call(f32[512,128]{1,0:T(8,128)S(1)} %add_divide_fusion.refs_0_, f32[512,128]{1,0:T(8,128)S(1)} %collective-permute-done.16.refs_1_, f32[512,128]{1,0:T(8,128)S(1)} %collective-permute-done.17.refs_2_, f32[512,128]{1,0:T(8,128)S(1)} %collective-permute-done.18.refs_3_, ...), custom_call_target="tpu_custom_call" | custom-call | flops 1073741824 | bytes 1048576 | tf_op jit(solution)/shard_map/pallas_call | solution.py:78
  (33 shorter events, 0.1 us)
Async XLA Ops:
  0.0 5.2 %copy-start = (f32[2,128,512]{2,1,0:T(8,128)S(1)}, f32[2,128,512]{2,1,0:T(8,128)}, u32[]{:S(2)}) copy-start(f32[2,128,512]{2,1,0:T(8,128)} %refs_0_.1) | copy-start | bytes 1572868
  0.0 6.9 %copy-start.3 = (s32[1,1,512]{2,1,0:T(1,128)S(1)}, s32[1,1,512]{2,1,0:T(1,128)}, u32[]{:S(2)}) copy-start(s32[1,1,512]{2,1,0:T(1,128)} %param.22) | copy-start | bytes 6148
  0.0 13.0 %collective-permute-start.7 = (f32[2,128,512]{2,1,0:T(8,128)}, f32[2,128,512]{2,1,0:T(8,128)S(1)}, u32[]{:S(2)}, u32[]{:S(2)}) collective-permute-start(f32[2,128,512]{2,1,0:T(8,128)} %refs_0_.1), channel_id=1, source_target_pairs={{0,2},{1,3},{2,0},{3,1},{4,6},{5,7},{6,4},{7,5},{8,10},{9,11},{10,... | collective-permute-start | bytes 1572872 | tf_op jit(solution)/shard_map/ppermute | solution.py:146
  1.2 8.4 %copy-start.5 = (f32[2,4,128]{2,1,0:T(4,128)S(1)}, f32[2,4,128]{2,1,0:T(4,128)}, u32[]{:S(2)}) copy-start(f32[2,4,128]{2,1,0:T(4,128)} %edge_ref.3) | copy-start | bytes 12292
  1.2 8.4 %copy-start.7 = (f32[2,128]{1,0:T(2,128)S(1)}, f32[2,128]{1,0:T(2,128)}, u32[]{:S(2)}) copy-start(f32[2,128]{1,0:T(2,128)} %bias_ref.3) | copy-start | bytes 3076
  1.2 8.4 %copy-start.9 = (f32[1,1,4,1024]{3,2,1,0:T(4,128)S(1)}, f32[1,1,4,1024]{3,2,1,0:T(4,128)}, u32[]{:S(2)}) copy-start(f32[1,1,4,1024]{3,2,1,0:T(4,128)} %param.18) | copy-start | bytes 49156
  1.2 8.4 %copy-start.10 = (s32[1,1,1024]{2,1,0:T(1,128)S(1)}, s32[1,1,1024]{2,1,0:T(1,128)}, u32[]{:S(2)}) copy-start(s32[1,1,1024]{2,1,0:T(1,128)} %param.19) | copy-start | bytes 12292
  3.9 3.0 %collective-permute-start = (f32[40,128]{1,0:T(8,128)S(1)}, f32[40,128]{1,0:T(8,128)S(1)}, u32[]{:S(2)}, u32[]{:S(2)}) collective-permute-start(f32[40,128]{1,0:T(8,128)S(1)} %get-tuple-element.21), channel_id=1, source_target_pairs={{0,4},{4,0},{1,5},{5,1},{2,6},{6,2},{3,7},{7,3},{8,12},{12,8},{9,1... | collective-permute-start | bytes 61448 | tf_op jit(solution)/shard_map/ppermute | solution.py:95
  5.2 24.8 %collective-permute-start.6 = (f32[2,128,512]{2,1,0:T(8,128)S(1)}, f32[2,128,512]{2,1,0:T(8,128)S(1)}, u32[]{:S(2)}, u32[]{:S(2)}) collective-permute-start(f32[2,128,512]{2,1,0:T(8,128)S(1)} %copy-done), channel_id=1, source_target_pairs={{0,1},{1,0},{2,3},{3,2},{4,5},{5,4},{6,7},{7,6},{8,9},{9,8},{10,11... | collective-permute-start | bytes 1572872 | tf_op jit(solution)/shard_map/ppermute | solution.py:146
  6.9 8.0 %collective-permute-start.1 = (f32[272,128]{1,0:T(8,128)S(1)}, f32[272,128]{1,0:T(8,128)S(1)}, u32[]{:S(2)}, u32[]{:S(2)}) collective-permute-start(f32[272,128]{1,0:T(8,128)S(1)} %get-tuple-element.22), channel_id=1, source_target_pairs={{0,8},{1,9},{2,10},{3,11},{4,12},{5,13},{6,14},{7,15},{8,0},{9,1},... | collective-permute-start | bytes 417800 | tf_op jit(solution)/shard_map/ppermute | solution.py:113
  7.2 7.7 %collective-permute-start.2 = (f32[272,128]{1,0:T(8,128)S(1)}, f32[272,128]{1,0:T(8,128)S(1)}, u32[]{:S(2)}, u32[]{:S(2)}) collective-permute-start(f32[272,128]{1,0:T(8,128)S(1)} %get-tuple-element.23), channel_id=1, source_target_pairs={{0,1},{1,0},{2,3},{3,2},{4,5},{5,4},{6,7},{7,6},{8,16},{9,17},{10,... | collective-permute-start | bytes 417800 | tf_op jit(solution)/shard_map/ppermute | solution.py:113
  9.6 1.3 %copy-start.2 = (f32[2,512,128]{2,1,0:T(8,128)S(1)}, f32[2,512,128]{2,1,0:T(8,128)}, u32[]{:S(2)}) copy-start(f32[2,512,128]{2,1,0:T(8,128)} %weight_ref.5) | copy-start | bytes 1572868
  9.6 1.4 %copy-start.8 = (f32[1,1,512,512]{3,2,1,0:T(8,128)S(1)}, f32[1,1,512,512]{3,2,1,0:T(8,128)}, u32[]{:S(2)}) copy-start(f32[1,1,512,512]{3,2,1,0:T(8,128)} %param.17) | copy-start | bytes 3145732
  9.6 1.4 %copy-start.11 = (s32[1,1,1024]{2,1,0:T(1,128)S(1)}, s32[1,1,1024]{2,1,0:T(1,128)}, u32[]{:S(2)}) copy-start(s32[1,1,1024]{2,1,0:T(1,128)} %param.20) | copy-start | bytes 12292
  12.4 17.9 %copy-start.12 = (f32[2,512]{1,0:T(2,128)S(1)}, f32[2,512]{1,0:T(2,128)}, u32[]{:S(2)}) copy-start(f32[2,512]{1,0:T(2,128)} %refs_5_.5) | copy-start | bytes 12292
  12.5 17.9 %copy-start.13 = (f32[2,512]{1,0:T(2,128)S(1)}, f32[2,512]{1,0:T(2,128)}, u32[]{:S(2)}) copy-start(f32[2,512]{1,0:T(2,128)} %refs_6_.5) | copy-start | bytes 12292
  12.5 17.9 %copy-start.14 = (f32[2,512]{1,0:T(2,128)S(1)}, f32[2,512]{1,0:T(2,128)}, u32[]{:S(2)}) copy-start(f32[2,512]{1,0:T(2,128)} %refs_7_.5) | copy-start | bytes 12292
  13.0 17.0 %collective-permute-start.8 = (f32[2,128,512]{2,1,0:T(8,128)S(1)}, f32[2,128,512]{2,1,0:T(8,128)S(1)}, u32[]{:S(2)}, u32[]{:S(2)}) collective-permute-start(f32[2,128,512]{2,1,0:T(8,128)S(1)} %collective-permute-done.7.refs_2_), channel_id=1, source_target_pairs={{0,1},{1,0},{2,3},{3,2},{4,5},{5,4},{6,7},{7,6},{8,9},{9,8},{10,11... | collective-permute-start | bytes 1572872 | tf_op jit(solution)/shard_map/ppermute | solution.py:146
  15.6 7.9 %collective-permute-start.10 = (f32[512,128]{1,0:T(8,128)S(1)}, f32[512,128]{1,0:T(8,128)S(1)}, u32[]{:S(2)}, u32[]{:S(2)}) collective-permute-start(f32[512,128]{1,0:T(8,128)S(1)} %get-tuple-element.26.refs_0_), channel_id=1, source_target_pairs={{0,2},{1,3},{2,0},{3,1},{4,6},{5,7},{6,4},{7,5},{8,10},{9,11},{10,... | collective-permute-start | bytes 786440 | tf_op jit(solution)/shard_map/ppermute | solution.py:146
  16.5 12.6 %collective-permute-start.4 = (f32[512,128]{1,0:T(8,128)S(1)}, f32[512,128]{1,0:T(8,128)S(1)}, u32[]{:S(2)}, u32[]{:S(2)}) collective-permute-start(f32[512,128]{1,0:T(8,128)S(1)} %get-tuple-element.24.refs_0_), channel_id=1, source_target_pairs={{0,2},{1,3},{2,0},{3,1},{4,6},{5,7},{6,4},{7,5},{8,10},{9,11},{10,... | collective-permute-start | bytes 786440 | tf_op jit(solution)/shard_map/ppermute | solution.py:146
  17.1 13.2 %collective-permute-start.9 = (f32[512,128]{1,0:T(8,128)S(1)}, f32[512,128]{1,0:T(8,128)S(1)}, u32[]{:S(2)}, u32[]{:S(2)}) collective-permute-start(f32[512,128]{1,0:T(8,128)S(1)} %get-tuple-element.26.refs_0_), channel_id=1, source_target_pairs={{0,1},{1,0},{2,3},{3,2},{4,5},{5,4},{6,7},{7,6},{8,9},{9,8},{10,11... | collective-permute-start | bytes 786440 | tf_op jit(solution)/shard_map/ppermute | solution.py:146
  23.5 6.9 %collective-permute-start.11 = (f32[512,128]{1,0:T(8,128)S(1)}, f32[512,128]{1,0:T(8,128)S(1)}, u32[]{:S(2)}, u32[]{:S(2)}) collective-permute-start(f32[512,128]{1,0:T(8,128)S(1)} %collective-permute-done.10.refs_2_), channel_id=1, source_target_pairs={{0,1},{1,0},{2,3},{3,2},{4,5},{5,4},{6,7},{7,6},{8,9},{9,8},{10,11... | collective-permute-start | bytes 786440 | tf_op jit(solution)/shard_map/ppermute | solution.py:146
  29.1 3.2 %collective-permute-start.3 = (f32[512,128]{1,0:T(8,128)S(1)}, f32[512,128]{1,0:T(8,128)S(1)}, u32[]{:S(2)}, u32[]{:S(2)}) collective-permute-start(f32[512,128]{1,0:T(8,128)S(1)} %get-tuple-element.24.refs_0_), channel_id=1, source_target_pairs={{0,1},{1,0},{2,3},{3,2},{4,5},{5,4},{6,7},{7,6},{8,9},{9,8},{10,11... | collective-permute-start | bytes 786440 | tf_op jit(solution)/shard_map/ppermute | solution.py:146
  30.0 2.3 %collective-permute-start.5 = (f32[512,128]{1,0:T(8,128)S(1)}, f32[512,128]{1,0:T(8,128)S(1)}, u32[]{:S(2)}, u32[]{:S(2)}) collective-permute-start(f32[512,128]{1,0:T(8,128)S(1)} %collective-permute-done.4.refs_2_), channel_id=1, source_target_pairs={{0,1},{1,0},{2,3},{3,2},{4,5},{5,4},{6,7},{7,6},{8,9},{9,8},{10,11... | collective-permute-start | bytes 786440 | tf_op jit(solution)/shard_map/ppermute | solution.py:146
  30.4 1.9 %copy-start.1 = (f32[2,512,128]{2,1,0:T(8,128)S(1)}, f32[2,512,128]{2,1,0:T(8,128)}, u32[]{:S(2)}) copy-start(f32[2,512,128]{2,1,0:T(8,128)} %refs_10_.1) | copy-start | bytes 1572868
  32.2 5.2 %copy-start.4 = (f32[1,1,4,512]{3,2,1,0:T(4,128)S(1)}, f32[1,1,4,512]{3,2,1,0:T(4,128)}, u32[]{:S(2)}) copy-start(f32[1,1,4,512]{3,2,1,0:T(4,128)} %param.21) | copy-start | bytes 24580
  32.2 5.2 %copy-start.6 = (s32[1,1,512]{2,1,0:T(1,128)S(1)}, s32[1,1,512]{2,1,0:T(1,128)}, u32[]{:S(2)}) copy-start(s32[1,1,512]{2,1,0:T(1,128)} %param.23) | copy-start | bytes 6148
  35.1 5.6 %collective-permute-start.12 = (f32[512,128]{1,0:T(8,128)S(1)}, f32[512,128]{1,0:T(8,128)S(1)}, u32[]{:S(2)}, u32[]{:S(2)}) collective-permute-start(f32[512,128]{1,0:T(8,128)S(1)} %get-tuple-element.27.term_ref), channel_id=1, source_target_pairs={{0,4},{1,9},{2,6},{3,11},{4,0},{5,13},{6,2},{7,15},{8,12},{9,1},{1... | collective-permute-start | bytes 786440 | tf_op jit(solution)/shard_map/ppermute | solution.py:113
  35.2 6.3 %collective-permute-start.13 = (f32[512,128]{1,0:T(8,128)S(1)}, f32[512,128]{1,0:T(8,128)S(1)}, u32[]{:S(2)}, u32[]{:S(2)}) collective-permute-start(f32[512,128]{1,0:T(8,128)S(1)} %get-tuple-element.27.term_ref), channel_id=1, source_target_pairs={{0,1},{1,0},{2,3},{3,2},{4,5},{5,4},{6,7},{7,6},{8,10},{9,17},{10,... | collective-permute-start | bytes 786440 | tf_op jit(solution)/shard_map/ppermute | solution.py:113
  42.4 5.6 %collective-permute-start.14 = (f32[512,128]{1,0:T(8,128)S(1)}, f32[512,128]{1,0:T(8,128)S(1)}, u32[]{:S(2)}, u32[]{:S(2)}) collective-permute-start(f32[512,128]{1,0:T(8,128)S(1)} %get-tuple-element.32), channel_id=1, source_target_pairs={{0,8},{1,5},{2,10},{3,7},{4,12},{5,1},{6,14},{7,3},{8,0},{9,13},{1... | collective-permute-start | bytes 786440 | tf_op jit(solution)/shard_map/ppermute | solution.py:113
  43.7 5.5 %collective-permute-start.15 = (f32[512,128]{1,0:T(8,128)S(1)}, f32[512,128]{1,0:T(8,128)S(1)}, u32[]{:S(2)}, u32[]{:S(2)}) collective-permute-start(f32[512,128]{1,0:T(8,128)S(1)} %get-tuple-element.33), channel_id=1, source_target_pairs={{0,1},{1,0},{2,3},{3,2},{4,5},{5,4},{6,7},{7,6},{8,16},{9,11},{10,... | collective-permute-start | bytes 786440 | tf_op jit(solution)/shard_map/ppermute | solution.py:113
  49.3 6.1 %collective-permute-start.17 = (f32[512,128]{1,0:T(8,128)S(1)}, f32[512,128]{1,0:T(8,128)S(1)}, u32[]{:S(2)}, u32[]{:S(2)}) collective-permute-start(f32[512,128]{1,0:T(8,128)S(1)} %add_divide_fusion.refs_0_), channel_id=1, source_target_pairs={{0,2},{1,3},{2,0},{3,1},{4,6},{5,7},{6,4},{7,5},{8,10},{9,11},{10,... | collective-permute-start | bytes 786440 | tf_op jit(solution)/shard_map/ppermute | solution.py:146
  50.6 7.5 %collective-permute-start.16 = (f32[512,128]{1,0:T(8,128)S(1)}, f32[512,128]{1,0:T(8,128)S(1)}, u32[]{:S(2)}, u32[]{:S(2)}) collective-permute-start(f32[512,128]{1,0:T(8,128)S(1)} %add_divide_fusion.refs_0_), channel_id=1, source_target_pairs={{0,1},{1,0},{2,3},{3,2},{4,5},{5,4},{6,7},{7,6},{8,9},{9,8},{10,11... | collective-permute-start | bytes 786440 | tf_op jit(solution)/shard_map/ppermute | solution.py:146
  55.5 3.8 %collective-permute-start.18 = (f32[512,128]{1,0:T(8,128)S(1)}, f32[512,128]{1,0:T(8,128)S(1)}, u32[]{:S(2)}, u32[]{:S(2)}) collective-permute-start(f32[512,128]{1,0:T(8,128)S(1)} %collective-permute-done.17.refs_2_), channel_id=1, source_target_pairs={{0,1},{1,0},{2,3},{3,2},{4,5},{5,4},{6,7},{7,6},{8,9},{9,8},{10,11... | collective-permute-start | bytes 786440 | tf_op jit(solution)/shard_map/ppermute | solution.py:146

commit v6 on v5

--- a/solution.py
+++ b/solution.py
@@ -46,13 +46,15 @@
     return jnp.concatenate(blocks, axis=1)
 
 
-def pick(index_row, table):
+def pick_hot(onehot, table):
     width = table.shape[1]
     high, low = split(table)
-    both = dot(
-        onehot_rows(down_lanes(index_row), table.shape[0]), jnp.concatenate([high, low], axis=1)
-    )
+    both = dot(onehot, jnp.concatenate([high, low], axis=1))
     return both[:, :width] + both[:, width:]
+
+
+def pick(index_row, table):
+    return pick_hot(onehot_rows(down_lanes(index_row), table.shape[0]), table)
 
 
 def edge_terms(feats, weight):
@@ -246,7 +248,8 @@
         first, second = lat_partners()
         first = jnp.where(odd, first * lon_count, own + (1 if two_lon else lon_count - 1))
         second = jnp.where(odd, second * lon_count, -1 if two_lon else own + 1)
-        return [jnp.where(tag == place, node, -1) for place in (own, first, second)]
+        received = jnp.where(tag == first, node, jnp.where(tag == second, node + nodes, -1))
+        return jnp.where(tag == own, node, -1), received
 
     def choose_ids(way, lat_ref, lon_ref):
         odd = lax.axis_index("hid") % 2 == 1
@@ -457,11 +460,15 @@
 
     def mesh_first_body(
         term_ref, mid_ref, weight_ref, feat_ref, edge_ref, bias_ref, recv_ref, id_ref,
-        rim_a_ref, rim_b_ref, low_ref, high_ref, pre_ref, a_ref, b_ref,
+        rim_a_ref, rim_b_ref, low_ref, high_ref, pre_ref, a_ref, b_ref, hot_ref,
     ):
         table = term_ref[...]
-        a_ref[...] = pick(sender_nodes(choose_ids(0, rim_a_ref, high_ref))[0], table)
-        b_ref[...] = pick(sender_nodes(choose_ids(1, rim_b_ref, low_ref))[0], table)
+        own_a, received_a = sender_nodes(choose_ids(0, rim_a_ref, high_ref))
+        own_b, received_b = sender_nodes(choose_ids(1, rim_b_ref, low_ref))
+        a_ref[...] = pick(own_a, table)
+        b_ref[...] = pick(own_b, table)
+        hot_ref[:mesh_edges, :] = onehot_rows(down_lanes(received_a), 2 * nodes)
+        hot_ref[mesh_edges:, :] = onehot_rows(down_lanes(received_b), 2 * nodes)
         received = dot_split(mid_ref[...], weight_ref[1])
         pre_ref[...] = (
             pick(sender_nodes(id_ref[...])[0], table)
@@ -471,9 +478,9 @@
         )
 
     edge_block = shape(mesh_edges, units)
-    mesh_pre, send_a, send_b = call(
+    mesh_pre, send_a, send_b, sent_hot = call(
         mesh_first_body,
-        (edge_block, edge_block, edge_block),
+        (edge_block, edge_block, edge_block, shape(2 * mesh_edges, 2 * nodes, dtype=BF16)),
         16 * mesh_edges * nodes * units,
         (
             mesh_terms, mesh_mid, receiver_weight, mesh_edge_feats.reshape(-1, mesh_edges), edge_weight,
@@ -481,30 +488,24 @@
         ),
     )
 
-    def add_others(first_ref, ids, table_refs):
-        total = first_ref[...]
-        for index_row, table_ref in zip(sender_nodes(ids)[1:], table_refs):
-            total = total + pick(index_row, table_ref[...])
-        return total
-
-    def mesh_sent_body(
-        table_a_ref, table_b_ref, first_a, first_b, rim_a_ref, rim_b_ref, low_ref, high_ref, a_ref, b_ref
-    ):
-        tables = (table_a_ref, table_b_ref)
-        a_ref[...] = add_others(first_a, choose_ids(0, rim_a_ref, high_ref), tables)
-        b_ref[...] = add_others(first_b, choose_ids(1, rim_b_ref, low_ref), tables)
+    def mesh_sent_body(table_a_ref, table_b_ref, first_a, first_b, hot_ref, a_ref, b_ref):
+        table = jnp.concatenate([table_a_ref[...], table_b_ref[...]], axis=0)
+        rows_of = pick_hot(hot_ref[...], table)
+        a_ref[...] = first_a[...] + rows_of[:mesh_edges, :]
+        b_ref[...] = first_b[...] + rows_of[mesh_edges:, :]
 
     send_a, send_b = call(
         mesh_sent_body,
         (edge_block, edge_block),
         16 * mesh_edges * nodes * units,
-        (table_a, table_b, send_a, send_b, rim_a, rim_b, side_low, side_high),
+        (table_a, table_b, send_a, send_b, sent_hot),
     )
     got_a = by_role(send_a, 1, 1, 0)
     got_b = by_role(send_b, 1, back, 1)
 
     def mesh_own_body(table_a_ref, table_b_ref, first_ref, id_ref, out_ref):
-        out_ref[...] = add_others(first_ref, id_ref[...], (table_a_ref, table_b_ref))
+        table = jnp.concatenate([table_a_ref[...], table_b_ref[...]], axis=0)
+        out_ref[...] = first_ref[...] + pick(sender_nodes(id_ref[...])[1], table)
 
     mesh_pre = call(mesh_own_body, edge_block, 8 * mesh_edges * nodes * units, (table_a, table_b, mesh_pre, mesh_ids))
     total = mesh_pre + got_a + got_b

time: 61.8 us -> 61.8 us (level)
  no operation moved by 1% of the time
where the time goes in v6:
time: 61.8 us; the launch traced here: 61.4 us
  starting transfers between devices  23.8 us (39%)
  waiting for transfers between devices  20.3 us (33%)
  Pallas kernels  16.8 us (27%)
    ppermute x12, starting transfers between devices, gather_hid(): lax.ppermute(source, 'hid', [(i, i ^ hop) for i in range(count)])  14.9 us
    ppermute x12, waiting for transfers between devices, gather_hid(): lax.ppermute(source, 'hid', [(i, i ^ hop) for i in range(count)])  14.4 us
    pallas_call x11, Pallas kernels, call(): pl.pallas_call(body, out_shape=outs, in_specs=[VMEM] * len(args), out_spe...  14.2 us
    ppermute x6, starting transfers between devices, exchange(): return lax.ppermute(value, ('lat', 'lon', 'hid'), pairs)  7.63 us
    ppermute x6, waiting for transfers between devices, exchange(): return lax.ppermute(value, ('lat', 'lon', 'hid'), pairs)  5.42 us
    pallas_call x1, Pallas kernels, per_device(): pl.pallas_call(terms_body, out_shape=(shape(rows * cols, units), shape(si...  2.63 us
    ppermute x1, starting transfers between devices, shift(): lax.ppermute(value, axis, [(i, (i + step) % count) for i in range(count)])  1.31 us
  transfers between devices with their start and end apart: 19, of which 10 were waited for; matrix products, arithmetic and copies ran while one was open for 0% of the time, Pallas kernels for 18%

profile of v6, /device:TPU:9, one launch (start us, length us, event | category | flops | bytes accessed | tf_op | source)
XLA Modules:
  0.0 61.4 jit_solution(7914720339508575022)
XLA Ops:
  0.0 1.3 %collective-permute-start.7 = (f32[2,128,512]{2,1,0:T(8,128)}, f32[2,128,512]{2,1,0:T(8,128)S(1)}, u32[]{:S(2)}, u32[]{:S(2)}) collective-permute-start(f32[2,128,512]{2,1,0:T(8,128)} %refs_0_.1), channel_id=1, source_target_pairs={{0,2},{1,3},{2,0},{3,1},{4,6},{5,7},{6,4},{7,5},{8,10},{9,11},{10,... | collective-permute-start | bytes 1572872 | tf_op jit(solution)/shard_map/ppermute | solution.py:148
  1.3 2.6 %grid_terms.1 = (f32[1024,128]{1,0:T(8,128)S(1)}, f32[40,128]{1,0:T(8,128)S(1)}) custom-call(f32[1024,512]{1,0:T(8,128)} %bitcast.24, f32[2,512,128]{2,1,0:T(8,128)} %refs_10_.1, s32[1,512]{1,0:T(1,128)} %bitcast.9), custom_call_target="tpu_custom_call" | custom-call | flops 402653184 | bytes 2097152 | tf_op jit(solution)/shard_map/grid_terms/pallas_call | solution.py:315
  4.0 1.3 %collective-permute-start = (f32[40,128]{1,0:T(8,128)S(1)}, f32[40,128]{1,0:T(8,128)S(1)}, u32[]{:S(2)}, u32[]{:S(2)}) collective-permute-start(f32[40,128]{1,0:T(8,128)S(1)} %get-tuple-element.22), channel_id=1, source_target_pairs={{0,4},{4,0},{1,5},{5,1},{2,6},{6,2},{3,7},{7,3},{8,12},{12,8},{9,1... | collective-permute-start | bytes 61448 | tf_op jit(solution)/shard_map/ppermute | solution.py:97
  5.3 1.2 %collective-permute-start.6 = (f32[2,128,512]{2,1,0:T(8,128)S(1)}, f32[2,128,512]{2,1,0:T(8,128)S(1)}, u32[]{:S(2)}, u32[]{:S(2)}) collective-permute-start(f32[2,128,512]{2,1,0:T(8,128)S(1)} %copy-done), channel_id=1, source_target_pairs={{0,1},{1,0},{2,3},{3,2},{4,5},{5,4},{6,7},{7,6},{8,9},{9,8},{10,11... | collective-permute-start | bytes 1572872 | tf_op jit(solution)/shard_map/ppermute | solution.py:148
  6.5 0.4 collective-permute-done.low_ref.high_ref
  7.0 0.0 copy-start.2
  7.0 0.0 copy-start.8
  7.0 0.0 copy-start.11
  7.0 0.2 collective-permute-start.1
  7.3 2.4 %collective-permute-start.2 = (f32[272,128]{1,0:T(8,128)S(1)}, f32[272,128]{1,0:T(8,128)S(1)}, u32[]{:S(2)}, u32[]{:S(2)}) collective-permute-start(f32[272,128]{1,0:T(8,128)S(1)} %get-tuple-element.24), channel_id=1, source_target_pairs={{0,1},{1,0},{2,3},{3,2},{4,5},{5,4},{6,7},{7,6},{8,16},{9,17},{10,... | collective-permute-start | bytes 417800 | tf_op jit(solution)/shard_map/ppermute | solution.py:115
  9.7 1.2 %shard_map.154.pre_ref = f32[1024,128]{1,0:T(8,128)S(1)} custom-call(f32[1024,128]{1,0:T(8,128)S(1)} %get-tuple-element.21.term_ref, f32[4,1024]{1,0:T(4,128)S(1)} %bitcast.18, f32[2,4,128]{2,1,0:T(4,128)S(1)} %copy-done.5, f32[2,128]{1,0:T(2,128)S(1)} %copy-done.7, s32[1,1024]{1,0:T(1,128)S(1)} %bitcast.19), custom_call_target="tpu_custom_call" | custom-call | flops 1073741824 | bytes 1048576 | tf_op jit(solution)/shard_map/pallas_call | solution.py:80
  10.9 1.4 %shard_map.155.pre_ref = f32[1024,128]{1,0:T(8,128)S(1)} custom-call(f32[1024,128]{1,0:T(8,128)S(1)} %shard_map.154.pre_ref, f32[512,512]{1,0:T(8,128)S(1)} %bitcast.16, f32[2,512,128]{2,1,0:T(8,128)S(1)} %copy-done.2, s32[1,1024]{1,0:T(1,128)S(1)} %bitcast.21), custom_call_target="tpu_custom_call" | custom-call | flops 1073741824 | bytes 1048576 | tf_op jit(solution)/shard_map/pallas_call | solution.py:80
  12.4 0.0 copy-start.12
  12.4 0.0 copy-start.13
  12.4 0.0 copy-start.14
  12.4 0.7 %collective-permute-done.7.refs_2_ = f32[2,128,512]{2,1,0:T(8,128)S(1)} collective-permute-done((f32[2,128,512]{2,1,0:T(8,128)}, f32[2,128,512]{2,1,0:T(8,128)S(1)}, u32[]{:S(2)}, u32[]{:S(2)}) %collective-permute-start.7) | collective-permute-done | bytes 524320 | tf_op jit(solution)/shard_map/ppermute | solution.py:148
  13.1 1.7 %collective-permute-start.8 = (f32[2,128,512]{2,1,0:T(8,128)S(1)}, f32[2,128,512]{2,1,0:T(8,128)S(1)}, u32[]{:S(2)}, u32[]{:S(2)}) collective-permute-start(f32[2,128,512]{2,1,0:T(8,128)S(1)} %collective-permute-done.7.refs_2_), channel_id=1, source_target_pairs={{0,1},{1,0},{2,3},{3,2},{4,5},{5,4},{6,7},{7,6},{8,9},{9,8},{10,11... | collective-permute-start | bytes 1572872 | tf_op jit(solution)/shard_map/ppermute | solution.py:148
  14.9 0.7 %shard_map.157 = (f32[512,128]{1,0:T(8,128)S(1)}, f32[512,128]{1,0:T(8,128)S(1)}) custom-call(f32[1024,128]{1,0:T(8,128)S(1)} %shard_map.155.pre_ref, f32[40,128]{1,0:T(8,128)S(1)} %collective-permute-done.low_ref.high_ref, f32[40,128]{1,0:T(8,128)S(1)} %collective-permute-done.low_ref.high_ref, f32[272,128]{1,0:T(8,128)S(1)} %collective-permute-done.1.a_ref.rim_a_ref, ...), custom_call_target="tpu_custom_call" | custom-call | flops 536870912 | bytes 1048576 | tf_op jit(solution)/shard_map/pallas_call | solution.py:80
  15.5 1.1 %collective-permute-start.10 = (f32[512,128]{1,0:T(8,128)S(1)}, f32[512,128]{1,0:T(8,128)S(1)}, u32[]{:S(2)}, u32[]{:S(2)}) collective-permute-start(f32[512,128]{1,0:T(8,128)S(1)} %get-tuple-element.27.refs_0_), channel_id=1, source_target_pairs={{0,2},{1,3},{2,0},{3,1},{4,6},{5,7},{6,4},{7,5},{8,10},{9,11},{10,... | collective-permute-start | bytes 786440 | tf_op jit(solution)/shard_map/ppermute | solution.py:148
  16.6 0.5 collective-permute-start.4
  17.1 0.8 %collective-permute-start.9 = (f32[512,128]{1,0:T(8,128)S(1)}, f32[512,128]{1,0:T(8,128)S(1)}, u32[]{:S(2)}, u32[]{:S(2)}) collective-permute-start(f32[512,128]{1,0:T(8,128)S(1)} %get-tuple-element.27.refs_0_), channel_id=1, source_target_pairs={{0,1},{1,0},{2,3},{3,2},{4,5},{5,4},{6,7},{7,6},{8,9},{9,8},{10,11... | collective-permute-start | bytes 786440 | tf_op jit(solution)/shard_map/ppermute | solution.py:148
  17.8 5.4 %collective-permute-done.10.refs_2_ = f32[512,128]{1,0:T(8,128)S(1)} collective-permute-done((f32[512,128]{1,0:T(8,128)S(1)}, f32[512,128]{1,0:T(8,128)S(1)}, u32[]{:S(2)}, u32[]{:S(2)}) %collective-permute-start.10) | collective-permute-done | bytes 262176 | tf_op jit(solution)/shard_map/ppermute | solution.py:148
  23.2 1.7 %collective-permute-start.11 = (f32[512,128]{1,0:T(8,128)S(1)}, f32[512,128]{1,0:T(8,128)S(1)}, u32[]{:S(2)}, u32[]{:S(2)}) collective-permute-start(f32[512,128]{1,0:T(8,128)S(1)} %collective-permute-done.10.refs_2_), channel_id=1, source_target_pairs={{0,1},{1,0},{2,3},{3,2},{4,5},{5,4},{6,7},{7,6},{8,9},{9,8},{10,11... | collective-permute-start | bytes 786440 | tf_op jit(solution)/shard_map/ppermute | solution.py:148
  25.0 3.9 %collective-permute-done.4.refs_2_ = f32[512,128]{1,0:T(8,128)S(1)} collective-permute-done((f32[512,128]{1,0:T(8,128)S(1)}, f32[512,128]{1,0:T(8,128)S(1)}, u32[]{:S(2)}, u32[]{:S(2)}) %collective-permute-start.4) | collective-permute-done | bytes 262176 | tf_op jit(solution)/shard_map/ppermute | solution.py:148
  28.9 1.1 %collective-permute-start.3 = (f32[512,128]{1,0:T(8,128)S(1)}, f32[512,128]{1,0:T(8,128)S(1)}, u32[]{:S(2)}, u32[]{:S(2)}) collective-permute-start(f32[512,128]{1,0:T(8,128)S(1)} %get-tuple-element.25.refs_0_), channel_id=1, source_target_pairs={{0,1},{1,0},{2,3},{3,2},{4,5},{5,4},{6,7},{7,6},{8,9},{9,8},{10,11... | collective-permute-start | bytes 786440 | tf_op jit(solution)/shard_map/ppermute | solution.py:148
  29.9 0.0 collective-permute-start.5
  30.0 0.3 shard_map.158
  30.4 1.8 %shard_map.159.refs_9_ = f32[512,512]{1,0:T(8,128)S(1)} custom-call(f32[512,128]{1,0:T(8,128)S(1)} %get-tuple-element.27.refs_0_, f32[512,128]{1,0:T(8,128)S(1)} %collective-permute-done.9.refs_1_, f32[512,128]{1,0:T(8,128)S(1)} %collective-permute-done.10.refs_2_, f32[512,128]{1,0:T(8,128)S(1)} %collective-permute-done.11.refs_3_, ...), custom_call_target="tpu_custom_call" | custom-call | flops 1342177280 | bytes 1048576 | tf_op jit(solution)/shard_map/pallas_call | solution.py:80
  32.2 0.0 copy-start.4
  32.2 2.8 %shard_map.160 = (f32[512,512]{1,0:T(8,128)S(1)}, f32[512,128]{1,0:T(8,128)S(1)}) custom-call(f32[512,128]{1,0:T(8,128)S(1)} %get-tuple-element.25.refs_0_, f32[512,128]{1,0:T(8,128)S(1)} %collective-permute-done.3.refs_1_, f32[512,128]{1,0:T(8,128)S(1)} %collective-permute-done.4.refs_2_, f32[512,128]{1,0:T(8,128)S(1)} %collective-permute-done.5.refs_3_, ...), custom_call_target="tpu_custom_call" | custom-call | flops 1610612736 | bytes 1048576 | tf_op jit(solution)/shard_map/pallas_call | solution.py:80
  35.1 0.1 collective-permute-start.12
  35.2 2.4 %collective-permute-start.13 = (f32[512,128]{1,0:T(8,128)S(1)}, f32[512,128]{1,0:T(8,128)S(1)}, u32[]{:S(2)}, u32[]{:S(2)}) collective-permute-start(f32[512,128]{1,0:T(8,128)S(1)} %get-tuple-element.28.term_ref), channel_id=1, source_target_pairs={{0,1},{1,0},{2,3},{3,2},{4,5},{5,4},{6,7},{7,6},{8,10},{9,17},{10,... | collective-permute-start | bytes 786440 | tf_op jit(solution)/shard_map/ppermute | solution.py:115
  37.6 2.4 %shard_map.161 = (f32[512,128]{1,0:T(8,128)S(1)}, f32[512,128]{1,0:T(8,128)S(1)}, f32[512,128]{1,0:T(8,128)S(1)}, bf16[1024,1024]{1,0:T(8,128)(2,1)S(1)}) custom-call(f32[512,128]{1,0:T(8,128)S(1)} %get-tuple-element.28.term_ref, f32[512,512]{1,0:T(8,128)S(1)} %get-tuple-element.29.mid_ref.refs_9_, f32[2,512,128]{2,1,0:T(8,128)S(1)} %copy-done.2, ...), custom_call_target="tpu_custom_call" | custom-call | flops 536870912 | bytes 1048576 | tf_op jit(solution)/shard_map/pallas_call | solution.py:80
  39.9 0.7 %collective-permute-done.12.table_a_ref = f32[512,128]{1,0:T(8,128)S(1)} collective-permute-done((f32[512,128]{1,0:T(8,128)S(1)}, f32[512,128]{1,0:T(8,128)S(1)}, u32[]{:S(2)}, u32[]{:S(2)}) %collective-permute-start.12) | collective-permute-done | bytes 262176 | tf_op jit(solution)/shard_map/ppermute | solution.py:115
  40.7 0.9 %collective-permute-done.13.table_b_ref = f32[512,128]{1,0:T(8,128)S(1)} collective-permute-done((f32[512,128]{1,0:T(8,128)S(1)}, f32[512,128]{1,0:T(8,128)S(1)}, u32[]{:S(2)}, u32[]{:S(2)}) %collective-permute-start.13) | collective-permute-done | bytes 262176 | tf_op jit(solution)/shard_map/ppermute | solution.py:115
  41.6 0.7 %shard_map.163 = (f32[512,128]{1,0:T(8,128)S(1)}, f32[512,128]{1,0:T(8,128)S(1)}) custom-call(f32[512,128]{1,0:T(8,128)S(1)} %collective-permute-done.12.table_a_ref, f32[512,128]{1,0:T(8,128)S(1)} %collective-permute-done.13.table_b_ref, f32[512,128]{1,0:T(8,128)S(1)} %get-tuple-element.31.first_a, f32[512,128]{1,0:T(8,128)S(1)} %get-tuple-element.32.first_b, ...), custom_call_target="tpu_custom_call" | custom-call | flops 536870912 | bytes 1048576 | tf_op jit(solution)/shard_map/pallas_call | solution.py:80
  42.3 1.3 %collective-permute-start.14 = (f32[512,128]{1,0:T(8,128)S(1)}, f32[512,128]{1,0:T(8,128)S(1)}, u32[]{:S(2)}, u32[]{:S(2)}) collective-permute-start(f32[512,128]{1,0:T(8,128)S(1)} %get-tuple-element.34), channel_id=1, source_target_pairs={{0,8},{1,5},{2,10},{3,7},{4,12},{5,1},{6,14},{7,3},{8,0},{9,13},{1... | collective-permute-start | bytes 786440 | tf_op jit(solution)/shard_map/ppermute | solution.py:115
  43.6 1.2 %collective-permute-start.15 = (f32[512,128]{1,0:T(8,128)S(1)}, f32[512,128]{1,0:T(8,128)S(1)}, u32[]{:S(2)}, u32[]{:S(2)}) collective-permute-start(f32[512,128]{1,0:T(8,128)S(1)} %get-tuple-element.35), channel_id=1, source_target_pairs={{0,1},{1,0},{2,3},{3,2},{4,5},{5,4},{6,7},{7,6},{8,16},{9,11},{10,... | collective-permute-start | bytes 786440 | tf_op jit(solution)/shard_map/ppermute | solution.py:115
  44.8 0.5 shard_map.162
  45.4 2.5 %collective-permute-done.14 = f32[512,128]{1,0:T(8,128)S(1)} collective-permute-done((f32[512,128]{1,0:T(8,128)S(1)}, f32[512,128]{1,0:T(8,128)S(1)}, u32[]{:S(2)}, u32[]{:S(2)}) %collective-permute-start.14) | collective-permute-done | bytes 262176 | tf_op jit(solution)/shard_map/ppermute | solution.py:115
  47.9 1.2 %collective-permute-done.15 = f32[512,128]{1,0:T(8,128)S(1)} collective-permute-done((f32[512,128]{1,0:T(8,128)S(1)}, f32[512,128]{1,0:T(8,128)S(1)}, u32[]{:S(2)}, u32[]{:S(2)}) %collective-permute-start.15) | collective-permute-done | bytes 262176 | tf_op jit(solution)/shard_map/ppermute | solution.py:115
  49.1 0.1 add_divide_fusion.refs_0_
  49.2 1.3 %collective-permute-start.17 = (f32[512,128]{1,0:T(8,128)S(1)}, f32[512,128]{1,0:T(8,128)S(1)}, u32[]{:S(2)}, u32[]{:S(2)}) collective-permute-start(f32[512,128]{1,0:T(8,128)S(1)} %add_divide_fusion.refs_0_), channel_id=1, source_target_pairs={{0,2},{1,3},{2,0},{3,1},{4,6},{5,7},{6,4},{7,5},{8,10},{9,11},{10,... | collective-permute-start | bytes 786440 | tf_op jit(solution)/shard_map/ppermute | solution.py:148
  50.5 1.7 %collective-permute-start.16 = (f32[512,128]{1,0:T(8,128)S(1)}, f32[512,128]{1,0:T(8,128)S(1)}, u32[]{:S(2)}, u32[]{:S(2)}) collective-permute-start(f32[512,128]{1,0:T(8,128)S(1)} %add_divide_fusion.refs_0_), channel_id=1, source_target_pairs={{0,1},{1,0},{2,3},{3,2},{4,5},{5,4},{6,7},{7,6},{8,9},{9,8},{10,11... | collective-permute-start | bytes 786440 | tf_op jit(solution)/shard_map/ppermute | solution.py:148
  52.2 3.3 %collective-permute-done.17.refs_2_ = f32[512,128]{1,0:T(8,128)S(1)} collective-permute-done((f32[512,128]{1,0:T(8,128)S(1)}, f32[512,128]{1,0:T(8,128)S(1)}, u32[]{:S(2)}, u32[]{:S(2)}) %collective-permute-start.17) | collective-permute-done | bytes 262176 | tf_op jit(solution)/shard_map/ppermute | solution.py:148
  55.5 2.5 %collective-permute-start.18 = (f32[512,128]{1,0:T(8,128)S(1)}, f32[512,128]{1,0:T(8,128)S(1)}, u32[]{:S(2)}, u32[]{:S(2)}) collective-permute-start(f32[512,128]{1,0:T(8,128)S(1)} %collective-permute-done.17.refs_2_), channel_id=1, source_target_pairs={{0,1},{1,0},{2,3},{3,2},{4,5},{5,4},{6,7},{7,6},{8,9},{9,8},{10,11... | collective-permute-start | bytes 786440 | tf_op jit(solution)/shard_map/ppermute | solution.py:148
  58.0 1.2 %collective-permute-done.18.refs_3_ = f32[512,128]{1,0:T(8,128)S(1)} collective-permute-done((f32[512,128]{1,0:T(8,128)S(1)}, f32[512,128]{1,0:T(8,128)S(1)}, u32[]{:S(2)}, u32[]{:S(2)}) %collective-permute-start.18) | collective-permute-done | bytes 262176 | tf_op jit(solution)/shard_map/ppermute | solution.py:148
  59.2 2.3 %shard_map.164 = f32[512,128]{1,0:T(8,128)} custom-call(f32[512,128]{1,0:T(8,128)S(1)} %add_divide_fusion.refs_0_, f32[512,128]{1,0:T(8,128)S(1)} %collective-permute-done.16.refs_1_, f32[512,128]{1,0:T(8,128)S(1)} %collective-permute-done.17.refs_2_, f32[512,128]{1,0:T(8,128)S(1)} %collective-permute-done.18.refs_3_, ...), custom_call_target="tpu_custom_call" | custom-call | flops 1073741824 | bytes 1048576 | tf_op jit(solution)/shard_map/pallas_call | solution.py:80
  (33 shorter events, 0.1 us)
Async XLA Ops:
  0.0 5.3 %copy-start = (f32[2,128,512]{2,1,0:T(8,128)S(1)}, f32[2,128,512]{2,1,0:T(8,128)}, u32[]{:S(2)}) copy-start(f32[2,128,512]{2,1,0:T(8,128)} %refs_0_.1) | copy-start | bytes 1572868
  0.0 7.0 %copy-start.3 = (s32[1,1,512]{2,1,0:T(1,128)S(1)}, s32[1,1,512]{2,1,0:T(1,128)}, u32[]{:S(2)}) copy-start(s32[1,1,512]{2,1,0:T(1,128)} %param.22) | copy-start | bytes 6148
  0.0 9.7 %copy-start.10 = (s32[1,1,1024]{2,1,0:T(1,128)S(1)}, s32[1,1,1024]{2,1,0:T(1,128)}, u32[]{:S(2)}) copy-start(s32[1,1,1024]{2,1,0:T(1,128)} %param.19) | copy-start | bytes 12292
  0.0 9.7 %copy-start.9 = (f32[1,1,4,1024]{3,2,1,0:T(4,128)S(1)}, f32[1,1,4,1024]{3,2,1,0:T(4,128)}, u32[]{:S(2)}) copy-start(f32[1,1,4,1024]{3,2,1,0:T(4,128)} %param.18) | copy-start | bytes 49156
  0.0 9.7 %copy-start.5 = (f32[2,4,128]{2,1,0:T(4,128)S(1)}, f32[2,4,128]{2,1,0:T(4,128)}, u32[]{:S(2)}) copy-start(f32[2,4,128]{2,1,0:T(4,128)} %edge_ref.3) | copy-start | bytes 12292
  0.0 9.7 %copy-start.7 = (f32[2,128]{1,0:T(2,128)S(1)}, f32[2,128]{1,0:T(2,128)}, u32[]{:S(2)}) copy-start(f32[2,128]{1,0:T(2,128)} %bias_ref.3) | copy-start | bytes 3076
  0.0 13.1 %collective-permute-start.7 = (f32[2,128,512]{2,1,0:T(8,128)}, f32[2,128,512]{2,1,0:T(8,128)S(1)}, u32[]{:S(2)}, u32[]{:S(2)}) collective-permute-start(f32[2,128,512]{2,1,0:T(8,128)} %refs_0_.1), channel_id=1, source_target_pairs={{0,2},{1,3},{2,0},{3,1},{4,6},{5,7},{6,4},{7,5},{8,10},{9,11},{10,... | collective-permute-start | bytes 1572872 | tf_op jit(solution)/shard_map/ppermute | solution.py:148
  4.0 3.0 %collective-permute-start = (f32[40,128]{1,0:T(8,128)S(1)}, f32[40,128]{1,0:T(8,128)S(1)}, u32[]{:S(2)}, u32[]{:S(2)}) collective-permute-start(f32[40,128]{1,0:T(8,128)S(1)} %get-tuple-element.22), channel_id=1, source_target_pairs={{0,4},{4,0},{1,5},{5,1},{2,6},{6,2},{3,7},{7,3},{8,12},{12,8},{9,1... | collective-permute-start | bytes 61448 | tf_op jit(solution)/shard_map/ppermute | solution.py:97
  5.3 24.7 %collective-permute-start.6 = (f32[2,128,512]{2,1,0:T(8,128)S(1)}, f32[2,128,512]{2,1,0:T(8,128)S(1)}, u32[]{:S(2)}, u32[]{:S(2)}) collective-permute-start(f32[2,128,512]{2,1,0:T(8,128)S(1)} %copy-done), channel_id=1, source_target_pairs={{0,1},{1,0},{2,3},{3,2},{4,5},{5,4},{6,7},{7,6},{8,9},{9,8},{10,11... | collective-permute-start | bytes 1572872 | tf_op jit(solution)/shard_map/ppermute | solution.py:148
  7.0 3.9 %copy-start.2 = (f32[2,512,128]{2,1,0:T(8,128)S(1)}, f32[2,512,128]{2,1,0:T(8,128)}, u32[]{:S(2)}) copy-start(f32[2,512,128]{2,1,0:T(8,128)} %weight_ref.5) | copy-start | bytes 1572868
  7.0 3.9 %copy-start.8 = (f32[1,1,512,512]{3,2,1,0:T(8,128)S(1)}, f32[1,1,512,512]{3,2,1,0:T(8,128)}, u32[]{:S(2)}) copy-start(f32[1,1,512,512]{3,2,1,0:T(8,128)} %param.17) | copy-start | bytes 3145732
  7.0 3.9 %copy-start.11 = (s32[1,1,1024]{2,1,0:T(1,128)S(1)}, s32[1,1,1024]{2,1,0:T(1,128)}, u32[]{:S(2)}) copy-start(s32[1,1,1024]{2,1,0:T(1,128)} %param.20) | copy-start | bytes 12292
  7.0 7.8 %collective-permute-start.1 = (f32[272,128]{1,0:T(8,128)S(1)}, f32[272,128]{1,0:T(8,128)S(1)}, u32[]{:S(2)}, u32[]{:S(2)}) collective-permute-start(f32[272,128]{1,0:T(8,128)S(1)} %get-tuple-element.23), channel_id=1, source_target_pairs={{0,8},{1,9},{2,10},{3,11},{4,12},{5,13},{6,14},{7,15},{8,0},{9,1},... | collective-permute-start | bytes 417800 | tf_op jit(solution)/shard_map/ppermute | solution.py:115
  7.3 7.6 %collective-permute-start.2 = (f32[272,128]{1,0:T(8,128)S(1)}, f32[272,128]{1,0:T(8,128)S(1)}, u32[]{:S(2)}, u32[]{:S(2)}) collective-permute-start(f32[272,128]{1,0:T(8,128)S(1)} %get-tuple-element.24), channel_id=1, source_target_pairs={{0,1},{1,0},{2,3},{3,2},{4,5},{5,4},{6,7},{7,6},{8,16},{9,17},{10,... | collective-permute-start | bytes 417800 | tf_op jit(solution)/shard_map/ppermute | solution.py:115
  12.4 17.9 %copy-start.12 = (f32[2,512]{1,0:T(2,128)S(1)}, f32[2,512]{1,0:T(2,128)}, u32[]{:S(2)}) copy-start(f32[2,512]{1,0:T(2,128)} %refs_5_.5) | copy-start | bytes 12292
  12.4 17.9 %copy-start.13 = (f32[2,512]{1,0:T(2,128)S(1)}, f32[2,512]{1,0:T(2,128)}, u32[]{:S(2)}) copy-start(f32[2,512]{1,0:T(2,128)} %refs_6_.5) | copy-start | bytes 12292
  12.4 17.9 %copy-start.14 = (f32[2,512]{1,0:T(2,128)S(1)}, f32[2,512]{1,0:T(2,128)}, u32[]{:S(2)}) copy-start(f32[2,512]{1,0:T(2,128)} %refs_7_.5) | copy-start | bytes 12292
  13.1 16.8 %collective-permute-start.8 = (f32[2,128,512]{2,1,0:T(8,128)S(1)}, f32[2,128,512]{2,1,0:T(8,128)S(1)}, u32[]{:S(2)}, u32[]{:S(2)}) collective-permute-start(f32[2,128,512]{2,1,0:T(8,128)S(1)} %collective-permute-done.7.refs_2_), channel_id=1, source_target_pairs={{0,1},{1,0},{2,3},{3,2},{4,5},{5,4},{6,7},{7,6},{8,9},{9,8},{10,11... | collective-permute-start | bytes 1572872 | tf_op jit(solution)/shard_map/ppermute | solution.py:148
  15.5 7.7 %collective-permute-start.10 = (f32[512,128]{1,0:T(8,128)S(1)}, f32[512,128]{1,0:T(8,128)S(1)}, u32[]{:S(2)}, u32[]{:S(2)}) collective-permute-start(f32[512,128]{1,0:T(8,128)S(1)} %get-tuple-element.27.refs_0_), channel_id=1, source_target_pairs={{0,2},{1,3},{2,0},{3,1},{4,6},{5,7},{6,4},{7,5},{8,10},{9,11},{10,... | collective-permute-start | bytes 786440 | tf_op jit(solution)/shard_map/ppermute | solution.py:148
  16.6 12.3 %collective-permute-start.4 = (f32[512,128]{1,0:T(8,128)S(1)}, f32[512,128]{1,0:T(8,128)S(1)}, u32[]{:S(2)}, u32[]{:S(2)}) collective-permute-start(f32[512,128]{1,0:T(8,128)S(1)} %get-tuple-element.25.refs_0_), channel_id=1, source_target_pairs={{0,2},{1,3},{2,0},{3,1},{4,6},{5,7},{6,4},{7,5},{8,10},{9,11},{10,... | collective-permute-start | bytes 786440 | tf_op jit(solution)/shard_map/ppermute | solution.py:148
  17.1 13.2 %collective-permute-start.9 = (f32[512,128]{1,0:T(8,128)S(1)}, f32[512,128]{1,0:T(8,128)S(1)}, u32[]{:S(2)}, u32[]{:S(2)}) collective-permute-start(f32[512,128]{1,0:T(8,128)S(1)} %get-tuple-element.27.refs_0_), channel_id=1, source_target_pairs={{0,1},{1,0},{2,3},{3,2},{4,5},{5,4},{6,7},{7,6},{8,9},{9,8},{10,11... | collective-permute-start | bytes 786440 | tf_op jit(solution)/shard_map/ppermute | solution.py:148
  23.2 7.1 %collective-permute-start.11 = (f32[512,128]{1,0:T(8,128)S(1)}, f32[512,128]{1,0:T(8,128)S(1)}, u32[]{:S(2)}, u32[]{:S(2)}) collective-permute-start(f32[512,128]{1,0:T(8,128)S(1)} %collective-permute-done.10.refs_2_), channel_id=1, source_target_pairs={{0,1},{1,0},{2,3},{3,2},{4,5},{5,4},{6,7},{7,6},{8,9},{9,8},{10,11... | collective-permute-start | bytes 786440 | tf_op jit(solution)/shard_map/ppermute | solution.py:148
  28.9 3.3 %collective-permute-start.3 = (f32[512,128]{1,0:T(8,128)S(1)}, f32[512,128]{1,0:T(8,128)S(1)}, u32[]{:S(2)}, u32[]{:S(2)}) collective-permute-start(f32[512,128]{1,0:T(8,128)S(1)} %get-tuple-element.25.refs_0_), channel_id=1, source_target_pairs={{0,1},{1,0},{2,3},{3,2},{4,5},{5,4},{6,7},{7,6},{8,9},{9,8},{10,11... | collective-permute-start | bytes 786440 | tf_op jit(solution)/shard_map/ppermute | solution.py:148
  29.9 2.3 %collective-permute-start.5 = (f32[512,128]{1,0:T(8,128)S(1)}, f32[512,128]{1,0:T(8,128)S(1)}, u32[]{:S(2)}, u32[]{:S(2)}) collective-permute-start(f32[512,128]{1,0:T(8,128)S(1)} %collective-permute-done.4.refs_2_), channel_id=1, source_target_pairs={{0,1},{1,0},{2,3},{3,2},{4,5},{5,4},{6,7},{7,6},{8,9},{9,8},{10,11... | collective-permute-start | bytes 786440 | tf_op jit(solution)/shard_map/ppermute | solution.py:148
  30.3 1.9 %copy-start.1 = (f32[2,512,128]{2,1,0:T(8,128)S(1)}, f32[2,512,128]{2,1,0:T(8,128)}, u32[]{:S(2)}) copy-start(f32[2,512,128]{2,1,0:T(8,128)} %refs_10_.1) | copy-start | bytes 1572868
  32.2 5.4 %copy-start.4 = (f32[1,1,4,512]{3,2,1,0:T(4,128)S(1)}, f32[1,1,4,512]{3,2,1,0:T(4,128)}, u32[]{:S(2)}) copy-start(f32[1,1,4,512]{3,2,1,0:T(4,128)} %param.21) | copy-start | bytes 24580
  32.2 5.4 %copy-start.6 = (s32[1,1,512]{2,1,0:T(1,128)S(1)}, s32[1,1,512]{2,1,0:T(1,128)}, u32[]{:S(2)}) copy-start(s32[1,1,512]{2,1,0:T(1,128)} %param.23) | copy-start | bytes 6148
  35.1 5.6 %collective-permute-start.12 = (f32[512,128]{1,0:T(8,128)S(1)}, f32[512,128]{1,0:T(8,128)S(1)}, u32[]{:S(2)}, u32[]{:S(2)}) collective-permute-start(f32[512,128]{1,0:T(8,128)S(1)} %get-tuple-element.28.term_ref), channel_id=1, source_target_pairs={{0,4},{1,9},{2,6},{3,11},{4,0},{5,13},{6,2},{7,15},{8,12},{9,1},{1... | collective-permute-start | bytes 786440 | tf_op jit(solution)/shard_map/ppermute | solution.py:115
  35.2 6.4 %collective-permute-start.13 = (f32[512,128]{1,0:T(8,128)S(1)}, f32[512,128]{1,0:T(8,128)S(1)}, u32[]{:S(2)}, u32[]{:S(2)}) collective-permute-start(f32[512,128]{1,0:T(8,128)S(1)} %get-tuple-element.28.term_ref), channel_id=1, source_target_pairs={{0,1},{1,0},{2,3},{3,2},{4,5},{5,4},{6,7},{7,6},{8,10},{9,17},{10,... | collective-permute-start | bytes 786440 | tf_op jit(solution)/shard_map/ppermute | solution.py:115
  42.3 5.6 %collective-permute-start.14 = (f32[512,128]{1,0:T(8,128)S(1)}, f32[512,128]{1,0:T(8,128)S(1)}, u32[]{:S(2)}, u32[]{:S(2)}) collective-permute-start(f32[512,128]{1,0:T(8,128)S(1)} %get-tuple-element.34), channel_id=1, source_target_pairs={{0,8},{1,5},{2,10},{3,7},{4,12},{5,1},{6,14},{7,3},{8,0},{9,13},{1... | collective-permute-start | bytes 786440 | tf_op jit(solution)/shard_map/ppermute | solution.py:115
  43.6 5.5 %collective-permute-start.15 = (f32[512,128]{1,0:T(8,128)S(1)}, f32[512,128]{1,0:T(8,128)S(1)}, u32[]{:S(2)}, u32[]{:S(2)}) collective-permute-start(f32[512,128]{1,0:T(8,128)S(1)} %get-tuple-element.35), channel_id=1, source_target_pairs={{0,1},{1,0},{2,3},{3,2},{4,5},{5,4},{6,7},{7,6},{8,16},{9,11},{10,... | collective-permute-start | bytes 786440 | tf_op jit(solution)/shard_map/ppermute | solution.py:115
  49.2 6.3 %collective-permute-start.17 = (f32[512,128]{1,0:T(8,128)S(1)}, f32[512,128]{1,0:T(8,128)S(1)}, u32[]{:S(2)}, u32[]{:S(2)}) collective-permute-start(f32[512,128]{1,0:T(8,128)S(1)} %add_divide_fusion.refs_0_), channel_id=1, source_target_pairs={{0,2},{1,3},{2,0},{3,1},{4,6},{5,7},{6,4},{7,5},{8,10},{9,11},{10,... | collective-permute-start | bytes 786440 | tf_op jit(solution)/shard_map/ppermute | solution.py:148
  50.5 7.5 %collective-permute-start.16 = (f32[512,128]{1,0:T(8,128)S(1)}, f32[512,128]{1,0:T(8,128)S(1)}, u32[]{:S(2)}, u32[]{:S(2)}) collective-permute-start(f32[512,128]{1,0:T(8,128)S(1)} %add_divide_fusion.refs_0_), channel_id=1, source_target_pairs={{0,1},{1,0},{2,3},{3,2},{4,5},{5,4},{6,7},{7,6},{8,9},{9,8},{10,11... | collective-permute-start | bytes 786440 | tf_op jit(solution)/shard_map/ppermute | solution.py:148
  55.5 3.7 %collective-permute-start.18 = (f32[512,128]{1,0:T(8,128)S(1)}, f32[512,128]{1,0:T(8,128)S(1)}, u32[]{:S(2)}, u32[]{:S(2)}) collective-permute-start(f32[512,128]{1,0:T(8,128)S(1)} %collective-permute-done.17.refs_2_), channel_id=1, source_target_pairs={{0,1},{1,0},{2,3},{3,2},{4,5},{5,4},{6,7},{7,6},{8,9},{9,8},{10,11... | collective-permute-start | bytes 786440 | tf_op jit(solution)/shard_map/ppermute | solution.py:148
